TPU v7x, 256 devices: a whole 4x4x8 slice. The times are simulated.
256 devices in a mesh: row: 8 (over y, core), col: 32 (over x, z).
Axes of the slice: x: 4, y: 4, z: 8, core: 2. Of those that a mesh axis runs over, the one named last changes fastest.
Arguments:
- eigvecs: float32 [1024, 100352], P('col', 'row'), may hold values from -6 to 6
- span_vectors: float32 [2, 64, 4, 128], P(None, 'row'), may hold values from -6 to 6
- span_offsets: int32 [2, 64], P(None, 'row'), may hold values from 0 to 12543, as said below
- panels: bfloat16 [2, 256, 100352], P(None, 'col', 'row'), may hold values from -0.01894036 to 0.01894036
Outputs:
- back_vectors: float32 [1024, 100352], P('col', 'row')
Inputs may be any that keep to these rules, and one draw needn't show every extreme that they name: `span_offsets`: each block starts within the rows of its index of row and ends at most 128 rows after them, and inside the matrix; on every index of row but the last the last block of each sweep reaches into the next index's rows.
All inputs are finite; a program needn't handle non-finite values.
Results may differ from a plain program's by a relative error of at most 0.0075.
Values may be sent and summed in bfloat16 or wider, within the bound.
A program may use at most 128 MiB of HBM per device.

v0:
```python
import jax
import jax.numpy as jnp
from jax import lax
from jax.sharding import Mesh
from jax.sharding import PartitionSpec as P

COL = ("col_0", "col_1")


CONTRACT_LAST = (((1,), (1,)), ((), ()))
CONTRACT_FIRST = (((0,), (0,)), ((), ()))


def from_behind(value, axis, steps):
    count = lax.axis_size(axis)
    first, last = (max(0, -steps), min(count, count - steps))
    return lax.ppermute(value, axis, [(source, source + steps) for source in range(first, last)])


def in_order(pieces, dim):
    pieces = jnp.moveaxis(pieces, 0, dim)
    shape = pieces.shape
    return pieces.reshape(*shape[:dim], shape[dim] * shape[dim + 1], *shape[dim + 2 :])


def all_blocks(x, axes, sequence):
    pieces = x[None]
    for k in sequence:
        pieces = lax.all_gather(pieces, axes[k], axis=0, tiled=True)
    current = [lax.axis_size(axes[k]) for k in reversed(sequence)]
    pieces = pieces.reshape(*current, *x.shape)
    turned = sorted(range(len(sequence)), key=lambda place: sequence[len(sequence) - 1 - place])
    return pieces.transpose(*turned, *range(len(sequence), pieces.ndim)).reshape(-1, *x.shape)


def gather_axes(x, axes, sequence, dim):
    return in_order(all_blocks(x, axes, sequence), dim)


def sent_to_all(x, axis):
    peers = lax.axis_size(axis)
    return lax.all_to_all(jnp.broadcast_to(x[None], (peers, *x.shape)), axis, 0, 0, tiled=True)


def over_copies(x, axis):
    everything = sent_to_all(x, axis)
    return jnp.sum(everything.astype(jnp.float32), axis=0)


def wy_matrix(gram_mat):
    return jnp.triu(gram_mat, 1) + 0.5 * jnp.diag(jnp.diag(gram_mat))


def upper_solve(matrix, right):
    order = matrix.shape[0]
    if order <= 8:
        solved = [None] * order
        for back_at in range(order - 1, -1, -1):
            value = right[back_at]
            for later in range(back_at + 1, order):
                value = value - matrix[back_at, later] * solved[later]
            solved[back_at] = value / matrix[back_at, back_at]
        return jnp.stack(solved, axis=0)

    def step(count, solution):
        place = (order - 1 - count).astype(jnp.int32)
        matrow = lax.dynamic_index_in_dim(matrix, place, 0, keepdims=False)
        rhsrow = lax.dynamic_index_in_dim(right, place, 0, keepdims=False)
        pivot = lax.dynamic_index_in_dim(matrow, place, 0, keepdims=False)
        partial_sum = jnp.dot(matrow, solution)
        value = (rhsrow - partial_sum) / pivot
        return lax.dynamic_update_index_in_dim(solution, value, place, 0)

    return lax.fori_loop(0, order, step, jnp.zeros(right.shape, jnp.float32))


def apply_span(window, vectors):
    gram_mat = jnp.dot(vectors, vectors.T)
    inner = jnp.dot(vectors, window.T)
    coeffs = upper_solve(wy_matrix(gram_mat), inner)
    return window - jnp.dot(coeffs.T, vectors)


def run_spans(block, vectors, offsets, band_len):

    def advance(span_at, state):
        begin_at = offsets[span_at]
        window = lax.dynamic_slice_in_dim(state, begin_at, band_len, 1)
        return lax.dynamic_update_slice_in_dim(
            state, apply_span(window, vectors[span_at]), begin_at, 1
        )

    return lax.fori_loop(0, vectors.shape[0], advance, block)


def sweep_chain(eigen, vectors, offsets, band_len):
    columns, rows_dev = eigen.shape
    row_count = lax.axis_size("row")
    row_index = lax.axis_index("row")
    below = from_behind(eigen[:, :band_len], "row", -1)
    extended = jnp.concatenate([eigen, below], axis=1)

    def section(moment, state):
        finished = lax.cond(
            row_index == moment,
            lambda inside: run_spans(inside, vectors, offsets, band_len),
            lambda inside: inside,
            state,
        )
        arrived = from_behind(finished[:, rows_dev:], "row", 1)
        replaced = lax.dynamic_update_slice_in_dim(finished, arrived, 0, 1)
        return jnp.where(row_index == moment + 1, replaced, finished)

    extended = lax.fori_loop(0, row_count, section, extended)
    return extended[:, :rows_dev]


def panel_update(eigen, reflect, gram_mat, inner):
    coeffs = upper_solve(wy_matrix(gram_mat), inner)
    return eigen - lax.dot_general(
        coeffs.astype(jnp.bfloat16), reflect, CONTRACT_FIRST, preferred_element_type=jnp.float32
    )


def local_sums(reflect, eigen):
    gram_mat = lax.dot_general(reflect, reflect, CONTRACT_LAST, preferred_element_type=jnp.float32)
    inner = lax.dot_general(
        reflect, eigen.astype(jnp.bfloat16), CONTRACT_LAST, preferred_element_type=jnp.float32
    )
    return (gram_mat, inner)


def local(eigvecs, span_vectors, span_offsets, panels):
    band_len = span_vectors.shape[3]
    eigen = eigvecs
    for sweep_at in range(span_vectors.shape[0]):
        eigen = sweep_chain(eigen, span_vectors[sweep_at], span_offsets[sweep_at], band_len)
    gathered = gather_axes(panels, COL, (0, 1), 1)
    for panel_at in range(gathered.shape[0]):
        reflect = gathered[panel_at]
        gram_mat, inner = local_sums(reflect, eigen)
        gram_mat, inner = (
            over_copies(gram_mat.astype(jnp.bfloat16), "row").astype(jnp.float32),
            over_copies(inner.astype(jnp.bfloat16), "row").astype(jnp.float32),
        )
        eigen = panel_update(eigen, reflect, gram_mat, inner)
    return eigen


def solution(mesh):
    finer = Mesh(mesh.devices.reshape(mesh.shape["row"], 4, 8), ("row", "col_0", "col_1"))
    placed = (P(COL, "row"), P(None, "row", None, None), P(None, "row"), P(None, COL, "row"))
    return jax.shard_map(
        local, mesh=finer, in_specs=placed, out_specs=P(COL, "row"), check_vma=False
    )
```

profile of v0, /device:TPU:1, one launch (start us, length us, event | category | flops | bytes accessed | tf_op | source)
XLA Modules:
  0.0 2024.3 jit_solution(10539556407410454324)
XLA Ops:
  7.3 34.7 %all-gather.6.cloned.1.call-done = bf16[8,8,12544]{2,1,0:T(8,128)(2,1)} async-done(((bf16[2,8,12544]{2,1,0:T(8,128)(2,1)}), bf16[8,8,12544]{2,1,0:T(8,128)(2,1)}) %all-gather.6.cloned.1.call-update) | async-done | bytes 1605648 | tf_op jit(solution)/shard_map/all_gather | solution.py:29
  42.1 2.7 collective-permute-start.2
  44.9 2.4 collective-permute-done.2
  47.5 447.9 %while.90 = (s32[]{:T(128)}, f32[32,12672]{1,0:T(8,128)S(1)}, s32[]{:T(128)}, s32[8]{0:T(128)S(1)}, bf16[8,4,128]{2,1,0:T(4,128)(2,1)S(1)}, /*index=5*/s32[]{:T(128)}) while((s32[]{:T(128)}, f32[32,12672]{1,0:T(8,128)S(1)}, s32[]{:T(128)}, s32[8]{0:T(128)S(1)}, bf16[8,4,128]{2,1,0:T(4,128)(2,1)S(1)}, /*index=5*/s32[]{:T(128)}) %tuple.233), condition=%wide.region_5.6_spmd, body=%wide.region_0.5_spmd.sunk | while | flops 79610 | bytes 228376 | solution.py:114
  47.5 1.9 collective-permute-start.1
  49.5 82.8 %collective-permute-done.1 = f32[32,128]{1,0:T(8,128)S(1)} collective-permute-done((f32[32,128]{1,0:T(8,128)S(1)}, f32[32,128]{1,0:T(8,128)S(1)}, u32[]{:S(2)}, u32[]{:S(2)}) %collective-permute-start.1) | collective-permute-done | bytes 16416 | tf_op jit(solution)/shard_map/while/body/eval_jaxpr/ppermute | solution.py:17
  132.3 84.1 %conditional.4 = (f32[32,12672]{1,0:T(8,128)S(1)}) conditional(s32[]{:T(128)} %convert_element_type.92, f32[32,12672]{1,0:T(8,128)S(1)} %get-tuple-element.1018, (s32[8]{0:T(128)S(1)}, bf16[8,4,128]{2,1,0:T(4,128)(2,1)S(1)}, f32[32,12672]{1,0:T(8,128)S(1)}) %tuple.216), branch_computations={%region_1.0_spmd, %region_2.4_spmd} | conditional | flops 75509 | bytes 80763 | solution.py:104
  132.3 84.1 %while.88 = (s32[]{:T(128)}, f32[32,12672]{1,0:T(8,128)S(1)}, s32[8]{0:T(128)S(1)}, bf16[8,4,128]{2,1,0:T(4,128)(2,1)S(1)}, s32[]{:T(128)}, /*index=5*/s32[]{:T(128)}, s32[]{:T(128)}) while((s32[]{:T(128)}, f32[32,12672]{1,0:T(8,128)S(1)}, s32[8]{0:T(128)S(1)}, bf16[8,4,128]{2,1,0:T(4,128)(2,1)S(1)}, s32[]{:T(128)}, /*index=5*/s32[]{:T(128)}, ...), condition=%wide.region_4.3_spmd, body=%wide.region_3.2_spmd.sunk | while | flops 75509 | bytes 80691 | solution.py:93
  136.2 6.0 subtract_divide_fusion.13
  146.7 6.0 subtract_divide_fusion.13
  157.2 6.0 subtract_divide_fusion.13
  167.7 6.0 subtract_divide_fusion.13
  178.2 6.0 subtract_divide_fusion.13
  188.8 6.0 subtract_divide_fusion.13
  199.3 6.0 subtract_divide_fusion.13
  209.8 6.0 subtract_divide_fusion.13
  216.4 1.9 collective-permute-start.1
  219.5 88.0 %collective-permute-start.1 = (f32[32,128]{1,0:T(8,128)S(1)}, f32[32,128]{1,0:T(8,128)S(1)}, u32[]{:S(2)}, u32[]{:S(2)}) collective-permute-start(f32[32,128]{1,0:T(8,128)S(1)} %slice.356), channel_id=1, source_target_pairs={{0,32},{32,64},{64,96},{96,128},{128,160},{160,192},{192,224},{1,3... | collective-permute-start | bytes 49160 | tf_op jit(solution)/shard_map/while/body/eval_jaxpr/ppermute | solution.py:17
  308.4 4.2 collective-permute-start.1
  313.5 84.0 %collective-permute-start.1 = (f32[32,128]{1,0:T(8,128)S(1)}, f32[32,128]{1,0:T(8,128)S(1)}, u32[]{:S(2)}, u32[]{:S(2)}) collective-permute-start(f32[32,128]{1,0:T(8,128)S(1)} %slice.356), channel_id=1, source_target_pairs={{0,32},{32,64},{64,96},{96,128},{128,160},{160,192},{192,224},{1,3... | collective-permute-start | bytes 49160 | tf_op jit(solution)/shard_map/while/body/eval_jaxpr/ppermute | solution.py:17
  398.4 4.2 collective-permute-start.1
  403.4 86.0 %collective-permute-start.1 = (f32[32,128]{1,0:T(8,128)S(1)}, f32[32,128]{1,0:T(8,128)S(1)}, u32[]{:S(2)}, u32[]{:S(2)}) collective-permute-start(f32[32,128]{1,0:T(8,128)S(1)} %slice.356), channel_id=1, source_target_pairs={{0,32},{32,64},{64,96},{96,128},{128,160},{160,192},{192,224},{1,3... | collective-permute-start | bytes 49160 | tf_op jit(solution)/shard_map/while/body/eval_jaxpr/ppermute | solution.py:17
  490.3 4.2 collective-permute-start.1
  495.4 1.9 collective-permute-start.3
  497.4 83.4 %collective-permute-done.3 = f32[32,128]{1,0:T(8,128)S(1)} collective-permute-done((f32[32,128]{1,0:T(8,128)S(1)}, f32[32,128]{1,0:T(8,128)S(1)}, u32[]{:S(2)}, u32[]{:S(2)}) %collective-permute-start.3) | collective-permute-done | bytes 16416 | tf_op jit(solution)/shard_map/ppermute | solution.py:17
  581.0 10.7 copy.16
  591.7 389.0 %while.91 = (s32[]{:T(128)}, f32[32,12672]{1,0:T(8,128)S(1)}, s32[]{:T(128)}, s32[8]{0:T(128)S(1)}, bf16[8,4,128]{2,1,0:T(4,128)(2,1)S(1)}, /*index=5*/s32[]{:T(128)}) while((s32[]{:T(128)}, f32[32,12672]{1,0:T(8,128)S(1)}, s32[]{:T(128)}, s32[8]{0:T(128)S(1)}, bf16[8,4,128]{2,1,0:T(4,128)(2,1)S(1)}, /*index=5*/s32[]{:T(128)}) %tuple.236), condition=%wide.region_11.12_spmd, body=%wide.region_6.11_spmd.sunk | while | flops 79610 | bytes 228376 | solution.py:114
  591.7 3.5 collective-permute-start
  595.2 4.7 collective-permute-done
  599.9 88.5 %conditional.5 = (f32[32,12672]{1,0:T(8,128)S(1)}) conditional(s32[]{:T(128)} %convert_element_type.93, f32[32,12672]{1,0:T(8,128)S(1)} %get-tuple-element.1036, (s32[8]{0:T(128)S(1)}, bf16[8,4,128]{2,1,0:T(4,128)(2,1)S(1)}, f32[32,12672]{1,0:T(8,128)S(1)}) %tuple.218), branch_computations={%region_7.7_spmd, %region_8.10_spmd} | conditional | flops 75509 | bytes 80763 | solution.py:104
  599.9 88.5 %while.89 = (s32[]{:T(128)}, f32[32,12672]{1,0:T(8,128)S(1)}, s32[8]{0:T(128)S(1)}, bf16[8,4,128]{2,1,0:T(4,128)(2,1)S(1)}, s32[]{:T(128)}, /*index=5*/s32[]{:T(128)}, s32[]{:T(128)}) while((s32[]{:T(128)}, f32[32,12672]{1,0:T(8,128)S(1)}, s32[8]{0:T(128)S(1)}, bf16[8,4,128]{2,1,0:T(4,128)(2,1)S(1)}, s32[]{:T(128)}, /*index=5*/s32[]{:T(128)}, ...), condition=%wide.region_10.9_spmd, body=%wide.region_9.8_spmd.sunk | while | flops 75509 | bytes 80691 | solution.py:93
  604.1 6.2 subtract_divide_fusion.12
  615.1 6.2 subtract_divide_fusion.12
  626.2 6.2 subtract_divide_fusion.12
  637.3 6.2 subtract_divide_fusion.12
  648.3 6.2 subtract_divide_fusion.12
  659.4 6.2 subtract_divide_fusion.12
  670.5 6.2 subtract_divide_fusion.12
  681.5 6.2 subtract_divide_fusion.12
  688.4 1.9 collective-permute-start
  690.4 1.1 collective-permute-done
  691.5 92.5 %collective-permute-start = (f32[32,128]{1,0:T(8,128)S(1)}, f32[32,128]{1,0:T(8,128)S(1)}, u32[]{:S(2)}, u32[]{:S(2)}) collective-permute-start(f32[32,128]{1,0:T(8,128)S(1)} %slice.357), channel_id=1, source_target_pairs={{0,32},{32,64},{64,96},{96,128},{128,160},{160,192},{192,224},{1,3... | collective-permute-start | bytes 49160 | tf_op jit(solution)/shard_map/while/body/eval_jaxpr/ppermute | solution.py:17
  784.9 4.2 collective-permute-start
  789.9 88.5 %collective-permute-start = (f32[32,128]{1,0:T(8,128)S(1)}, f32[32,128]{1,0:T(8,128)S(1)}, u32[]{:S(2)}, u32[]{:S(2)}) collective-permute-start(f32[32,128]{1,0:T(8,128)S(1)} %slice.357), channel_id=1, source_target_pairs={{0,32},{32,64},{64,96},{96,128},{128,160},{160,192},{192,224},{1,3... | collective-permute-start | bytes 49160 | tf_op jit(solution)/shard_map/while/body/eval_jaxpr/ppermute | solution.py:17
  879.3 4.2 collective-permute-start
  884.3 90.5 %collective-permute-start = (f32[32,128]{1,0:T(8,128)S(1)}, f32[32,128]{1,0:T(8,128)S(1)}, u32[]{:S(2)}, u32[]{:S(2)}) collective-permute-start(f32[32,128]{1,0:T(8,128)S(1)} %slice.357), channel_id=1, source_target_pairs={{0,32},{32,64},{64,96},{96,128},{128,160},{160,192},{192,224},{1,3... | collective-permute-start | bytes 49160 | tf_op jit(solution)/shard_map/while/body/eval_jaxpr/ppermute | solution.py:17
  975.7 4.2 collective-permute-start
  980.7 4.8 fusion.62
  986.2 266.2 %all-to-all-start = ((bf16[8,256,32]{1,2,0:T(8,128)(2,1)}), bf16[8,256,32]{1,2,0:T(8,128)(2,1)S(1)}, u32[]{:S(2)}, u32[]{:S(2)}) async-start(bf16[8,256,32]{1,2,0:T(8,128)(2,1)} %broadcast_in_dim.142), calls=%async_computation | async-start | bytes 262144 | tf_op jit(solution)/shard_map/all_to_all | solution.py:42
  1252.4 6.7 fusion.59
  1260.1 4.8 all-to-all-start.1
  1264.9 6.6 fusion.58
  1271.6 8.3 all-to-all-done.1
  1280.9 5.1 all-to-all-start.3
  1286.2 2.3 gather_fusion.2
  1288.7 343.0 %while.92 = (s32[]{:T(128)}, bf16[256,32]{1,0:T(8,128)(2,1)S(1)}, f32[256,32]{1,0:T(8,128)S(1)}, f32[256,256]{1,0:T(8,128)S(1)}, s32[]{:T(128)}, /*index=5*/s32[]{:T(128)}, s32[]{:T(128)}, s32[]{:T(128)}) while((s32[]{:T(128)}, bf16[256,32]{1,0:T(8,128)(2,1)S(1)}, f32[256,32]{1,0:T(8,128)S(1)}, f32[256,256]{1,0:T(8,128)S(1)}, s32[]{:T(128)}, ...), condition=%wide.region_15.16_spmd, body=%wide.region_14.15_spmd.sunk | while | flops 16487 | bytes 68463 | solution.py:74
  1631.7 4.1 convolution_subtract_fusion.3
  1635.8 4.8 fusion.63
  1641.3 4.8 all-to-all-start.2
  1646.1 1.4 convert_reduce_fusion
  1647.5 2.3 gather_fusion.3
  1650.0 1.4 all-to-all-done.2
  1651.5 360.7 %while.93 = (s32[]{:T(128)}, bf16[256,32]{1,0:T(8,128)(2,1)S(1)}, f32[256,32]{1,0:T(8,128)S(1)}, f32[256,256]{1,0:T(8,128)S(1)}, s32[]{:T(128)}, /*index=5*/s32[]{:T(128)}, s32[]{:T(128)}, s32[]{:T(128)}) while((s32[]{:T(128)}, bf16[256,32]{1,0:T(8,128)(2,1)S(1)}, f32[256,32]{1,0:T(8,128)S(1)}, f32[256,256]{1,0:T(8,128)S(1)}, s32[]{:T(128)}, ...), condition=%wide.region_19.20_spmd, body=%wide.region_18.19_spmd.sunk | while | flops 16487 | bytes 68463 | solution.py:74
  2012.2 5.3 convolution_subtract_fusion.2
  (1773 shorter events, 757.5 us)
Async XLA Ops:
  6.5 35.5 %copy-start = (f32[32,12544]{1,0:T(8,128)S(1)}, f32[32,12544]{1,0:T(8,128)}, u32[]{:S(2)}) copy-start(f32[32,12544]{1,0:T(8,128)} %param.20) | copy-start | bytes 4816900
  6.5 38.3 %copy-start.1 = (f32[2,8,4,128]{3,2,1,0:T(4,128)S(1)}, f32[2,8,4,128]{3,2,1,0:T(4,128)}, u32[]{:S(2)}) copy-start(f32[2,8,4,128]{3,2,1,0:T(4,128)} %param.21) | copy-start | bytes 98308
  6.5 38.3 %copy-start.2 = (s32[2,8]{1,0:T(2,128)S(1)}, s32[2,8]{1,0:T(2,128)}, u32[]{:S(2)}) copy-start(s32[2,8]{1,0:T(2,128)} %param.22) | copy-start | bytes 196
  6.5 35.5 %all-gather.6.cloned.1.call-start = ((), (), s32[]{:S(2)}) async-start(), calls=%async_computation.5 | async-start | bytes 2007040 | tf_op jit(solution)/shard_map/all_gather | solution.py:29
  7.3 573.7 %all-gather.4.cloned.1.call-start = ((), (), s32[]{:S(2)}) async-start(), calls=%async_computation.4 | async-start | bytes 14450688 | tf_op jit(solution)/shard_map/all_gather | solution.py:29
  42.1 5.3 collective-permute-start.2
  47.5 84.8 %collective-permute-start.1 = (f32[32,128]{1,0:T(8,128)S(1)}, f32[32,128]{1,0:T(8,128)S(1)}, u32[]{:S(2)}, u32[]{:S(2)}) collective-permute-start(f32[32,128]{1,0:T(8,128)S(1)} %slice.356), channel_id=1, source_target_pairs={{0,32},{32,64},{64,96},{96,128},{128,160},{160,192},{192,224},{1,3... | collective-permute-start | bytes 49160 | tf_op jit(solution)/shard_map/while/body/eval_jaxpr/ppermute | solution.py:17
  216.4 3.1 collective-permute-start.1
  219.5 88.9 %collective-permute-start.1 = (f32[32,128]{1,0:T(8,128)S(1)}, f32[32,128]{1,0:T(8,128)S(1)}, u32[]{:S(2)}, u32[]{:S(2)}) collective-permute-start(f32[32,128]{1,0:T(8,128)S(1)} %slice.356), channel_id=1, source_target_pairs={{0,32},{32,64},{64,96},{96,128},{128,160},{160,192},{192,224},{1,3... | collective-permute-start | bytes 49160 | tf_op jit(solution)/shard_map/while/body/eval_jaxpr/ppermute | solution.py:17
  308.4 5.1 collective-permute-start.1
  313.5 84.9 %collective-permute-start.1 = (f32[32,128]{1,0:T(8,128)S(1)}, f32[32,128]{1,0:T(8,128)S(1)}, u32[]{:S(2)}, u32[]{:S(2)}) collective-permute-start(f32[32,128]{1,0:T(8,128)S(1)} %slice.356), channel_id=1, source_target_pairs={{0,32},{32,64},{64,96},{96,128},{128,160},{160,192},{192,224},{1,3... | collective-permute-start | bytes 49160 | tf_op jit(solution)/shard_map/while/body/eval_jaxpr/ppermute | solution.py:17
  398.4 5.1 collective-permute-start.1
  403.4 86.9 %collective-permute-start.1 = (f32[32,128]{1,0:T(8,128)S(1)}, f32[32,128]{1,0:T(8,128)S(1)}, u32[]{:S(2)}, u32[]{:S(2)}) collective-permute-start(f32[32,128]{1,0:T(8,128)S(1)} %slice.356), channel_id=1, source_target_pairs={{0,32},{32,64},{64,96},{96,128},{128,160},{160,192},{192,224},{1,3... | collective-permute-start | bytes 49160 | tf_op jit(solution)/shard_map/while/body/eval_jaxpr/ppermute | solution.py:17
  490.3 5.1 collective-permute-start.1
  495.4 85.4 %collective-permute-start.3 = (f32[32,128]{1,0:T(8,128)S(1)}, f32[32,128]{1,0:T(8,128)S(1)}, u32[]{:S(2)}, u32[]{:S(2)}) collective-permute-start(f32[32,128]{1,0:T(8,128)S(1)} %slice.253), channel_id=1, source_target_pairs={{32,0},{64,32},{96,64},{128,96},{160,128},{192,160},{224,192},{33,... | collective-permute-start | bytes 49160 | tf_op jit(solution)/shard_map/ppermute | solution.py:17
  591.7 8.2 collective-permute-start
  688.4 3.1 collective-permute-start
  691.5 93.3 %collective-permute-start = (f32[32,128]{1,0:T(8,128)S(1)}, f32[32,128]{1,0:T(8,128)S(1)}, u32[]{:S(2)}, u32[]{:S(2)}) collective-permute-start(f32[32,128]{1,0:T(8,128)S(1)} %slice.357), channel_id=1, source_target_pairs={{0,32},{32,64},{64,96},{96,128},{128,160},{160,192},{192,224},{1,3... | collective-permute-start | bytes 49160 | tf_op jit(solution)/shard_map/while/body/eval_jaxpr/ppermute | solution.py:17
  784.9 5.1 collective-permute-start
  789.9 89.3 %collective-permute-start = (f32[32,128]{1,0:T(8,128)S(1)}, f32[32,128]{1,0:T(8,128)S(1)}, u32[]{:S(2)}, u32[]{:S(2)}) collective-permute-start(f32[32,128]{1,0:T(8,128)S(1)} %slice.357), channel_id=1, source_target_pairs={{0,32},{32,64},{64,96},{96,128},{128,160},{160,192},{192,224},{1,3... | collective-permute-start | bytes 49160 | tf_op jit(solution)/shard_map/while/body/eval_jaxpr/ppermute | solution.py:17
  879.3 5.1 collective-permute-start
  884.3 91.3 %collective-permute-start = (f32[32,128]{1,0:T(8,128)S(1)}, f32[32,128]{1,0:T(8,128)S(1)}, u32[]{:S(2)}, u32[]{:S(2)}) collective-permute-start(f32[32,128]{1,0:T(8,128)S(1)} %slice.357), channel_id=1, source_target_pairs={{0,32},{32,64},{64,96},{96,128},{128,160},{160,192},{192,224},{1,3... | collective-permute-start | bytes 49160 | tf_op jit(solution)/shard_map/while/body/eval_jaxpr/ppermute | solution.py:17
  975.7 5.1 collective-permute-start
  986.2 272.9 %all-to-all-start = ((bf16[8,256,32]{1,2,0:T(8,128)(2,1)}), bf16[8,256,32]{1,2,0:T(8,128)(2,1)S(1)}, u32[]{:S(2)}, u32[]{:S(2)}) async-start(bf16[8,256,32]{1,2,0:T(8,128)(2,1)} %broadcast_in_dim.142), calls=%async_computation | async-start | bytes 262144 | tf_op jit(solution)/shard_map/all_to_all | solution.py:42
  1260.1 19.8 all-to-all-start.1
  1280.9 359.6 %all-to-all-start.3 = ((bf16[8,256,256]{2,1,0:T(8,128)(2,1)}), bf16[8,256,256]{2,1,0:T(8,128)(2,1)}, u32[]{:S(2)}, u32[]{:S(2)}) async-start(bf16[8,256,256]{2,1,0:T(8,128)(2,1)} %broadcast_in_dim.147), calls=%async_computation.3 | async-start | bytes 2097152 | tf_op jit(solution)/shard_map/all_to_all | solution.py:42
  1641.3 10.1 all-to-all-start.2
Sparse Core Ops, SparseCore 0:
  9.1 32.8 all-gather.5
  43.8 135.8 all-gather.3
where the time goes:
time: 2030 us; the launch traced here: 2020 us
  starting transfers between devices  850 us (42%)
  matrix products  416 us (20%)
  local copies, waits for them, and re-layouts  375 us (18%)
  waiting for transfers between devices  231 us (11%)
  other arithmetic  101 us (5%)
  loops' own time  38 us (2%)
    ppermute x18, starting transfers between devices, from_behind(): lax.ppermute(value, axis, [(source, source + steps) for source in range(f...  569 us
    dot_general x512, matrix products, step(): partial_sum = jnp.dot(matrow, solution)  377 us
    dynamic_slice x512, local copies, waits for them, and re-layouts, step(): pivot = lax.dynamic_index_in_dim(matrow, place, 0, keepdims=False)  303 us
    all_to_all x4, starting transfers between devices, sent_to_all(): lax.all_to_all(jnp.broadcast_to(x[None], (peers, *x.shape)), axis, 0, 0,...  281 us
    ppermute x18, waiting for transfers between devices, from_behind(): lax.ppermute(value, axis, [(source, source + steps) for source in range(f...  186 us
    div x16, other arithmetic, upper_solve(): solved[back_at] = value / matrix[back_at, back_at]  97.9 us
  transfers between devices with their start and end apart: 24, of which 21 were waited for; matrix products, arithmetic and copies ran while one was open for 22% of the time, Pallas kernels for 0%

commit v1 on v0

v1 whole, which is shorter than its diff:
```python
import functools

import jax
import jax.numpy as jnp
from jax import lax
from jax.experimental import pallas as pl
from jax.experimental.pallas import tpu as pltpu
from jax.sharding import Mesh
from jax.sharding import PartitionSpec as P

LANE = 128
BLOCK = 128
NX = 4
NZ = 8
F32 = jnp.float32
BF16 = jnp.bfloat16
HI = lax.Precision.HIGHEST
NT = (((1,), (1,)), ((), ()))
NN = (((1,), (0,)), ((), ()))


def dot_hi(a, b, dims=NN):
    return lax.dot_general(a, b, dims, precision=HI, preferred_element_type=F32)


def halves(a):
    top = a.astype(BF16)
    return top, (a - top.astype(F32)).astype(BF16)


def dot3(a, b):
    a_top, a_low = halves(a)
    b_top, b_low = halves(b)
    d = functools.partial(lax.dot_general, dimension_numbers=NN, preferred_element_type=F32)
    return d(a_top, b_top) + (d(a_top, b_low) + d(a_low, b_top))


def solve_wy(gram, right, unit):
    order = gram.shape[0]
    p = lax.broadcasted_iota(jnp.int32, gram.shape, 0)
    q = lax.broadcasted_iota(jnp.int32, gram.shape, 1)
    on_diag = p == q
    same = (p // unit) == (q // unit)
    keep = (same & (p > q)) | (jnp.logical_not(same) & (p < q))
    picked = jnp.where(on_diag, gram, 0.0)
    down = 2.0 / jnp.sum(picked, axis=1, keepdims=True)
    across = 2.0 / jnp.sum(picked, axis=0, keepdims=True)
    strict = jnp.where(keep, gram * down, 0.0)
    bp = lax.broadcasted_iota(jnp.int32, (BLOCK, BLOCK), 0)
    bq = lax.broadcasted_iota(jnp.int32, (BLOCK, BLOCK), 1)
    count = order // BLOCK
    tiles = [strict[t * BLOCK : (t + 1) * BLOCK, t * BLOCK : (t + 1) * BLOCK] for t in range(count)]
    eye = (bp == bq).astype(F32)
    inverse = [eye - jnp.where(bp // 2 == bq // 2, tile, 0.0) for tile in tiles]
    size = 2
    while size < BLOCK:
        joined = (bp // (2 * size) == bq // (2 * size)) & (bp // size != bq // size)
        middle = [jnp.where(joined, tile, 0.0) for tile in tiles]
        left = [dot3(inverse[t], middle[t]) for t in range(count)]
        inverse = [inverse[t] - dot3(left[t], inverse[t]) for t in range(count)]
        size *= 2
    per = max(1, unit // BLOCK)
    sequence = [base + k for base in range(0, count, per) for k in reversed(range(per))]
    found = [None] * count
    done = []
    for t in sequence:
        value = right[:, t * BLOCK : (t + 1) * BLOCK]
        for u in done:
            value = value - dot3(found[u], strict[u * BLOCK : (u + 1) * BLOCK, t * BLOCK : (t + 1) * BLOCK])
        found[t] = dot3(value, inverse[t])
        done.append(t)
    return jnp.concatenate(found, axis=1) * across


def span_products(tiles_dev, own_tile, vectors, shift, tile_down, tile_across, own, own_shift, prev, prev_shift,
                  prev_over, eigen, gram_ref, own_ref, prev_ref, inner_ref, windows):
    def placed(values, amount):
        wide = jnp.concatenate([values, jnp.zeros_like(values)], axis=1)
        for bit in range(7):
            wide = jnp.where(((amount >> bit) & 1) == 1, pltpu.roll(wide, 1 << bit, 1), wide)
        return wide

    wide = placed(vectors[...], shift[...])
    low, high = wide[:, :LANE], wide[:, LANE:]
    down, across = tile_down[...], tile_across[...]
    level = dot_hi(wide, wide, NT)
    after = dot_hi(high, low, NT)
    before = dot_hi(low, high, NT)
    gram_ref[...] = jnp.where(
        down == across,
        level,
        jnp.where(across == down + 1, after, jnp.where(across == down - 1, before, 0.0)),
    )
    own_wide = placed(own[...], own_shift[...])
    own_ref[...] = own_wide
    prev_high = jnp.where(prev_over[...] == 1, placed(prev[...], prev_shift[...])[:, LANE:], 0.0)
    prev_ref[...] = prev_high
    rows = eigen.shape[0]
    count = own_tile.shape[0]
    for c in range(count):
        at = own_tile[c]
        inside = jnp.where(at + 1 < tiles_dev, 1.0, 0.0).astype(F32)
        then = jnp.minimum(at + 1, tiles_dev - 1)
        windows[c * rows : (c + 1) * rows, :LANE] = eigen[:, pl.ds(pl.multiple_of(at * LANE, LANE), LANE)]
        windows[c * rows : (c + 1) * rows, LANE:] = (
            eigen[:, pl.ds(pl.multiple_of(then * LANE, LANE), LANE)] * inside
        )
    table = dot_hi(windows[...], own_wide, NT)
    width = own_wide.shape[0]
    place = lax.broadcasted_iota(jnp.int32, (rows, width), 1) // (width // count)
    total = jnp.zeros((rows, width), F32)
    for c in range(count):
        total = total + jnp.where(place == c, table[c * rows : (c + 1) * rows], 0.0)
    behind = dot_hi(eigen[:, :LANE], prev_high, NT)
    inner_ref[...] = jnp.concatenate([total, behind], axis=1)


def span_coeffs(unit, gram, right, coeffs):
    coeffs[...] = solve_wy(gram[...], right[...], unit)


def span_apply(tiles_dev, own_tile, eigen, own_wide, prev_high, own_coeffs, prev_coeffs, out, rounded):
    rows, cols = eigen.shape
    count = own_tile.shape[0]
    width = own_wide.shape[0]
    out[...] = eigen[...]
    mine = own_coeffs[...]
    place = lax.broadcasted_iota(jnp.int32, (rows, width), 1) // (width // count)
    spread = jnp.concatenate([jnp.where(place == c, mine, 0.0) for c in range(count)], axis=0)
    change = dot_hi(spread, own_wide[...])
    out[:, :LANE] = out[:, :LANE] - dot_hi(prev_coeffs[...], prev_high[...])
    for c in range(count):
        at = own_tile[c]
        inside = jnp.where(at + 1 < tiles_dev, 1.0, 0.0).astype(F32)
        then = jnp.minimum(at + 1, tiles_dev - 1)
        first = pl.ds(pl.multiple_of(at * LANE, LANE), LANE)
        second = pl.ds(pl.multiple_of(then * LANE, LANE), LANE)
        out[:, first] = out[:, first] - change[c * rows : (c + 1) * rows, :LANE]
        out[:, second] = out[:, second] - change[c * rows : (c + 1) * rows, LANE:] * inside
    rounded[:, :cols] = out[...].astype(BF16)
    rounded[:, cols:] = jnp.zeros((rows, rounded.shape[1] - cols), BF16)


def panel_coeffs(unit, gram, right, coeffs):
    coeffs[...] = solve_wy(gram[...].astype(F32), right[...].astype(F32), unit).astype(BF16)


def sent_to_all(x, axis):
    peers = lax.psum(1, axis)
    return lax.all_to_all(jnp.broadcast_to(x[None], (peers, *x.shape)), axis, 0, 0, tiled=True)


def call(kernel, outs, smem, *args, scratch=(), cost=2_000_000_000):
    specs = [pl.BlockSpec(memory_space=pltpu.SMEM)] * smem
    specs += [pl.BlockSpec(memory_space=pltpu.VMEM)] * (len(args) - smem)
    return pl.pallas_call(
        kernel,
        out_shape=[jax.ShapeDtypeStruct(s, d) for s, d in outs],
        in_specs=specs,
        out_specs=[pl.BlockSpec(memory_space=pltpu.VMEM)] * len(outs),
        scratch_shapes=list(scratch),
        compiler_params=pltpu.CompilerParams(vmem_limit_bytes=40 * 1024 * 1024),
        cost_estimate=pl.CostEstimate(flops=cost, bytes_accessed=4_000_000, transcendentals=0),
    )(*args)


def local(eigvecs, span_vectors, span_offsets, panels):
    rows, cols = eigvecs.shape
    sweeps, spans_dev, refl, band = span_vectors.shape
    n_row = lax.psum(1, "row")
    row = lax.axis_index("row")
    tiles_dev = cols // LANE
    part = -(-tiles_dev // NX) * LANE
    full = part * NX
    n_panel, refl_dev, _ = panels.shape
    width = refl_dev * NX * NZ
    every = n_panel * width

    padded = jnp.pad(panels, ((0, 0), (0, 0), (0, full - cols)))
    cut = padded.reshape(n_panel, refl_dev, NX, part).transpose(2, 0, 1, 3)
    block = lax.all_to_all(cut, "cx", 0, 0, tiled=True)
    up = [(k, (k + 1) % NZ) for k in range(NZ)]
    down = [(k, (k - 1) % NZ) for k in range(NZ)]
    blocks = {0: block}
    forward = backward = block
    for step in range(1, NZ // 2 + 1):
        forward = lax.ppermute(forward, "cz", up)
        blocks[step] = forward
        if step < NZ - step:
            backward = lax.ppermute(backward, "cz", down)
            blocks[NZ - step] = backward

    per_dev = sweeps * spans_dev * refl
    flat_off = span_offsets.reshape(1, sweeps * spans_dev).astype(F32)
    note = jnp.pad(flat_off, ((0, 7), (0, band - sweeps * spans_dev)))
    pack = jnp.concatenate([span_vectors.reshape(per_dev, band), note], axis=0)
    packs = sent_to_all(pack, "row").reshape(n_row, per_dev + 8, band)
    by_row = packs[:, :per_dev]
    half = spans_dev * refl
    vectors = by_row.reshape(n_row, sweeps, half, band).transpose(1, 0, 2, 3).reshape(-1, band)
    offs = packs[:, per_dev, : sweeps * spans_dev].astype(jnp.int32)
    tile_dev = jnp.repeat(offs // LANE, refl, axis=1)
    shift_dev = jnp.repeat(offs % LANE, refl, axis=1)

    def swept(x):
        return x.reshape(n_row, sweeps, half).transpose(1, 0, 2).reshape(-1)

    tile_all = swept(tile_dev + jnp.arange(n_row, dtype=jnp.int32)[:, None] * tiles_dev)
    shift_all = swept(shift_dev)
    prev_row = jnp.maximum(row - 1, 0)
    own = span_vectors.reshape(per_dev, band)
    own_tile = span_offsets.reshape(-1) // LANE
    own_shift = jnp.repeat(span_offsets.reshape(-1) % LANE, refl)[:, None]
    prev = lax.dynamic_index_in_dim(by_row, prev_row, 0, keepdims=False)
    prev_shift = lax.dynamic_index_in_dim(shift_dev, prev_row, 0, keepdims=False)[:, None]
    prev_tile = lax.dynamic_index_in_dim(tile_dev, prev_row, 0, keepdims=False)[:, None]
    prev_over = ((prev_tile == tiles_dev - 1) & (row > 0)).astype(jnp.int32)
    total = n_row * per_dev
    gram, own_wide, prev_high, inner = call(
        functools.partial(span_products, tiles_dev),
        [((total, total), F32), ((per_dev, 2 * LANE), F32), ((per_dev, LANE), F32), ((rows, 2 * per_dev), F32)],
        1,
        own_tile, vectors, shift_all[:, None], tile_all[:, None], tile_all[None, :], own, own_shift, prev,
        prev_shift, prev_over, eigvecs,
        scratch=[pltpu.VMEM((sweeps * spans_dev * rows, 2 * LANE), F32)],
    )
    inners = sent_to_all(inner, "row").reshape(n_row, rows, 2, sweeps, half)
    sums = inners[:, :, 0] + jnp.pad(inners[1:, :, 1], ((0, 1), (0, 0), (0, 0), (0, 0)))
    right = sums.transpose(1, 2, 0, 3).reshape(rows, total)
    (coeffs,) = call(functools.partial(span_coeffs, refl), [((rows, total), F32)], 0, gram, right)
    by_sweep = coeffs.reshape(rows, sweeps, n_row, half)
    own_coeffs = lax.dynamic_index_in_dim(by_sweep, row, 2, keepdims=False).reshape(rows, per_dev)
    prev_coeffs = lax.dynamic_index_in_dim(by_sweep, prev_row, 2, keepdims=False).reshape(rows, per_dev)
    eigen, rounded = call(
        functools.partial(span_apply, tiles_dev),
        [((rows, cols), F32), ((rows, full), BF16)],
        1,
        own_tile, eigvecs, own_wide, prev_high, own_coeffs, prev_coeffs,
    )

    traded = lax.all_to_all(rounded.reshape(rows, NX, part).transpose(1, 0, 2), "cx", 0, 0, tiled=True)
    traded = traded.reshape(NX * rows, part)
    at_z = lax.axis_index("cz")
    gathered = jnp.zeros((n_panel, NX, NZ, refl_dev, part), BF16)
    for step in range(NZ):
        piece = blocks[step].transpose(1, 0, 2, 3)[:, :, None]
        gathered = lax.dynamic_update_slice(gathered, piece, (0, 0, (at_z - step) % NZ, 0, 0))
    reflect = gathered.reshape(every, part)
    gram_mat = lax.dot_general(reflect, reflect, NT, preferred_element_type=F32)
    inner_mat = lax.dot_general(traded, reflect, NT, preferred_element_type=F32)
    group = n_row * NX
    piece_rows = every // group
    sending = jnp.concatenate(
        [
            gram_mat.astype(BF16).reshape(group, piece_rows, every),
            inner_mat.astype(BF16).reshape(group, piece_rows, -1),
        ],
        axis=2,
    )
    arrived = lax.all_to_all(sending, ("row", "cx"), 0, 0, tiled=True)
    added = jnp.sum(arrived.astype(F32), axis=0).astype(BF16)
    whole = sent_to_all(added, ("row", "cx"))
    gram_sum = whole[:, :, :every].reshape(every, every)
    inner_sum = whole[:, :, every:].reshape(NX * rows, every)
    (coeffs_mat,) = call(
        functools.partial(panel_coeffs, width), [((NX * rows, every), BF16)], 0, gram_sum, inner_sum
    )
    update = lax.dot_general(coeffs_mat, reflect, NN, preferred_element_type=F32).astype(BF16)
    home = lax.all_to_all(update.reshape(NX, rows, part), "cx", 0, 0, tiled=True)
    home = home.transpose(1, 0, 2).reshape(rows, full)[:, :cols]
    return eigen - home.astype(F32)


def solution(mesh):
    finer = Mesh(mesh.devices.reshape(mesh.shape["row"], NX, NZ), ("row", "cx", "cz"))
    col = ("cx", "cz")
    placed = (P(col, "row"), P(None, "row", None, None), P(None, "row"), P(None, col, "row"))
    return jax.shard_map(local, mesh=finer, in_specs=placed, out_specs=P(col, "row"), check_vma=False)
```

time: 2030 us -> 163 us (0.08)
  starting transfers between devices: 850 us -> 30 us
  matrix products: 416 us -> 10.5 us
  local copies, waits for them, and re-layouts: 375 us -> 23.5 us
  waiting for transfers between devices: 231 us -> 27.5 us
  other arithmetic: 101 us -> 4.14 us
  blocking collectives: 0 us -> 53.1 us
  loops' own time: 38 us -> 0 us
    ppermute x18 -> x7, starting transfers between devices: 569 us -> 10.9 us  [the longest x3 9.28 us: local(): backward = lax.ppermute(backward, 'cz', down)]
    dot_general x566 -> x3, matrix products: 416 us -> 10.5 us  [the longest x1 4.87 us: local(): gram_mat = lax.dot_general(reflect, reflect, NT, preferred_element_type=F32)]
    dynamic_slice x528 -> x1, local copies, waits for them, and re-layouts: 312 us -> 0.05 us  [local(): lax.dynamic_index_in_dim(by_sweep, prev_row, 2, keepdims=False)]
    all_to_all x4 -> x2, starting transfers between devices: 281 us -> 11.7 us  [sent_to_all(): lax.all_to_all(jnp.broadcast_to(x[None], (peers, *x.shape)), axis, 0, 0,...]
    ppermute x18 -> x7, waiting for transfers between devices: 186 us -> 23.6 us  [the longest x4 23.6 us: local(): forward = lax.ppermute(forward, 'cz', up)]
    div x16 -> x0, other arithmetic: 97.9 us -> none  [upper_solve(): solved[back_at] = value / matrix[back_at, back_at]]
    all_to_all x0 -> x3, blocking collectives: none -> 53.1 us  [the longest x1 21.8 us: local(): arrived = lax.all_to_all(sending, ('row', 'cx'), 0, 0, tiled=True)]
    another operation x22 -> x0, loops' own time: 38 us -> none  [the longest x2 28.4 us: run_spans(): return lax.fori_loop(0, vectors.shape[0], advance, block)]
  transfers between devices with their start and end apart: 24 -> 11, of which waited for: 21 -> 4; matrix products, arithmetic and copies ran while one was open for 22% -> 16% of each run, Pallas kernels for 0% -> 6%
where the time goes in v1:
time: 163 us; the launch traced here: 162 us
  blocking collectives  53.1 us (33%)
  starting transfers between devices  30 us (18%)
  waiting for transfers between devices  27.5 us (17%)
  local copies, waits for them, and re-layouts  23.5 us (14%)
  Pallas kernels  13.1 us (8%)
  matrix products  10.5 us (6%)
  other arithmetic  4.14 us (3%)
    ppermute x4, waiting for transfers between devices, local(): forward = lax.ppermute(forward, 'cz', up)  23.6 us
    all_to_all x1, blocking collectives, local(): arrived = lax.all_to_all(sending, ('row', 'cx'), 0, 0, tiled=True)  21.8 us
    all_to_all x1, blocking collectives, sent_to_all(): lax.all_to_all(jnp.broadcast_to(x[None], (peers, *x.shape)), axis, 0, 0,...  16.9 us
    all_to_all x1, blocking collectives, local(): lax.all_to_all(update.reshape(NX, rows, part), 'cx', 0, 0, tiled=True)  14.4 us
    pallas_call x4, Pallas kernels, call(): pl.pallas_call(kernel, out_shape=[jax.ShapeDtypeStruct(s, d) for s, d in...  13.1 us
    all_to_all x2, starting transfers between devices, sent_to_all(): lax.all_to_all(jnp.broadcast_to(x[None], (peers, *x.shape)), axis, 0, 0,...  11.7 us
    ppermute x3, starting transfers between devices, local(): backward = lax.ppermute(backward, 'cz', down)  9.28 us
    dynamic_update_slice x8, local copies, waits for them, and re-layouts, local(): lax.dynamic_update_slice(gathered, piece, (0, 0, (at_z - step) % NZ, 0, 0))  8.49 us
  transfers between devices with their start and end apart: 11, of which 4 were waited for; matrix products, arithmetic and copies ran while one was open for 16% of the time, Pallas kernels for 6%

profile of v1, /device:TPU:1, one launch (start us, length us, event | category | flops | bytes accessed | tf_op | source)
XLA Modules:
  0.0 162.1 jit_solution(2504651884241039819)
XLA Ops:
  0.0 0.7 convert_element_type.45
  0.7 0.1 convert_element_type.46
  0.8 0.8 select_maximum_fusion
  1.5 0.7 broadcast_in_dim.59
  2.3 6.5 %all-to-all-start = ((f32[8,72,128]{2,1,0:T(8,128)}), f32[8,72,128]{2,1,0:T(8,128)S(1)}, u32[]{:S(2)}, u32[]{:S(2)}) async-start(f32[8,72,128]{2,1,0:T(8,128)} %broadcast_in_dim.59), calls=%async_computation | async-start | bytes 589824 | tf_op jit(solution)/shard_map/all_to_all | solution.py:150
  8.8 0.8 reshape.127
  9.6 1.0 pad.14
  10.6 0.1 reshape.139
  10.7 0.8 copy.102
  11.5 0.1 broadcast_in_dim.62
  11.6 0.1 broadcast_in_dim_reshape.18.own_shift
  11.7 3.9 %all-to-all-done = f32[8,72,128]{2,1,0:T(8,128)S(1)} async-done(((f32[8,72,128]{2,1,0:T(8,128)}), f32[8,72,128]{2,1,0:T(8,128)S(1)}, u32[]{:S(2)}, u32[]{:S(2)}) %all-to-all-start) | async-done | bytes 294944 | tf_op jit(solution)/shard_map/all_to_all | solution.py:150
  15.6 3.5 %all-to-all-start.2 = ((bf16[4,2,8,3200]{3,2,1,0:T(8,128)(2,1)}), bf16[4,2,8,3200]{3,2,1,0:T(8,128)(2,1)S(1)}, u32[]{:S(2)}, u32[]{:S(2)}) async-start(bf16[4,2,8,3200]{3,2,1,0:T(8,128)(2,1)} %copy.102), calls=%async_computation.2 | async-start | bytes 819200 | tf_op jit(solution)/shard_map/all_to_all | solution.py:181
  19.1 0.1 copy.90
  19.2 0.1 copy.88
  19.3 0.1 dynamic-slice_bitcast_fusion.prev_shift
  19.5 0.3 broadcast_in_dim_reshape.17.tile_down
  19.7 0.1 broadcast_in_dim_reshape.14.tile_across
  19.9 0.3 broadcast_in_dim_reshape.16.shift
  20.2 0.1 convert_bitcast_fusion.prev_over
  20.3 5.1 %shard_map.46 = (f32[512,512]{1,0:T(8,128)S(1)}, f32[64,256]{1,0:T(8,128)S(1)}, f32[64,128]{1,0:T(8,128)S(1)}, f32[32,128]{1,0:T(8,128)S(1)}) custom-call(s32[16]{0:T(128)S(1)} %get-tuple-element.22.own_tile, f32[512,128]{1,0:T(8,128)S(1)} %bitcast.136, s32[512,1]{1,0:T(8,128)S(1)} %broadcast_in_dim_reshape.16.shift, ...), custom_call_target="tpu_custom_call" | custom-call | flops 2000000000 | bytes 4000000 | tf_op jit(solution)/shard_map/pallas_call | solution.py:156
  25.4 1.0 copy-done.2
  26.3 0.7 broadcast_in_dim.64
  27.0 5.2 %all-to-all-start.1 = ((f32[8,32,128]{2,1,0:T(8,128)}), f32[8,32,128]{2,1,0:T(8,128)S(1)}, u32[]{:S(2)}, u32[]{:S(2)}) async-start(f32[8,32,128]{2,1,0:T(8,128)} %broadcast_in_dim.64), calls=%async_computation.1 | async-start | bytes 262144 | tf_op jit(solution)/shard_map/all_to_all | solution.py:150
  32.2 0.8 copy.103
  32.9 1.6 %collective-permute-start = (bf16[4,2,8,3200]{3,2,0,1:T(8,128)(2,1)}, bf16[4,2,8,3200]{3,2,0,1:T(8,128)(2,1)}, u32[]{:S(2)}, u32[]{:S(2)}) collective-permute-start(bf16[4,2,8,3200]{3,2,0,1:T(8,128)(2,1)} %copy.103), channel_id=1, source_target_pairs={{0,1},{1,2},{2,3},{3,4},{4,5},{5,6},{6,7},{7,0},{8,9},{9,10},{10,1... | collective-permute-start | bytes 1228808 | tf_op jit(solution)/shard_map/ppermute | solution.py:187
  34.6 3.9 %collective-permute-start.4 = (bf16[4,2,8,3200]{3,2,0,1:T(8,128)(2,1)}, bf16[4,2,8,3200]{3,2,0,1:T(8,128)(2,1)}, u32[]{:S(2)}, u32[]{:S(2)}) collective-permute-start(bf16[4,2,8,3200]{3,2,0,1:T(8,128)(2,1)} %copy.103), channel_id=1, source_target_pairs={{0,7},{1,0},{2,1},{3,2},{4,3},{5,4},{6,5},{7,6},{8,15},{9,8},{10,9... | collective-permute-start | bytes 1228808 | tf_op jit(solution)/shard_map/ppermute | solution.py:190
  38.5 2.1 %broadcast_in_dim.65 = bf16[2,4,8,8,3200]{4,3,2,1,0:T(8,128)(2,1)} broadcast(bf16[]{:T(256)} %constant.135.clone.1), dimensions={} | broadcast | bytes 3276802 | tf_op jit(solution)/shard_map/broadcast_in_dim | solution.py:244
  40.6 0.8 bitcast_dynamic-update-slice_fusion.7
  41.4 1.2 reshape.134
  42.6 1.0 slice_bitcast_fusion.1
  43.6 1.1 fusion.1
  44.7 0.9 copy.99
  45.5 1.1 reshape.135.right
  46.6 3.4 %shard_map.47 = f32[32,512]{1,0:T(8,128)S(1)} custom-call(f32[512,512]{1,0:T(8,128)S(1)} %copy-done.3, f32[32,512]{1,0:T(8,128)S(1)} %reshape.135.right), custom_call_target="tpu_custom_call" | custom-call | flops 2000000000 | bytes 4000000 | tf_op jit(solution)/shard_map/pallas_call | solution.py:156
  50.0 0.1 reshape.136
  50.2 0.1 reshape.137.own_coeffs
  50.3 0.1 reshape.138.prev_coeffs
  50.4 1.4 shard_map.48
  51.8 0.9 copy.121
  52.7 3.9 %all-to-all-start.3 = ((bf16[4,32,3200]{2,1,0:T(8,128)(2,1)}), bf16[4,32,3200]{2,1,0:T(8,128)(2,1)S(1)}, u32[]{:S(2)}, u32[]{:S(2)}) async-start(bf16[4,32,3200]{2,1,0:T(8,128)(2,1)} %bitcast.132), calls=%async_computation.3 | async-start | bytes 1638400 | tf_op jit(solution)/shard_map/all_to_all | solution.py:241
  56.7 2.7 %collective-permute-start.5 = (bf16[4,2,8,3200]{3,2,0,1:T(8,128)(2,1)}, bf16[4,2,8,3200]{3,2,0,1:T(8,128)(2,1)S(1)}, u32[]{:S(2)}, u32[]{:S(2)}) collective-permute-start(bf16[4,2,8,3200]{3,2,0,1:T(8,128)(2,1)} %collective-permute-done.4), channel_id=1, source_target_pairs={{0,7},{1,0},{2,1},{3,2},{4,3},{5,4},{6,5},{7,6},{8,15},{9,8},{10,9... | collective-permute-start | bytes 1228808 | tf_op jit(solution)/shard_map/ppermute | solution.py:190
  59.3 1.8 %bitcast_dynamic-update-slice_fusion.6 = bf16[2,4,8,8,3200]{4,3,2,1,0:T(8,128)(2,1)} fusion(bf16[2,4,8,8,3200]{4,3,2,1,0:T(8,128)(2,1)} %bitcast_dynamic-update-slice_fusion.7, s32[]{:T(128)S(6)} %select_n.99, bf16[4,2,8,3200]{3,2,0,1:T(8,128)(2,1)} %collective-permute-done), kind=kLoop, calls=%fused_computation.12 | loop fusion | bytes 819204 | tf_op jit(solution)/shard_map/dynamic_update_slice | solution.py:247
  61.1 7.3 %collective-permute-done.1 = bf16[4,2,8,3200]{3,2,0,1:T(8,128)(2,1)S(1)} collective-permute-done((bf16[4,2,8,3200]{3,2,0,1:T(8,128)(2,1)}, bf16[4,2,8,3200]{3,2,0,1:T(8,128)(2,1)S(1)}, u32[]{:S(2)}, u32[]{:S(2)}) %collective-permute-start.1) | collective-permute-done | bytes 409632 | tf_op jit(solution)/shard_map/ppermute | solution.py:187
  68.4 2.7 %collective-permute-start.6 = (bf16[4,2,8,3200]{3,2,0,1:T(8,128)(2,1)S(1)}, bf16[4,2,8,3200]{3,2,0,1:T(8,128)(2,1)S(1)}, u32[]{:S(2)}, u32[]{:S(2)}) collective-permute-start(bf16[4,2,8,3200]{3,2,0,1:T(8,128)(2,1)S(1)} %collective-permute-done.5), channel_id=1, source_target_pairs={{0,7},{1,0},{2,1},{3,2},{4,3},{5,4},{6,5},{7,6},{8,15},{9,8},{10,9... | collective-permute-start | bytes 1228808 | tf_op jit(solution)/shard_map/ppermute | solution.py:190
  71.1 0.8 bitcast_dynamic-update-slice_fusion.5
  71.9 7.2 %collective-permute-done.2 = bf16[4,2,8,3200]{3,2,0,1:T(8,128)(2,1)S(1)} collective-permute-done((bf16[4,2,8,3200]{3,2,0,1:T(8,128)(2,1)S(1)}, bf16[4,2,8,3200]{3,2,0,1:T(8,128)(2,1)S(1)}, u32[]{:S(2)}, u32[]{:S(2)}) %collective-permute-start.2) | collective-permute-done | bytes 409632 | tf_op jit(solution)/shard_map/ppermute | solution.py:187
  79.1 0.8 bitcast_dynamic-update-slice_fusion.4
  80.0 9.0 %collective-permute-done.3 = bf16[4,2,8,3200]{3,2,0,1:T(8,128)(2,1)S(1)} collective-permute-done((bf16[4,2,8,3200]{3,2,0,1:T(8,128)(2,1)S(1)}, bf16[4,2,8,3200]{3,2,0,1:T(8,128)(2,1)S(1)}, u32[]{:S(2)}, u32[]{:S(2)}) %collective-permute-start.3) | collective-permute-done | bytes 409632 | tf_op jit(solution)/shard_map/ppermute | solution.py:187
  89.0 0.9 bitcast_dynamic-update-slice_fusion.3
  89.8 0.8 bitcast_dynamic-update-slice_fusion.2
  90.6 0.8 bitcast_dynamic-update-slice_fusion.1
  91.5 1.8 %bitcast_dynamic-update-slice_fusion = bf16[2,4,8,8,3200]{4,3,2,1,0:T(8,128)(2,1)} fusion(bf16[2,4,8,8,3200]{4,3,2,1,0:T(8,128)(2,1)} %bitcast_dynamic-update-slice_fusion.1, s32[]{:T(128)S(6)} %select_n.111, bf16[4,2,8,3200]{3,2,0,1:T(8,128)(2,1)} %collective-permute-done.4), kind=kLoop, calls=%fused_computation.6 | loop fusion | bytes 819204 | tf_op jit(solution)/shard_map/dynamic_update_slice | solution.py:247
  93.3 4.9 %convolution_convert_fusion.1 = bf16[512,512]{1,0:T(8,128)(2,1)S(1)} fusion(bf16[512,3200]{1,0:T(8,128)(2,1)} %bitcast.39), kind=kOutput, calls=%fused_computation.2 | convolution fusion | flops 1677983744 | bytes 3801088 | tf_op jit(solution)/shard_map/dot_general | solution.py:249
  98.2 3.1 %convolution_convert_fusion.2 = bf16[128,512]{1,0:T(8,128)(2,1)S(1)} fusion(bf16[128,3200]{1,0:T(8,128)(2,1)S(1)} %bitcast.140, bf16[512,3200]{1,0:T(8,128)(2,1)} %bitcast.39), kind=kOutput, calls=%fused_computation.3 | convolution fusion | flops 419495936 | bytes 4227072 | tf_op jit(solution)/shard_map/dot_general | solution.py:250
  101.3 0.1 reshape.144
  101.4 21.8 %all_to_all.35 = bf16[32,16,640]{2,1,0:T(8,128)(2,1)S(1)} all-to-all(bf16[32,16,640]{2,1,0:T(8,128)(2,1)S(1)} %pad_maximum_fusion), channel_id=1, replica_groups=mesh['row'=8,'cx'=4,'cz'=8] {'row','cx'}, dimensions={0} | all-to-all | bytes 1310720 | tf_op jit(solution)/shard_map/all_to_all | solution.py:260
  123.2 0.1 reduce_sum.12
  123.4 16.9 %all_to_all.36 = bf16[32,16,640]{2,1,0:T(8,128)(2,1)S(1)} all-to-all(bf16[32,16,640]{2,1,0:T(8,128)(2,1)S(1)} %broadcast_in_dim.74), channel_id=1, replica_groups=mesh['row'=8,'cx'=4,'cz'=8] {'row','cx'}, dimensions={0} | all-to-all | bytes 1310720 | tf_op jit(solution)/shard_map/all_to_all | solution.py:150
  140.3 0.1 reshape.146.right
  140.4 3.3 %shard_map.49 = bf16[128,512]{1,0:T(8,128)(2,1)S(1)} custom-call(bf16[512,512]{1,0:T(8,128)(2,1)S(1)} %bitcast.135, bf16[128,512]{1,0:T(8,128)(2,1)S(1)} %reshape.146.right), custom_call_target="tpu_custom_call" | custom-call | flops 2000000000 | bytes 4000000 | tf_op jit(solution)/shard_map/pallas_call | solution.py:156
  143.7 2.6 %convolution_convert_fusion = bf16[128,3200]{1,0:T(8,128)(2,1)S(1)} fusion(bf16[128,512]{1,0:T(8,128)(2,1)S(1)} %shard_map.49, bf16[512,3200]{1,0:T(8,128)(2,1)} %bitcast.39), kind=kOutput, calls=%fused_computation | convolution fusion | flops 419840000 | bytes 4227072 | tf_op jit(solution)/shard_map/dot_general | solution.py:268
  146.3 14.4 %all_to_all.37 = bf16[4,32,3200]{2,1,0:T(8,128)(2,1)S(1)} all-to-all(bf16[4,32,3200]{2,1,0:T(8,128)(2,1)S(1)} %bitcast.141), channel_id=1, replica_groups=mesh['row'=8,'cx'=4,'cz'=8] {'cx'}, dimensions={0} | all-to-all | bytes 1638400 | tf_op jit(solution)/shard_map/all_to_all | solution.py:269
  160.8 1.3 convert_subtract_fusion
  (35 shorter events, 0.6 us)
Async XLA Ops:
  1.5 18.7 %copy-start = (f32[2,8,4,128]{3,2,1,0:T(4,128)S(1)}, f32[2,8,4,128]{3,2,1,0:T(4,128)}, u32[]{:S(2)}) copy-start(f32[2,8,4,128]{3,2,1,0:T(4,128)} %param.5) | copy-start | bytes 98308
  1.5 18.7 %copy-start.1 = (f32[32,12544]{1,0:T(8,128)S(1)}, f32[32,12544]{1,0:T(8,128)}, u32[]{:S(2)}) copy-start(f32[32,12544]{1,0:T(8,128)} %eigen.3) | copy-start | bytes 4816900
  2.3 13.3 %all-to-all-start = ((f32[8,72,128]{2,1,0:T(8,128)}), f32[8,72,128]{2,1,0:T(8,128)S(1)}, u32[]{:S(2)}, u32[]{:S(2)}) async-start(f32[8,72,128]{2,1,0:T(8,128)} %broadcast_in_dim.59), calls=%async_computation | async-start | bytes 589824 | tf_op jit(solution)/shard_map/all_to_all | solution.py:150
  15.6 10.7 %all-to-all-start.2 = ((bf16[4,2,8,3200]{3,2,1,0:T(8,128)(2,1)}), bf16[4,2,8,3200]{3,2,1,0:T(8,128)(2,1)S(1)}, u32[]{:S(2)}, u32[]{:S(2)}) async-start(bf16[4,2,8,3200]{3,2,1,0:T(8,128)(2,1)} %copy.102), calls=%async_computation.2 | async-start | bytes 819200 | tf_op jit(solution)/shard_map/all_to_all | solution.py:181
  25.4 1.0 copy-start.2
  27.0 14.4 %all-to-all-start.1 = ((f32[8,32,128]{2,1,0:T(8,128)}), f32[8,32,128]{2,1,0:T(8,128)S(1)}, u32[]{:S(2)}, u32[]{:S(2)}) async-start(f32[8,32,128]{2,1,0:T(8,128)} %broadcast_in_dim.64), calls=%async_computation.1 | async-start | bytes 262144 | tf_op jit(solution)/shard_map/all_to_all | solution.py:150
  32.9 13.7 %copy-start.3 = (f32[512,512]{1,0:T(8,128)S(1)}, f32[512,512]{1,0:T(8,128)}, u32[]{:S(2)}) copy-start(f32[512,512]{1,0:T(8,128)} %copy-done.2) | copy-start | bytes 3145732
  32.9 23.7 %collective-permute-start = (bf16[4,2,8,3200]{3,2,0,1:T(8,128)(2,1)}, bf16[4,2,8,3200]{3,2,0,1:T(8,128)(2,1)}, u32[]{:S(2)}, u32[]{:S(2)}) collective-permute-start(bf16[4,2,8,3200]{3,2,0,1:T(8,128)(2,1)} %copy.103), channel_id=1, source_target_pairs={{0,1},{1,2},{2,3},{3,4},{4,5},{5,6},{6,7},{7,0},{8,9},{9,10},{10,1... | collective-permute-start | bytes 1228808 | tf_op jit(solution)/shard_map/ppermute | solution.py:187
  34.6 22.1 %collective-permute-start.4 = (bf16[4,2,8,3200]{3,2,0,1:T(8,128)(2,1)}, bf16[4,2,8,3200]{3,2,0,1:T(8,128)(2,1)}, u32[]{:S(2)}, u32[]{:S(2)}) collective-permute-start(bf16[4,2,8,3200]{3,2,0,1:T(8,128)(2,1)} %copy.103), channel_id=1, source_target_pairs={{0,7},{1,0},{2,1},{3,2},{4,3},{5,4},{6,5},{7,6},{8,15},{9,8},{10,9... | collective-permute-start | bytes 1228808 | tf_op jit(solution)/shard_map/ppermute | solution.py:190
  52.7 45.4 %all-to-all-start.3 = ((bf16[4,32,3200]{2,1,0:T(8,128)(2,1)}), bf16[4,32,3200]{2,1,0:T(8,128)(2,1)S(1)}, u32[]{:S(2)}, u32[]{:S(2)}) async-start(bf16[4,32,3200]{2,1,0:T(8,128)(2,1)} %bitcast.132), calls=%async_computation.3 | async-start | bytes 1638400 | tf_op jit(solution)/shard_map/all_to_all | solution.py:241
  56.6 11.8 %collective-permute-start.1 = (bf16[4,2,8,3200]{3,2,0,1:T(8,128)(2,1)}, bf16[4,2,8,3200]{3,2,0,1:T(8,128)(2,1)S(1)}, u32[]{:S(2)}, u32[]{:S(2)}) collective-permute-start(bf16[4,2,8,3200]{3,2,0,1:T(8,128)(2,1)} %collective-permute-done), channel_id=1, source_target_pairs={{0,1},{1,2},{2,3},{3,4},{4,5},{5,6},{6,7},{7,0},{8,9},{9,10},{10,1... | collective-permute-start | bytes 1228808 | tf_op jit(solution)/shard_map/ppermute | solution.py:187
  56.7 11.8 %collective-permute-start.5 = (bf16[4,2,8,3200]{3,2,0,1:T(8,128)(2,1)}, bf16[4,2,8,3200]{3,2,0,1:T(8,128)(2,1)S(1)}, u32[]{:S(2)}, u32[]{:S(2)}) collective-permute-start(bf16[4,2,8,3200]{3,2,0,1:T(8,128)(2,1)} %collective-permute-done.4), channel_id=1, source_target_pairs={{0,7},{1,0},{2,1},{3,2},{4,3},{5,4},{6,5},{7,6},{8,15},{9,8},{10,9... | collective-permute-start | bytes 1228808 | tf_op jit(solution)/shard_map/ppermute | solution.py:190
  68.4 10.7 %collective-permute-start.2 = (bf16[4,2,8,3200]{3,2,0,1:T(8,128)(2,1)S(1)}, bf16[4,2,8,3200]{3,2,0,1:T(8,128)(2,1)S(1)}, u32[]{:S(2)}, u32[]{:S(2)}) collective-permute-start(bf16[4,2,8,3200]{3,2,0,1:T(8,128)(2,1)S(1)} %collective-permute-done.1), channel_id=1, source_target_pairs={{0,1},{1,2},{2,3},{3,4},{4,5},{5,6},{6,7},{7,0},{8,9},{9,10},{10,1... | collective-permute-start | bytes 1228808 | tf_op jit(solution)/shard_map/ppermute | solution.py:187
  68.4 21.4 %collective-permute-start.6 = (bf16[4,2,8,3200]{3,2,0,1:T(8,128)(2,1)S(1)}, bf16[4,2,8,3200]{3,2,0,1:T(8,128)(2,1)S(1)}, u32[]{:S(2)}, u32[]{:S(2)}) collective-permute-start(bf16[4,2,8,3200]{3,2,0,1:T(8,128)(2,1)S(1)} %collective-permute-done.5), channel_id=1, source_target_pairs={{0,7},{1,0},{2,1},{3,2},{4,3},{5,4},{6,5},{7,6},{8,15},{9,8},{10,9... | collective-permute-start | bytes 1228808 | tf_op jit(solution)/shard_map/ppermute | solution.py:190
  79.1 9.9 %collective-permute-start.3 = (bf16[4,2,8,3200]{3,2,0,1:T(8,128)(2,1)S(1)}, bf16[4,2,8,3200]{3,2,0,1:T(8,128)(2,1)S(1)}, u32[]{:S(2)}, u32[]{:S(2)}) collective-permute-start(bf16[4,2,8,3200]{3,2,0,1:T(8,128)(2,1)S(1)} %collective-permute-done.2), channel_id=1, source_target_pairs={{0,1},{1,2},{2,3},{3,4},{4,5},{5,6},{6,7},{7,0},{8,9},{9,10},{10,1... | collective-permute-start | bytes 1228808 | tf_op jit(solution)/shard_map/ppermute | solution.py:187

commit v2 on v1

--- a/solution.py
+++ b/solution.py
@@ -141,8 +141,225 @@
     rounded[:, cols:] = jnp.zeros((rows, rounded.shape[1] - cols), BF16)
 
 
-def panel_coeffs(unit, gram, right, coeffs):
-    coeffs[...] = solve_wy(gram[...].astype(F32), right[...].astype(F32), unit).astype(BF16)
+GRAM_TILES = ((0, 0), (0, 2), (0, 3), (1, 0), (1, 1), (1, 2), (1, 3), (2, 2), (3, 2), (3, 3))
+
+
+def tile_inverses(tiles):
+    bp = lax.broadcasted_iota(jnp.int32, (BLOCK, BLOCK), 0)
+    bq = lax.broadcasted_iota(jnp.int32, (BLOCK, BLOCK), 1)
+    eye = (bp == bq).astype(F32)
+    inverse = [eye - jnp.where(bp // 2 == bq // 2, tile, 0.0) for tile in tiles]
+    size = 2
+    while size < BLOCK:
+        joined = (bp // (2 * size) == bq // (2 * size)) & (bp // size != bq // size)
+        left = [dot3(inv, jnp.where(joined, tile, 0.0)) for inv, tile in zip(inverse, tiles)]
+        inverse = [inv - dot3(lhs, inv) for inv, lhs in zip(inverse, left)]
+        size *= 2
+    return inverse
+
+
+def panel_kernel(traded, reflect, home, acc_top, acc_low, work, slots, whole, change, send_rs, recv_rs, send_ag,
+                 recv_ag, send_x, recv_x, own_x):
+    row, cx = lax.axis_index("row"), lax.axis_index("cx")
+    n_row = lax.axis_size("row")
+    peers = n_row * NX
+    me = row * NX + cx
+    owners = work.shape[0]
+    rows = traded.shape[0]
+    part = reflect.shape[1]
+
+    def device(place):
+        return {"row": place // NX, "cx": place % NX}
+
+    barrier = pltpu.get_barrier_semaphore()
+    for k in range(1, peers):
+        pl.semaphore_signal(
+            barrier, inc=1, device_id=device((me + k) % peers), device_id_type=pl.DeviceIdType.MESH
+        )
+
+    acc_top[...] = jnp.zeros_like(acc_top)
+    acc_low[...] = jnp.zeros_like(acc_low)
+    chunk = 5 * LANE
+
+    def product(step, carry):
+        at = pl.ds(pl.multiple_of(step * chunk, LANE), chunk)
+        low = reflect[2 * BLOCK :, at]
+        both = reflect[:, at]
+        top = jnp.concatenate([traded[:, at], reflect[: 2 * BLOCK, at]], axis=0)
+        acc_top[...] += lax.dot_general(top, both, NT, preferred_element_type=F32)
+        acc_low[...] += lax.dot_general(low, low, NT, preferred_element_type=F32)
+        return carry
+
+    lax.fori_loop(0, part // chunk, product, 0)
+    half = BLOCK // 2
+
+    def put(place, value):
+        rounded = value.astype(BF16)
+        work[2 * place] = rounded[:half]
+        work[2 * place + 1] = rounded[half:]
+
+    for place, (u, t) in enumerate(GRAM_TILES):
+        if u < 2:
+            put(place, acc_top[(1 + u) * BLOCK : (2 + u) * BLOCK, t * BLOCK : (t + 1) * BLOCK])
+        else:
+            put(place, acc_low[(u - 2) * BLOCK : (u - 1) * BLOCK, (t - 2) * BLOCK : (t - 1) * BLOCK])
+    for t in range(4):
+        put(len(GRAM_TILES) + t, acc_top[:rows, t * BLOCK : (t + 1) * BLOCK])
+
+    pl.semaphore_wait(barrier, peers - 1)
+
+    def scatter(k):
+        target = (me + k) % peers
+        return target, pltpu.make_async_remote_copy(
+            src_ref=work.at[lax.rem(target, owners)],
+            dst_ref=slots.at[k - 1],
+            send_sem=send_rs.at[k - 1],
+            recv_sem=recv_rs.at[k - 1],
+            device_id=device(target),
+            device_id_type=pl.DeviceIdType.MESH,
+        )
+
+    def gather(k):
+        return pltpu.make_async_remote_copy(
+            src_ref=whole.at[lax.rem(me, owners)],
+            dst_ref=whole.at[lax.rem(me, owners)],
+            send_sem=send_ag.at[k - 1],
+            recv_sem=recv_ag.at[k - 1],
+            device_id=device((me + k) % peers),
+            device_id_type=pl.DeviceIdType.MESH,
+        )
+
+    def arrival(k):
+        source = lax.rem((me + peers - k) % peers, owners)
+        return pltpu.make_async_remote_copy(
+            src_ref=whole.at[source],
+            dst_ref=whole.at[source],
+            send_sem=send_ag.at[k - 1],
+            recv_sem=recv_ag.at[k - 1],
+            device_id=device((me + k) % peers),
+            device_id_type=pl.DeviceIdType.MESH,
+        )
+
+    for k in range(1, peers):
+        target, copy = scatter(k)
+        pl.when(target < owners)(copy.start)
+
+    @pl.when(me < owners)
+    def _():
+        total = work[lax.rem(me, owners)].astype(F32)
+        for k in range(1, peers):
+            scatter(k)[1].wait_recv()
+            total = total + slots[k - 1].astype(F32)
+        whole[lax.rem(me, owners)] = total.astype(BF16)
+        for k in range(1, peers):
+            gather(k).start()
+
+    for k in range(1, peers):
+        source = (me + peers - k) % peers
+        pl.when(source < owners)(arrival(k).wait_recv)
+
+    for k in range(1, peers):
+        target, copy = scatter(k)
+        pl.when(target < owners)(copy.wait_send)
+
+    @pl.when(me < owners)
+    def _():
+        for k in range(1, peers):
+            gather(k).wait_send()
+
+    def got(place):
+        return jnp.concatenate([whole[2 * place].astype(F32), whole[2 * place + 1].astype(F32)], axis=0)
+
+    gram = {key: got(place) for place, key in enumerate(GRAM_TILES)}
+    bp = lax.broadcasted_iota(jnp.int32, (BLOCK, BLOCK), 0)
+    bq = lax.broadcasted_iota(jnp.int32, (BLOCK, BLOCK), 1)
+    picked = [jnp.where(bp == bq, gram[t, t], 0.0) for t in range(4)]
+    down = [2.0 / jnp.sum(p, axis=1, keepdims=True) for p in picked]
+    across = [2.0 / jnp.sum(p, axis=0, keepdims=True) for p in picked]
+    strict = {(u, t): gram[u, t] * down[u] for u, t in GRAM_TILES}
+    for t in range(4):
+        strict[t, t] = jnp.where(bp > bq, strict[t, t], 0.0)
+    inverse = tile_inverses([strict[t, t] for t in range(4)])
+    found = {}
+    for t in (1, 0, 3, 2):
+        value = got(len(GRAM_TILES) + t)
+        for u in tuple(found):
+            value = value - dot3(found[u], strict[u, t])
+        found[t] = dot3(value, inverse[t])
+    coeffs = jnp.concatenate([(found[t] * across[t]).astype(BF16) for t in range(4)], axis=1)
+
+    def update(step, carry):
+        at = pl.ds(pl.multiple_of(step * chunk, LANE), chunk)
+        value = jnp.dot(coeffs, reflect[:, at], preferred_element_type=F32).astype(BF16)
+        for k in range(NX):
+            change[k, :, at] = value[k * (rows // NX) : (k + 1) * (rows // NX)]
+        return carry
+
+    lax.fori_loop(0, part // chunk, update, 0)
+
+    def back(k):
+        target = (cx + k) % NX
+        return pltpu.make_async_remote_copy(
+            src_ref=change.at[target],
+            dst_ref=home.at[cx],
+            send_sem=send_x.at[k - 1],
+            recv_sem=recv_x.at[k - 1],
+            device_id={"cx": target},
+            device_id_type=pl.DeviceIdType.MESH,
+        )
+
+    def back_arrival(k):
+        source = (cx + NX - k) % NX
+        return pltpu.make_async_remote_copy(
+            src_ref=change.at[source],
+            dst_ref=home.at[source],
+            send_sem=send_x.at[k - 1],
+            recv_sem=recv_x.at[k - 1],
+            device_id={"cx": source},
+            device_id_type=pl.DeviceIdType.MESH,
+        )
+
+    for k in range(1, NX):
+        back(k).start()
+    keep = pltpu.make_async_copy(change.at[cx], home.at[cx], own_x)
+    keep.start()
+    keep.wait()
+    for k in range(1, NX):
+        back(k).wait_send()
+        back_arrival(k).wait_recv()
+
+
+def panel_step(traded, reflect, n_row):
+    rows, part = traded.shape
+    peers = n_row * NX
+    owners = 2 * (len(GRAM_TILES) + 4)
+    half = BLOCK // 2
+    dma = pltpu.SemaphoreType.DMA
+    return pl.pallas_call(
+        panel_kernel,
+        out_shape=jax.ShapeDtypeStruct((NX, rows // NX, part), BF16),
+        in_specs=[pl.BlockSpec(memory_space=pltpu.VMEM)] * 2,
+        out_specs=pl.BlockSpec(memory_space=pltpu.VMEM),
+        scratch_shapes=[
+            pltpu.VMEM((rows + 2 * BLOCK, 4 * BLOCK), F32),
+            pltpu.VMEM((2 * BLOCK, 2 * BLOCK), F32),
+            pltpu.VMEM((owners, half, BLOCK), BF16),
+            pltpu.VMEM((peers - 1, half, BLOCK), BF16),
+            pltpu.VMEM((owners, half, BLOCK), BF16),
+            pltpu.VMEM((NX, rows // NX, part), BF16),
+            dma((peers - 1,)),
+            dma((peers - 1,)),
+            dma((peers - 1,)),
+            dma((peers - 1,)),
+            dma((NX - 1,)),
+            dma((NX - 1,)),
+            dma(()),
+        ],
+        compiler_params=pltpu.CompilerParams(
+            collective_id=0, has_side_effects=True, vmem_limit_bytes=40 * 1024 * 1024
+        ),
+        cost_estimate=pl.CostEstimate(flops=20_000_000_000, bytes_accessed=4_000_000, transcendentals=0),
+    )(traded, reflect)
 
 
 def sent_to_all(x, axis):
@@ -246,27 +463,7 @@
         piece = blocks[step].transpose(1, 0, 2, 3)[:, :, None]
         gathered = lax.dynamic_update_slice(gathered, piece, (0, 0, (at_z - step) % NZ, 0, 0))
     reflect = gathered.reshape(every, part)
-    gram_mat = lax.dot_general(reflect, reflect, NT, preferred_element_type=F32)
-    inner_mat = lax.dot_general(traded, reflect, NT, preferred_element_type=F32)
-    group = n_row * NX
-    piece_rows = every // group
-    sending = jnp.concatenate(
-        [
-            gram_mat.astype(BF16).reshape(group, piece_rows, every),
-            inner_mat.astype(BF16).reshape(group, piece_rows, -1),
-        ],
-        axis=2,
-    )
-    arrived = lax.all_to_all(sending, ("row", "cx"), 0, 0, tiled=True)
-    added = jnp.sum(arrived.astype(F32), axis=0).astype(BF16)
-    whole = sent_to_all(added, ("row", "cx"))
-    gram_sum = whole[:, :, :every].reshape(every, every)
-    inner_sum = whole[:, :, every:].reshape(NX * rows, every)
-    (coeffs_mat,) = call(
-        functools.partial(panel_coeffs, width), [((NX * rows, every), BF16)], 0, gram_sum, inner_sum
-    )
-    update = lax.dot_general(coeffs_mat, reflect, NN, preferred_element_type=F32).astype(BF16)
-    home = lax.all_to_all(update.reshape(NX, rows, part), "cx", 0, 0, tiled=True)
+    home = panel_step(traded, reflect, n_row)
     home = home.transpose(1, 0, 2).reshape(rows, full)[:, :cols]
     return eigen - home.astype(F32)
 

time: 163 us -> 140 us (0.86)
  blocking collectives: 53.1 us -> 0 us
  Pallas kernels: 13.1 us -> 51.4 us
  matrix products: 10.5 us -> 0 us
  waiting for transfers between devices: 27.5 us -> 30.2 us
  local copies, waits for them, and re-layouts: 23.5 us -> 21.1 us
  starting transfers between devices: 30 us -> 31.8 us
    all_to_all x3 -> x0, blocking collectives: 53.1 us -> none  [the longest x1 21.8 us: local(): arrived = lax.all_to_all(sending, ('row', 'cx'), 0, 0, tiled=True)]
    pallas_call x0 -> x1, Pallas kernels: none -> 41.6 us  [panel_step(): pl.pallas_call(panel_kernel, out_shape=jax.ShapeDtypeStruct((NX, rows //...]
    dot_general x3 -> x0, matrix products: 10.5 us -> none  [the longest x1 4.87 us: local(): gram_mat = lax.dot_general(reflect, reflect, NT, preferred_element_type=F32)]
    dynamic_update_slice x8, local copies, waits for them, and re-layouts: 8.49 us -> 3.31 us  [local(): lax.dynamic_update_slice(gathered, piece, (0, 0, (at_z - step) % NZ, 0, 0))]
    unnamed x8 -> x14, local copies, waits for them, and re-layouts: 0.99 us -> 4.77 us
    pallas_call x4 -> x3, Pallas kernels: 13.1 us -> 9.78 us  [call(): pl.pallas_call(kernel, out_shape=[jax.ShapeDtypeStruct(s, d) for s, d in...]
    ppermute x4, waiting for transfers between devices: 23.6 us -> 26.3 us  [local(): forward = lax.ppermute(forward, 'cz', up)]
    broadcast_in_dim x1, local copies, waits for them, and re-layouts: 2.07 us -> 0.38 us  [local(): gathered = jnp.zeros((n_panel, NX, NZ, refl_dev, part), BF16)]
  transfers between devices with their start and end apart: 11 -> 11, of which waited for: 4 -> 4; matrix products, arithmetic and copies ran while one was open for 16% -> 12% of each run, Pallas kernels for 6% -> 7%
where the time goes in v2:
time: 140 us; the launch traced here: 139 us
  Pallas kernels  51.4 us (37%)
  starting transfers between devices  31.8 us (23%)
  waiting for transfers between devices  30.2 us (22%)
  local copies, waits for them, and re-layouts  21.1 us (15%)
  other arithmetic  3.98 us (3%)
    pallas_call x1, Pallas kernels, panel_step(): pl.pallas_call(panel_kernel, out_shape=jax.ShapeDtypeStruct((NX, rows //...  41.6 us
    ppermute x4, waiting for transfers between devices, local(): forward = lax.ppermute(forward, 'cz', up)  26.3 us
    all_to_all x2, starting transfers between devices, sent_to_all(): lax.all_to_all(jnp.broadcast_to(x[None], (peers, *x.shape)), axis, 0, 0,...  11.8 us
    ppermute x3, starting transfers between devices, local(): backward = lax.ppermute(backward, 'cz', down)  10.5 us
    pallas_call x3, Pallas kernels, call(): pl.pallas_call(kernel, out_shape=[jax.ShapeDtypeStruct(s, d) for s, d in...  9.78 us
    unnamed x14, local copies, waits for them, and re-layouts  4.77 us
    all_to_all x1, starting transfers between devices, local(): lax.all_to_all(rounded.reshape(rows, NX, part).transpose(1, 0, 2), 'cx',...  4.2 us
    all_to_all x1, starting transfers between devices, local(): block = lax.all_to_all(cut, 'cx', 0, 0, tiled=True)  4.13 us
  transfers between devices with their start and end apart: 11, of which 4 were waited for; matrix products, arithmetic and copies ran while one was open for 12% of the time, Pallas kernels for 7%

profile of v2, /device:TPU:1, one launch (start us, length us, event | category | flops | bytes accessed | tf_op | source)
XLA Modules:
  0.0 138.8 jit_solution(15658672571946186694)
XLA Ops:
  0.0 0.7 convert_element_type.34
  0.7 0.1 convert_element_type.35
  0.8 0.8 select_maximum_fusion
  1.5 0.7 broadcast_in_dim.53
  2.3 6.5 %all-to-all-start = ((f32[8,72,128]{2,1,0:T(8,128)}), f32[8,72,128]{2,1,0:T(8,128)S(1)}, u32[]{:S(2)}, u32[]{:S(2)}) async-start(f32[8,72,128]{2,1,0:T(8,128)} %broadcast_in_dim.53), calls=%async_computation | async-start | bytes 589824 | tf_op jit(solution)/shard_map/all_to_all | solution.py:367
  8.8 0.8 reshape.111
  9.6 1.0 pad.14
  10.6 0.1 reshape.125
  10.7 0.8 copy.110
  11.5 0.1 broadcast_in_dim.56
  11.6 0.1 broadcast_in_dim_reshape.18.own_shift
  11.7 3.9 %all-to-all-done = f32[8,72,128]{2,1,0:T(8,128)S(1)} async-done(((f32[8,72,128]{2,1,0:T(8,128)}), f32[8,72,128]{2,1,0:T(8,128)S(1)}, u32[]{:S(2)}, u32[]{:S(2)}) %all-to-all-start) | async-done | bytes 294944 | tf_op jit(solution)/shard_map/all_to_all | solution.py:367
  15.6 4.1 %all-to-all-start.3 = ((bf16[4,2,8,3200]{3,2,1,0:T(8,128)(2,1)}), bf16[4,2,8,3200]{3,2,1,0:T(8,128)(2,1)}, u32[]{:S(2)}, u32[]{:S(2)}) async-start(bf16[4,2,8,3200]{3,2,1,0:T(8,128)(2,1)} %copy.110), calls=%async_computation.3 | async-start | bytes 819200 | tf_op jit(solution)/shard_map/all_to_all | solution.py:398
  19.8 0.1 copy.97
  19.8 0.1 copy.95
  19.9 0.1 dynamic-slice_bitcast_fusion.prev_shift
  20.1 0.1 copy.98
  20.1 0.3 broadcast_in_dim_reshape.17.tile_down
  20.4 0.1 broadcast_in_dim_reshape.14.tile_across
  20.5 0.1 copy.96
  20.5 0.3 broadcast_in_dim_reshape.16.shift
  20.8 0.1 convert_bitcast_fusion.prev_over
  20.9 5.0 %shard_map.46 = (f32[512,512]{1,0:T(8,128)S(1)}, f32[64,256]{1,0:T(8,128)S(1)}, f32[64,128]{1,0:T(8,128)S(1)}, f32[32,128]{1,0:T(8,128)S(1)}) custom-call(s32[16]{0:T(128)S(1)} %get-tuple-element.22.own_tile, f32[512,128]{1,0:T(8,128)S(1)} %bitcast.126, s32[512,1]{1,0:T(8,128)S(1)} %broadcast_in_dim_reshape.16.shift, ...), custom_call_target="tpu_custom_call" | custom-call | flops 2000000000 | bytes 4000000 | tf_op jit(solution)/shard_map/pallas_call | solution.py:373
  26.0 1.0 copy-done.5
  27.0 0.0 all-to-all-done.3
  27.0 0.7 broadcast_in_dim.58
  27.6 5.3 %all-to-all-start.1 = ((f32[8,32,128]{2,1,0:T(8,128)}), f32[8,32,128]{2,1,0:T(8,128)S(1)}, u32[]{:S(2)}, u32[]{:S(2)}) async-start(f32[8,32,128]{2,1,0:T(8,128)} %broadcast_in_dim.58), calls=%async_computation.1 | async-start | bytes 262144 | tf_op jit(solution)/shard_map/all_to_all | solution.py:367
  32.9 1.0 collective-permute-start
  34.0 3.9 %collective-permute-start.4 = (bf16[4,2,8,3200]{3,2,1,0:T(8,128)(2,1)}, bf16[4,2,8,3200]{3,2,1,0:T(8,128)(2,1)}, u32[]{:S(2)}, u32[]{:S(2)}) collective-permute-start(bf16[4,2,8,3200]{3,2,1,0:T(8,128)(2,1)} %all-to-all-done.3), channel_id=1, source_target_pairs={{0,7},{1,0},{2,1},{3,2},{4,3},{5,4},{6,5},{7,6},{8,15},{9,8},{10,9... | collective-permute-start | bytes 1228808 | tf_op jit(solution)/shard_map/ppermute | solution.py:407
  37.9 0.4 broadcast_in_dim.59
  38.3 1.0 copy_dynamic-update-slice_fusion.7
  39.4 1.2 reshape.118
  40.6 1.0 slice_bitcast_fusion.1
  41.6 1.1 fusion.1
  42.7 0.9 copy.106
  43.5 1.1 reshape.119.right
  44.6 1.2 copy-done.6
  45.8 3.4 %shard_map.47 = f32[32,512]{1,0:T(8,128)S(1)} custom-call(f32[512,512]{1,0:T(8,128)S(1)} %copy-done.6, f32[32,512]{1,0:T(8,128)S(1)} %reshape.119.right), custom_call_target="tpu_custom_call" | custom-call | flops 2000000000 | bytes 4000000 | tf_op jit(solution)/shard_map/pallas_call | solution.py:373
  49.2 0.8 reshape.120
  50.0 1.1 constant_dynamic-slice_fusion
  51.1 0.1 reshape.121.own_coeffs
  51.2 0.1 reshape.122.prev_coeffs
  51.3 1.4 %copy-done.4 = f32[32,12544]{1,0:T(8,128)S(1)} copy-done((f32[32,12544]{1,0:T(8,128)S(1)}, f32[32,12544]{1,0:T(8,128)}, u32[]{:S(2)}) %copy-start.4) | copy-done | bytes 1605656
  52.7 1.4 shard_map.48
  54.1 0.0 copy-start
  54.1 1.1 copy-done
  55.2 1.0 copy.135
  56.3 4.2 %all-to-all-start.2 = ((bf16[4,32,3200]{2,1,0:T(8,128)(2,1)}), bf16[4,32,3200]{2,1,0:T(8,128)(2,1)}, u32[]{:S(2)}, u32[]{:S(2)}) async-start(bf16[4,32,3200]{2,1,0:T(8,128)(2,1)} %bitcast.129), calls=%async_computation.2 | async-start | bytes 1638400 | tf_op jit(solution)/shard_map/all_to_all | solution.py:458
  60.5 0.1 collective-permute-start.1
  60.6 3.9 %collective-permute-start.5 = (bf16[4,2,8,3200]{3,2,1,0:T(8,128)(2,1)}, bf16[4,2,8,3200]{3,2,1,0:T(8,128)(2,1)S(1)}, u32[]{:S(2)}, u32[]{:S(2)}) collective-permute-start(bf16[4,2,8,3200]{3,2,1,0:T(8,128)(2,1)} %collective-permute-done.4), channel_id=1, source_target_pairs={{0,7},{1,0},{2,1},{3,2},{4,3},{5,4},{6,5},{7,6},{8,15},{9,8},{10,9... | collective-permute-start | bytes 1228808 | tf_op jit(solution)/shard_map/ppermute | solution.py:407
  64.5 1.0 copy_dynamic-update-slice_fusion.6
  65.5 8.1 %collective-permute-done.1 = bf16[4,2,8,3200]{3,2,1,0:T(8,128)(2,1)S(1)} collective-permute-done((bf16[4,2,8,3200]{3,2,1,0:T(8,128)(2,1)}, bf16[4,2,8,3200]{3,2,1,0:T(8,128)(2,1)S(1)}, u32[]{:S(2)}, u32[]{:S(2)}) %collective-permute-start.1) | collective-permute-done | bytes 409632 | tf_op jit(solution)/shard_map/ppermute | solution.py:404
  73.6 0.0 collective-permute-start.2
  73.6 0.0 collective-permute-done.5
  73.6 2.7 %collective-permute-start.6 = (bf16[4,2,8,3200]{3,2,1,0:T(8,128)(2,1)S(1)}, bf16[4,2,8,3200]{3,2,1,0:T(8,128)(2,1)S(1)}, u32[]{:S(2)}, u32[]{:S(2)}) collective-permute-start(bf16[4,2,8,3200]{3,2,1,0:T(8,128)(2,1)S(1)} %collective-permute-done.5), channel_id=1, source_target_pairs={{0,7},{1,0},{2,1},{3,2},{4,3},{5,4},{6,5},{7,6},{8,15},{9,8},{10,9... | collective-permute-start | bytes 1228808 | tf_op jit(solution)/shard_map/ppermute | solution.py:407
  76.4 8.2 %collective-permute-done.2 = bf16[4,2,8,3200]{3,2,1,0:T(8,128)(2,1)S(1)} collective-permute-done((bf16[4,2,8,3200]{3,2,1,0:T(8,128)(2,1)S(1)}, bf16[4,2,8,3200]{3,2,1,0:T(8,128)(2,1)S(1)}, u32[]{:S(2)}, u32[]{:S(2)}) %collective-permute-start.2) | collective-permute-done | bytes 409632 | tf_op jit(solution)/shard_map/ppermute | solution.py:404
  84.5 0.0 collective-permute-start.3
  84.6 10.0 %collective-permute-done.3 = bf16[4,2,8,3200]{3,2,1,0:T(8,128)(2,1)S(1)} collective-permute-done((bf16[4,2,8,3200]{3,2,1,0:T(8,128)(2,1)S(1)}, bf16[4,2,8,3200]{3,2,1,0:T(8,128)(2,1)S(1)}, u32[]{:S(2)}, u32[]{:S(2)}) %collective-permute-start.3) | collective-permute-done | bytes 409632 | tf_op jit(solution)/shard_map/ppermute | solution.py:404
  94.6 0.0 collective-permute-done.6
  94.7 1.0 copy_dynamic-update-slice_fusion
  95.8 0.0 copy-start.1
  95.8 41.6 %shard_map.49 = bf16[4,32,3200]{2,1,0:T(8,128)(2,1)S(1)} custom-call(bf16[128,3200]{1,0:T(8,128)(2,1)} %bitcast.18.traded, bf16[512,3200]{1,0:T(8,128)(2,1)S(1)} %bitcast.123), custom_call_target="tpu_custom_call" | custom-call | flops 20000000000 | bytes 4000000 | tf_op jit(solution)/shard_map/pallas_call | solution.py:338
  137.4 0.1 copy.125
  137.4 1.3 convert_subtract_fusion
  (27 shorter events, 0.3 us)
Async XLA Ops:
  1.5 19.4 %copy-start.2 = (f32[2,8,4,128]{3,2,1,0:T(4,128)S(1)}, f32[2,8,4,128]{3,2,1,0:T(4,128)}, u32[]{:S(2)}) copy-start(f32[2,8,4,128]{3,2,1,0:T(4,128)} %param.5) | copy-start | bytes 98308
  1.5 19.4 %copy-start.3 = (f32[32,12544]{1,0:T(8,128)S(1)}, f32[32,12544]{1,0:T(8,128)}, u32[]{:S(2)}) copy-start(f32[32,12544]{1,0:T(8,128)} %eigen.3) | copy-start | bytes 4816900
  2.3 13.3 %all-to-all-start = ((f32[8,72,128]{2,1,0:T(8,128)}), f32[8,72,128]{2,1,0:T(8,128)S(1)}, u32[]{:S(2)}, u32[]{:S(2)}) async-start(f32[8,72,128]{2,1,0:T(8,128)} %broadcast_in_dim.53), calls=%async_computation | async-start | bytes 589824 | tf_op jit(solution)/shard_map/all_to_all | solution.py:367
  15.6 11.4 %all-to-all-start.3 = ((bf16[4,2,8,3200]{3,2,1,0:T(8,128)(2,1)}), bf16[4,2,8,3200]{3,2,1,0:T(8,128)(2,1)}, u32[]{:S(2)}, u32[]{:S(2)}) async-start(bf16[4,2,8,3200]{3,2,1,0:T(8,128)(2,1)} %copy.110), calls=%async_computation.3 | async-start | bytes 819200 | tf_op jit(solution)/shard_map/all_to_all | solution.py:398
  26.0 1.0 copy-start.5
  27.6 11.7 %all-to-all-start.1 = ((f32[8,32,128]{2,1,0:T(8,128)}), f32[8,32,128]{2,1,0:T(8,128)S(1)}, u32[]{:S(2)}, u32[]{:S(2)}) async-start(f32[8,32,128]{2,1,0:T(8,128)} %broadcast_in_dim.58), calls=%async_computation.1 | async-start | bytes 262144 | tf_op jit(solution)/shard_map/all_to_all | solution.py:367
  32.9 27.5 %collective-permute-start = (bf16[4,2,8,3200]{3,2,1,0:T(8,128)(2,1)}, bf16[4,2,8,3200]{3,2,1,0:T(8,128)(2,1)}, u32[]{:S(2)}, u32[]{:S(2)}) collective-permute-start(bf16[4,2,8,3200]{3,2,1,0:T(8,128)(2,1)} %all-to-all-done.3), channel_id=1, source_target_pairs={{0,1},{1,2},{2,3},{3,4},{4,5},{5,6},{6,7},{7,0},{8,9},{9,10},{10,1... | collective-permute-start | bytes 1228808 | tf_op jit(solution)/shard_map/ppermute | solution.py:404
  34.0 26.6 %collective-permute-start.4 = (bf16[4,2,8,3200]{3,2,1,0:T(8,128)(2,1)}, bf16[4,2,8,3200]{3,2,1,0:T(8,128)(2,1)}, u32[]{:S(2)}, u32[]{:S(2)}) collective-permute-start(bf16[4,2,8,3200]{3,2,1,0:T(8,128)(2,1)} %all-to-all-done.3), channel_id=1, source_target_pairs={{0,7},{1,0},{2,1},{3,2},{4,3},{5,4},{6,5},{7,6},{8,15},{9,8},{10,9... | collective-permute-start | bytes 1228808 | tf_op jit(solution)/shard_map/ppermute | solution.py:407
  44.6 1.2 copy-start.6
  51.3 1.4 %copy-start.4 = (f32[32,12544]{1,0:T(8,128)S(1)}, f32[32,12544]{1,0:T(8,128)}, u32[]{:S(2)}) copy-start(f32[32,12544]{1,0:T(8,128)} %eigen.3) | copy-start | bytes 4816900
  54.1 1.2 copy-start
  56.3 39.5 %all-to-all-start.2 = ((bf16[4,32,3200]{2,1,0:T(8,128)(2,1)}), bf16[4,32,3200]{2,1,0:T(8,128)(2,1)}, u32[]{:S(2)}, u32[]{:S(2)}) async-start(bf16[4,32,3200]{2,1,0:T(8,128)(2,1)} %bitcast.129), calls=%async_computation.2 | async-start | bytes 1638400 | tf_op jit(solution)/shard_map/all_to_all | solution.py:458
  60.5 13.2 %collective-permute-start.1 = (bf16[4,2,8,3200]{3,2,1,0:T(8,128)(2,1)}, bf16[4,2,8,3200]{3,2,1,0:T(8,128)(2,1)S(1)}, u32[]{:S(2)}, u32[]{:S(2)}) collective-permute-start(bf16[4,2,8,3200]{3,2,1,0:T(8,128)(2,1)} %collective-permute-done), channel_id=1, source_target_pairs={{0,1},{1,2},{2,3},{3,4},{4,5},{5,6},{6,7},{7,0},{8,9},{9,10},{10,1... | collective-permute-start | bytes 1228808 | tf_op jit(solution)/shard_map/ppermute | solution.py:404
  60.6 13.1 %collective-permute-start.5 = (bf16[4,2,8,3200]{3,2,1,0:T(8,128)(2,1)}, bf16[4,2,8,3200]{3,2,1,0:T(8,128)(2,1)S(1)}, u32[]{:S(2)}, u32[]{:S(2)}) collective-permute-start(bf16[4,2,8,3200]{3,2,1,0:T(8,128)(2,1)} %collective-permute-done.4), channel_id=1, source_target_pairs={{0,7},{1,0},{2,1},{3,2},{4,3},{5,4},{6,5},{7,6},{8,15},{9,8},{10,9... | collective-permute-start | bytes 1228808 | tf_op jit(solution)/shard_map/ppermute | solution.py:407
  73.6 10.9 %collective-permute-start.2 = (bf16[4,2,8,3200]{3,2,1,0:T(8,128)(2,1)S(1)}, bf16[4,2,8,3200]{3,2,1,0:T(8,128)(2,1)S(1)}, u32[]{:S(2)}, u32[]{:S(2)}) collective-permute-start(bf16[4,2,8,3200]{3,2,1,0:T(8,128)(2,1)S(1)} %collective-permute-done.1), channel_id=1, source_target_pairs={{0,1},{1,2},{2,3},{3,4},{4,5},{5,6},{6,7},{7,0},{8,9},{9,10},{10,1... | collective-permute-start | bytes 1228808 | tf_op jit(solution)/shard_map/ppermute | solution.py:404
  73.6 21.0 %collective-permute-start.6 = (bf16[4,2,8,3200]{3,2,1,0:T(8,128)(2,1)S(1)}, bf16[4,2,8,3200]{3,2,1,0:T(8,128)(2,1)S(1)}, u32[]{:S(2)}, u32[]{:S(2)}) collective-permute-start(bf16[4,2,8,3200]{3,2,1,0:T(8,128)(2,1)S(1)} %collective-permute-done.5), channel_id=1, source_target_pairs={{0,7},{1,0},{2,1},{3,2},{4,3},{5,4},{6,5},{7,6},{8,15},{9,8},{10,9... | collective-permute-start | bytes 1228808 | tf_op jit(solution)/shard_map/ppermute | solution.py:407
  84.5 10.0 %collective-permute-start.3 = (bf16[4,2,8,3200]{3,2,1,0:T(8,128)(2,1)S(1)}, bf16[4,2,8,3200]{3,2,1,0:T(8,128)(2,1)S(1)}, u32[]{:S(2)}, u32[]{:S(2)}) collective-permute-start(bf16[4,2,8,3200]{3,2,1,0:T(8,128)(2,1)S(1)} %collective-permute-done.2), channel_id=1, source_target_pairs={{0,1},{1,2},{2,3},{3,4},{4,5},{5,6},{6,7},{7,0},{8,9},{9,10},{10,1... | collective-permute-start | bytes 1228808 | tf_op jit(solution)/shard_map/ppermute | solution.py:404
  95.8 41.7 %copy-start.1 = (f32[32,12544]{1,0:T(8,128)S(1)}, f32[32,12544]{1,0:T(8,128)}, u32[]{:S(2)}) copy-start(f32[32,12544]{1,0:T(8,128)} %copy-done) | copy-start | bytes 4816900

commit v3 on v2

v3 whole, which is shorter than its diff:
```python
import functools

import jax
import jax.numpy as jnp
from jax import lax
from jax.experimental import pallas as pl
from jax.experimental.pallas import tpu as pltpu
from jax.sharding import Mesh
from jax.sharding import PartitionSpec as P

LANE = 128
BLOCK = 128
NX = 4
NZ = 8
F32 = jnp.float32
BF16 = jnp.bfloat16
NT = (((1,), (1,)), ((), ()))
NN = (((1,), (0,)), ((), ()))


def halves(a):
    top = a.astype(BF16)
    return top, (a - top.astype(F32)).astype(BF16)


def dot3(a, b):
    a_top, a_low = halves(a)
    b_top, b_low = halves(b)
    d = functools.partial(lax.dot_general, dimension_numbers=NN, preferred_element_type=F32)
    return d(a_top, b_top) + (d(a_top, b_low) + d(a_low, b_top))


GRAM_TILES = ((0, 0), (0, 2), (0, 3), (1, 0), (1, 1), (1, 2), (1, 3), (2, 2), (3, 2), (3, 3))


def tile_inverses(tiles):
    bp = lax.broadcasted_iota(jnp.int32, (BLOCK, BLOCK), 0)
    bq = lax.broadcasted_iota(jnp.int32, (BLOCK, BLOCK), 1)
    eye = (bp == bq).astype(F32)
    inverse = [eye - jnp.where(bp // 2 == bq // 2, tile, 0.0) for tile in tiles]
    size = 2
    while size < BLOCK:
        joined = (bp // (2 * size) == bq // (2 * size)) & (bp // size != bq // size)
        left = [dot3(inv, jnp.where(joined, tile, 0.0)) for inv, tile in zip(inverse, tiles)]
        inverse = [inv - dot3(lhs, inv) for inv, lhs in zip(inverse, left)]
        size *= 2
    return inverse


def panel_kernel(traded, reflect, home, acc_top, acc_low, work, slots, whole, change, send_rs, recv_rs, send_ag,
                 recv_ag, send_x, recv_x, own_x):
    row, cx = lax.axis_index("row"), lax.axis_index("cx")
    n_row = lax.axis_size("row")
    peers = n_row * NX
    me = row * NX + cx
    owners = work.shape[0]
    rows = traded.shape[0]
    part = reflect.shape[1]

    def device(place):
        return {"row": place // NX, "cx": place % NX}

    barrier = pltpu.get_barrier_semaphore()
    for k in range(1, peers):
        pl.semaphore_signal(
            barrier, inc=1, device_id=device((me + k) % peers), device_id_type=pl.DeviceIdType.MESH
        )

    acc_top[...] = jnp.zeros_like(acc_top)
    acc_low[...] = jnp.zeros_like(acc_low)
    chunk = 5 * LANE

    def product(step, carry):
        at = pl.ds(pl.multiple_of(step * chunk, LANE), chunk)
        low = reflect[2 * BLOCK :, at]
        both = reflect[:, at]
        top = jnp.concatenate([traded[:, at], reflect[: 2 * BLOCK, at]], axis=0)
        acc_top[...] += lax.dot_general(top, both, NT, preferred_element_type=F32)
        acc_low[...] += lax.dot_general(low, low, NT, preferred_element_type=F32)
        return carry

    lax.fori_loop(0, part // chunk, product, 0)
    half = BLOCK // 2

    def put(place, value):
        rounded = value.astype(BF16)
        work[2 * place] = rounded[:half]
        work[2 * place + 1] = rounded[half:]

    for place, (u, t) in enumerate(GRAM_TILES):
        if u < 2:
            put(place, acc_top[(1 + u) * BLOCK : (2 + u) * BLOCK, t * BLOCK : (t + 1) * BLOCK])
        else:
            put(place, acc_low[(u - 2) * BLOCK : (u - 1) * BLOCK, (t - 2) * BLOCK : (t - 1) * BLOCK])
    for t in range(4):
        put(len(GRAM_TILES) + t, acc_top[:rows, t * BLOCK : (t + 1) * BLOCK])

    pl.semaphore_wait(barrier, peers - 1)

    def scatter(k):
        target = (me + k) % peers
        return target, pltpu.make_async_remote_copy(
            src_ref=work.at[lax.rem(target, owners)],
            dst_ref=slots.at[k - 1],
            send_sem=send_rs.at[k - 1],
            recv_sem=recv_rs.at[k - 1],
            device_id=device(target),
            device_id_type=pl.DeviceIdType.MESH,
        )

    def gather(k):
        return pltpu.make_async_remote_copy(
            src_ref=whole.at[lax.rem(me, owners)],
            dst_ref=whole.at[lax.rem(me, owners)],
            send_sem=send_ag.at[k - 1],
            recv_sem=recv_ag.at[k - 1],
            device_id=device((me + k) % peers),
            device_id_type=pl.DeviceIdType.MESH,
        )

    def arrival(k):
        source = lax.rem((me + peers - k) % peers, owners)
        return pltpu.make_async_remote_copy(
            src_ref=whole.at[source],
            dst_ref=whole.at[source],
            send_sem=send_ag.at[k - 1],
            recv_sem=recv_ag.at[k - 1],
            device_id=device((me + k) % peers),
            device_id_type=pl.DeviceIdType.MESH,
        )

    for k in range(1, peers):
        target, copy = scatter(k)
        pl.when(target < owners)(copy.start)

    @pl.when(me < owners)
    def _():
        total = work[lax.rem(me, owners)].astype(F32)
        for k in range(1, peers):
            scatter(k)[1].wait_recv()
            total = total + slots[k - 1].astype(F32)
        whole[lax.rem(me, owners)] = total.astype(BF16)
        for k in range(1, peers):
            gather(k).start()

    for k in range(1, peers):
        source = (me + peers - k) % peers
        pl.when(source < owners)(arrival(k).wait_recv)

    for k in range(1, peers):
        target, copy = scatter(k)
        pl.when(target < owners)(copy.wait_send)

    @pl.when(me < owners)
    def _():
        for k in range(1, peers):
            gather(k).wait_send()

    def got(place):
        return jnp.concatenate([whole[2 * place].astype(F32), whole[2 * place + 1].astype(F32)], axis=0)

    gram = {key: got(place) for place, key in enumerate(GRAM_TILES)}
    bp = lax.broadcasted_iota(jnp.int32, (BLOCK, BLOCK), 0)
    bq = lax.broadcasted_iota(jnp.int32, (BLOCK, BLOCK), 1)
    picked = [jnp.where(bp == bq, gram[t, t], 0.0) for t in range(4)]
    down = [2.0 / jnp.sum(p, axis=1, keepdims=True) for p in picked]
    across = [2.0 / jnp.sum(p, axis=0, keepdims=True) for p in picked]
    strict = {(u, t): gram[u, t] * down[u] for u, t in GRAM_TILES}
    for t in range(4):
        strict[t, t] = jnp.where(bp > bq, strict[t, t], 0.0)
    inverse = tile_inverses([strict[t, t] for t in range(4)])
    found = {}
    for t in (1, 0, 3, 2):
        value = got(len(GRAM_TILES) + t)
        for u in tuple(found):
            value = value - dot3(found[u], strict[u, t])
        found[t] = dot3(value, inverse[t])
    coeffs = jnp.concatenate([(found[t] * across[t]).astype(BF16) for t in range(4)], axis=1)

    def update(step, carry):
        at = pl.ds(pl.multiple_of(step * chunk, LANE), chunk)
        value = jnp.dot(coeffs, reflect[:, at], preferred_element_type=F32).astype(BF16)
        for k in range(NX):
            change[k, :, at] = value[k * (rows // NX) : (k + 1) * (rows // NX)]
        return carry

    lax.fori_loop(0, part // chunk, update, 0)

    def back(k):
        target = (cx + k) % NX
        return pltpu.make_async_remote_copy(
            src_ref=change.at[target],
            dst_ref=home.at[cx],
            send_sem=send_x.at[k - 1],
            recv_sem=recv_x.at[k - 1],
            device_id={"cx": target},
            device_id_type=pl.DeviceIdType.MESH,
        )

    def back_arrival(k):
        source = (cx + NX - k) % NX
        return pltpu.make_async_remote_copy(
            src_ref=change.at[source],
            dst_ref=home.at[source],
            send_sem=send_x.at[k - 1],
            recv_sem=recv_x.at[k - 1],
            device_id={"cx": source},
            device_id_type=pl.DeviceIdType.MESH,
        )

    for k in range(1, NX):
        back(k).start()
    keep = pltpu.make_async_copy(change.at[cx], home.at[cx], own_x)
    keep.start()
    keep.wait()
    for k in range(1, NX):
        back(k).wait_send()
        back_arrival(k).wait_recv()


def panel_step(traded, reflect, n_row):
    rows, part = traded.shape
    peers = n_row * NX
    owners = 2 * (len(GRAM_TILES) + 4)
    half = BLOCK // 2
    dma = pltpu.SemaphoreType.DMA
    return pl.pallas_call(
        panel_kernel,
        out_shape=jax.ShapeDtypeStruct((NX, rows // NX, part), BF16),
        in_specs=[pl.BlockSpec(memory_space=pltpu.VMEM)] * 2,
        out_specs=pl.BlockSpec(memory_space=pltpu.VMEM),
        scratch_shapes=[
            pltpu.VMEM((rows + 2 * BLOCK, 4 * BLOCK), F32),
            pltpu.VMEM((2 * BLOCK, 2 * BLOCK), F32),
            pltpu.VMEM((owners, half, BLOCK), BF16),
            pltpu.VMEM((peers - 1, half, BLOCK), BF16),
            pltpu.VMEM((owners, half, BLOCK), BF16),
            pltpu.VMEM((NX, rows // NX, part), BF16),
            dma((peers - 1,)),
            dma((peers - 1,)),
            dma((peers - 1,)),
            dma((peers - 1,)),
            dma((NX - 1,)),
            dma((NX - 1,)),
            dma(()),
        ],
        compiler_params=pltpu.CompilerParams(
            collective_id=0, has_side_effects=True, vmem_limit_bytes=40 * 1024 * 1024
        ),
        cost_estimate=pl.CostEstimate(flops=20_000_000_000, bytes_accessed=4_000_000, transcendentals=0),
    )(traded, reflect)


def spread_dot(coeffs_top, coeffs_both, top, low):
    rows = coeffs_top.shape[0]
    d = functools.partial(lax.dot_general, dimension_numbers=NN, preferred_element_type=F32)
    first = d(coeffs_both, top)
    return first[:rows] + first[rows:] + d(coeffs_top, low)


def dot3_nt(a, b):
    a_top, a_low = halves(a)
    b_top, b_low = halves(b)
    d = functools.partial(lax.dot_general, dimension_numbers=NT, preferred_element_type=F32)
    return d(a_top, b_top) + (d(a_top, b_low) + d(a_low, b_top))


def span_kernel(offs, vectors, windows, eigen, cut, gathered, traded, kept, packs, inners, wide, tile_of, outgoing,
                send_a, recv_a, send_p, recv_p, send_w, recv_w, send_f, recv_f, send_b, recv_b, send_x, recv_x, own_sem):
    row, cx, cz = lax.axis_index("row"), lax.axis_index("cx"), lax.axis_index("cz")
    n_row = lax.axis_size("row")
    rows, cols = eigen.shape
    tiles_dev = cols // LANE
    part = cut.shape[3]
    per_dev = vectors.shape[0]
    half = per_dev // 2
    refl = 4
    spans = half // refl
    per_tile = BLOCK // half
    mesh = pl.DeviceIdType.MESH

    barrier = pltpu.get_barrier_semaphore()
    for k in range(1, n_row):
        pl.semaphore_signal(barrier, inc=1, device_id={"row": (row + k) % n_row}, device_id_type=mesh)
    for k in range(1, NX):
        pl.semaphore_signal(barrier, inc=1, device_id={"cx": (cx + k) % NX}, device_id_type=mesh)
    for k in (1, NZ - 1):
        pl.semaphore_signal(barrier, inc=1, device_id={"cz": (cz + k) % NZ}, device_id_type=mesh)

    lane8 = lax.broadcasted_iota(jnp.int32, (8, LANE), 1)
    line8 = lax.broadcasted_iota(jnp.int32, (8, LANE), 0)
    meta = jnp.zeros((8, LANE), F32)
    for s in range(2):
        for b in range(spans):
            at = offs[s * spans + b]
            place = (row % per_tile) * half + b * refl
            mine = (lane8 >= place) & (lane8 < place + refl)
            line = s * 2 + row // per_tile
            meta = jnp.where(mine & (line8 == line), ((at >> 7) + row * tiles_dev).astype(F32), meta)
            meta = jnp.where(mine & (line8 == line + 4), (at & 127).astype(F32), meta)
    packs[row, :per_dev] = vectors[...]
    packs[row, per_dev:] = meta

    pl.semaphore_wait(barrier, n_row - 1 + NX - 1 + 2)

    def over_x(k):
        return pltpu.make_async_remote_copy(
            src_ref=cut.at[(cx + k) % NX],
            dst_ref=gathered.at[:, cx, cz],
            send_sem=send_a.at[k - 1],
            recv_sem=recv_a.at[k - 1],
            device_id={"cx": (cx + k) % NX},
            device_id_type=mesh,
        )

    def over_x_arrival(k):
        source = (cx + NX - k) % NX
        return pltpu.make_async_remote_copy(
            src_ref=cut.at[source],
            dst_ref=gathered.at[:, source, cz],
            send_sem=send_a.at[k - 1],
            recv_sem=recv_a.at[k - 1],
            device_id={"cx": source},
            device_id_type=mesh,
        )

    def over_row(ref, sends, recvs, k):
        return pltpu.make_async_remote_copy(
            src_ref=ref.at[row],
            dst_ref=ref.at[row],
            send_sem=sends.at[k - 1],
            recv_sem=recvs.at[k - 1],
            device_id={"row": (row + k) % n_row},
            device_id_type=mesh,
        )

    def over_row_arrival(ref, sends, recvs, k):
        source = (row + n_row - k) % n_row
        return pltpu.make_async_remote_copy(
            src_ref=ref.at[source],
            dst_ref=ref.at[source],
            send_sem=sends.at[k - 1],
            recv_sem=recvs.at[k - 1],
            device_id={"row": source},
            device_id_type=mesh,
        )

    pieces = (0, 1, 3, 2)

    def ring(ahead, d, q, arriving):
        step = 1 if ahead else NZ - 1
        held = (cz + (NZ - d * step)) % NZ if ahead else (cz + d) % NZ
        if arriving:
            held = (held + (NZ - step)) % NZ
        source = (cx + NX - pieces[q]) % NX
        place = gathered.at[:, source, held]
        first = d == 0 and q == 0 and not arriving
        return pltpu.make_async_remote_copy(
            src_ref=cut.at[cx] if first else place,
            dst_ref=place,
            send_sem=(send_f if ahead else send_b).at[d * NX + q],
            recv_sem=(recv_f if ahead else recv_b).at[d * NX + q],
            device_id={"cz": (cz + step) % NZ},
            device_id_type=mesh,
        )

    last = NZ // 2 - 1

    def goes(ahead, d, q):
        return d < last or (q < NX // 2) == ahead

    def launch(d, q):
        for ahead in (True, False):
            if goes(ahead, d, q):
                ring(ahead, d, q, False).start()

    def pump(d, q):
        for ahead in (True, False):
            if goes(ahead, d, q):
                ring(ahead, d, q, True).wait_recv()
                if d < last and goes(ahead, d + 1, q):
                    ring(ahead, d + 1, q, False).start()

    launch(0, 0)
    for k in range(1, n_row):
        over_row(packs, send_p, recv_p, k).start()
    for k in (1, 3, 2):
        over_x(k).start()
    own_copy = pltpu.make_async_copy(cut.at[cx], gathered.at[:, cx, cz], own_sem)
    own_copy.start()

    for k in range(1, n_row):
        over_row_arrival(packs, send_p, recv_p, k).wait_recv()
    for q in range(1, NX):
        over_x_arrival(pieces[q]).wait_recv()
        launch(0, q)

    every_meta = packs[0, per_dev:]
    for r in range(1, n_row):
        every_meta = every_meta + packs[r, per_dev:]
    bp = lax.broadcasted_iota(jnp.int32, (BLOCK, BLOCK), 0)
    bq = lax.broadcasted_iota(jnp.int32, (BLOCK, BLOCK), 1)
    diag = bp == bq

    def turned(line):
        return jnp.sum(jnp.where(diag, line, 0.0), axis=1, keepdims=True)

    count = 2 * n_row * half // BLOCK
    across_tile = [every_meta[u : u + 1] for u in range(count)]
    down_tile = []
    for u in range(count):
        s, h = u // 2, u % 2
        low = jnp.concatenate(
            [packs[h * per_tile + k, s * half : (s + 1) * half] for k in range(per_tile)], axis=0
        )
        amount = turned(every_meta[u + 4 : u + 5]).astype(jnp.int32)
        both = jnp.concatenate([low, jnp.zeros_like(low)], axis=1)
        for bit in range(7):
            both = jnp.where(((amount >> bit) & 1) == 1, pltpu.roll(both, 1 << bit, 1), both)
        wide[u * BLOCK : (u + 1) * BLOCK] = both
        down = turned(across_tile[u])
        down_tile.append(down)
        tile_of[u * BLOCK : (u + 1) * BLOCK] = jnp.broadcast_to(down, (BLOCK, LANE))

    def of_row(ref, r):
        return jnp.concatenate(
            [ref[pl.ds(pl.multiple_of(s * n_row * half + r * half, half), half)] for s in range(2)], axis=0
        )

    prev_row = jnp.maximum(row - 1, 0)
    own_wide = of_row(wide, row)
    own_tile = of_row(tile_of, row) - (row * tiles_dev).astype(F32)
    prev_tile = of_row(tile_of, prev_row) - (row * tiles_dev).astype(F32)
    prev_high = jnp.where(prev_tile == -1.0, of_row(wide, prev_row)[:, LANE:], 0.0)

    table = dot3_nt(windows[...], own_wide)
    place = lax.broadcasted_iota(jnp.int32, (rows, per_dev), 1) // refl
    total = jnp.zeros((rows, per_dev), F32)
    for c in range(2 * spans):
        total = total + jnp.where(place == c, table[c * rows : (c + 1) * rows], 0.0)
    behind = dot3_nt(eigen[:, :LANE], prev_high)
    inners[row] = jnp.concatenate([total, behind], axis=1)
    for k in range(1, n_row):
        over_row(inners, send_w, recv_w, k).start()
    pump(0, 0)

    keep = (((bp // refl) == (bq // refl)) & (bp > bq)) | (((bp // refl) != (bq // refl)) & (bp < bq))
    strict, across = {}, []
    for u in range(count):
        mine = wide[u * BLOCK : (u + 1) * BLOCK]
        rest = wide[u * BLOCK :]
        level = dot3_nt(mine, rest)
        after = dot3_nt(mine[:, LANE:], rest[:, :LANE])
        before = dot3_nt(mine[:, :LANE], rest[:, LANE:])
        for t in range(u, count):
            cols_at = slice((t - u) * BLOCK, (t - u + 1) * BLOCK)
            gap = across_tile[t] - down_tile[u]
            tile = jnp.where(
                gap == 0.0,
                level[:, cols_at],
                jnp.where(gap == 1.0, after[:, cols_at], jnp.where(gap == -1.0, before[:, cols_at], 0.0)),
            )
            if t == u:
                picked = jnp.where(diag, tile, 0.0)
                scale = 2.0 / jnp.sum(picked, axis=1, keepdims=True)
                across.append(2.0 / jnp.sum(picked, axis=0, keepdims=True))
                tile = jnp.where(keep, tile, 0.0)
            strict[u, t] = tile * scale
        if u == 1:
            pump(0, 1)
    pump(0, 2)
    inverse = tile_inverses([strict[t, t] for t in range(count)])
    pump(0, 3)

    for k in range(1, n_row):
        over_row_arrival(inners, send_w, recv_w, k).wait_recv()
    lane = lax.broadcasted_iota(jnp.int32, (rows, LANE), 1) // half
    right = [jnp.zeros((rows, LANE), F32) for _ in range(count)]
    for r in range(n_row):
        values = inners[r]
        for s in range(2):
            u = s * 2 + r // per_tile
            moved = pltpu.roll(values, (half * (r % per_tile) - half * s) % LANE, 1)
            right[u] = right[u] + jnp.where(lane == r % per_tile, moved, 0.0)
            if r > 0:
                u = s * 2 + (r - 1) // per_tile
                moved = pltpu.roll(values, (half * ((r - 1) % per_tile) - per_dev - half * s) % LANE, 1)
                right[u] = right[u] + jnp.where(lane == (r - 1) % per_tile, moved, 0.0)
    found = []
    for t in range(count):
        value = right[t]
        for u in range(t):
            value = value - dot3(found[u], strict[u, t])
        found.append(dot3(value, inverse[t]))
    solved = [found[t] * across[t] for t in range(count)]
    pump(1, 0)

    def coeffs_of(r):
        result = jnp.zeros((rows, LANE), F32)
        for s in range(2):
            tile = jnp.where(r // per_tile == 0, solved[s * 2], solved[s * 2 + 1])
            moved = pltpu.roll(tile, (LANE - half * (r % per_tile) + half * s) % LANE, 1)
            result = jnp.where(lane == s, moved, result)
        return result[:, :per_dev]

    own_coeffs = coeffs_of(row)
    coeffs_top, coeffs_low = halves(own_coeffs)
    coeffs_both = jnp.concatenate([coeffs_top, coeffs_low], axis=0)
    first_change = dot3(coeffs_of(prev_row), prev_high)
    low_top, low_low = [v.astype(F32) for v in halves(own_wide[:, :LANE])]
    high_top, high_low = [v.astype(F32) for v in halves(own_wide[:, LANE:])]

    def over(first, second, tile):
        return jnp.where(own_tile == tile, first, jnp.where(own_tile == tile - 1.0, second, 0.0)).astype(BF16)

    def trade(k):
        target = (cx + k) % NX
        return pltpu.make_async_remote_copy(
            src_ref=outgoing.at[target],
            dst_ref=traded.at[cx],
            send_sem=send_x.at[k - 1],
            recv_sem=recv_x.at[k - 1],
            device_id={"cx": target},
            device_id_type=mesh,
        )

    def trade_arrival(k):
        source = (cx + NX - k) % NX
        return pltpu.make_async_remote_copy(
            src_ref=outgoing.at[source],
            dst_ref=traded.at[source],
            send_sem=send_x.at[k - 1],
            recv_sem=recv_x.at[k - 1],
            device_id={"cx": source},
            device_id_type=mesh,
        )

    group = 5
    per_part = part // LANE

    def changed(tile, tiles):
        base = tile.astype(F32) if not isinstance(tile, int) else jnp.float32(tile)
        top = jnp.concatenate([over(low_top, high_top, base + k) for k in range(tiles)], axis=1)
        low = jnp.concatenate([over(low_low, high_low, base + k) for k in range(tiles)], axis=1)
        return spread_dot(coeffs_top, coeffs_both, top, low)

    def apply(x):
        whole_groups = min(per_part, tiles_dev - x * per_part) // group

        def one(step, carry):
            tile = x * per_part + step * group
            at = pl.ds(pl.multiple_of(tile * LANE, LANE), group * LANE)
            value = eigen[:, at] - changed(tile, group)
            kept[:, at] = value
            outgoing[x, :, pl.ds(pl.multiple_of(step * group * LANE, LANE), group * LANE)] = value.astype(BF16)
            return carry

        lax.fori_loop(0, whole_groups, one, 0)
        tile = x * per_part + whole_groups * group
        over_tiles = min((x + 1) * per_part, tiles_dev) - tile
        begin = whole_groups * group * LANE
        if over_tiles > 0:
            value = eigen[:, tile * LANE :] - changed(tile, over_tiles)
            kept[:, tile * LANE :] = value
            outgoing[x, :, begin : begin + over_tiles * LANE] = value.astype(BF16)
            begin += over_tiles * LANE
        if begin < part:
            outgoing[x, :, begin:] = jnp.zeros((rows, part - begin), BF16)
        if x == 0:
            value = kept[:, :LANE] - first_change
            kept[:, :LANE] = value
            outgoing[0, :, :LANE] = value.astype(BF16)

    for x in range(NX):
        apply(x)
        pump(1, x + 1) if x + 1 < NX else None
    for k in (1, 3, 2):
        trade(k).start()
    own_copy.wait()
    keep_own = pltpu.make_async_copy(outgoing.at[cx], traded.at[cx], own_sem)
    keep_own.start()
    for d in range(2, last + 1):
        for q in range(NX):
            pump(d, q)
    keep_own.wait()
    for k in range(1, NX):
        trade(k).wait_send()
        trade_arrival(k).wait_recv()
        over_x(k).wait_send()
    for k in range(1, n_row):
        over_row(packs, send_p, recv_p, k).wait_send()
        over_row(inners, send_w, recv_w, k).wait_send()
    for d in range(last + 1):
        for q in range(NX):
            for ahead in (True, False):
                if goes(ahead, d, q):
                    ring(ahead, d, q, False).wait_send()


def span_step(offs, vectors, windows, eigen, cut, n_row):
    rows, cols = eigen.shape
    n_x, n_panel, refl_dev, part = cut.shape
    per_dev, band = vectors.shape
    dma = pltpu.SemaphoreType.DMA
    vmem = pl.BlockSpec(memory_space=pltpu.VMEM)
    units = (NZ // 2) * NX
    return pl.pallas_call(
        span_kernel,
        out_shape=[
            jax.ShapeDtypeStruct((n_panel, NX, NZ, refl_dev, part), BF16),
            jax.ShapeDtypeStruct((NX, rows, part), BF16),
            jax.ShapeDtypeStruct((rows, cols), F32),
        ],
        in_specs=[pl.BlockSpec(memory_space=pltpu.SMEM), vmem, vmem, vmem, vmem],
        out_specs=[vmem] * 3,
        scratch_shapes=[
            pltpu.VMEM((n_row, per_dev + 8, band), F32),
            pltpu.VMEM((n_row, rows, LANE), F32),
            pltpu.VMEM((n_row * per_dev, 2 * LANE), F32),
            pltpu.VMEM((n_row * per_dev, LANE), F32),
            pltpu.VMEM((NX, rows, part), BF16),
            dma((NX - 1,)),
            dma((NX - 1,)),
            dma((n_row - 1,)),
            dma((n_row - 1,)),
            dma((n_row - 1,)),
            dma((n_row - 1,)),
            dma((units,)),
            dma((units,)),
            dma((units,)),
            dma((units,)),
            dma((NX - 1,)),
            dma((NX - 1,)),
            dma(()),
        ],
        compiler_params=pltpu.CompilerParams(
            collective_id=1, has_side_effects=True, vmem_limit_bytes=50 * 1024 * 1024
        ),
        cost_estimate=pl.CostEstimate(flops=20_000_000_000, bytes_accessed=8_000_000, transcendentals=0),
    )(offs, vectors, windows, eigen, cut)


def prepare_kernel(offs, eigen, panels, windows, cut):
    rows, cols = eigen.shape
    tiles_dev = cols // LANE
    part = cut.shape[3]
    for c in range(windows.shape[0] // rows):
        at = offs[c] >> 7
        inside = jnp.where(at + 1 < tiles_dev, 1.0, 0.0).astype(F32)
        then = jnp.minimum(at + 1, tiles_dev - 1)
        windows[c * rows : (c + 1) * rows, :LANE] = eigen[:, pl.ds(pl.multiple_of(at * LANE, LANE), LANE)]
        windows[c * rows : (c + 1) * rows, LANE:] = (
            eigen[:, pl.ds(pl.multiple_of(then * LANE, LANE), LANE)] * inside
        )
    for x in range(NX):
        size = min(part, cols - x * part)
        for p in range(panels.shape[0]):
            cut[x, p, :, :size] = panels[p, :, x * part : x * part + size]
            if size < part:
                cut[x, p, :, size:] = jnp.zeros((panels.shape[1], part - size), BF16)


def prepare(offs, eigen, panels, part):
    rows = eigen.shape[0]
    n_panel, refl_dev, _ = panels.shape
    vmem = pl.BlockSpec(memory_space=pltpu.VMEM)
    return pl.pallas_call(
        prepare_kernel,
        out_shape=[
            jax.ShapeDtypeStruct((offs.shape[0] * rows, 2 * LANE), F32),
            jax.ShapeDtypeStruct((NX, n_panel, refl_dev, part), BF16),
        ],
        in_specs=[pl.BlockSpec(memory_space=pltpu.SMEM), vmem, vmem],
        out_specs=[vmem] * 2,
    )(offs, eigen, panels)


def local(eigvecs, span_vectors, span_offsets, panels):
    rows, cols = eigvecs.shape
    sweeps, spans_dev, refl, band = span_vectors.shape
    n_row = lax.psum(1, "row")
    part = -(-(cols // LANE) // NX) * LANE
    full = part * NX
    offs = span_offsets.reshape(-1)
    windows, cut = prepare(offs, eigvecs, panels, part)
    gathered, traded, eigen = span_step(offs, span_vectors.reshape(-1, band), windows, eigvecs, cut, n_row)
    home = panel_step(traded.reshape(NX * rows, part), gathered.reshape(-1, part), n_row)
    home = home.transpose(1, 0, 2).reshape(rows, full)[:, :cols]
    return eigen - home.astype(F32)


def solution(mesh):
    finer = Mesh(mesh.devices.reshape(mesh.shape["row"], NX, NZ), ("row", "cx", "cz"))
    col = ("cx", "cz")
    placed = (P(col, "row"), P(None, "row", None, None), P(None, "row"), P(None, col, "row"))
    return jax.shard_map(local, mesh=finer, in_specs=placed, out_specs=P(col, "row"), check_vma=False)
```

time: 140 us -> 97.4 us (0.70)
  Pallas kernels: 51.4 us -> 90.4 us
  starting transfers between devices: 31.8 us -> 0 us
  waiting for transfers between devices: 30.2 us -> 0 us
  local copies, waits for them, and re-layouts: 21.1 us -> 5.38 us
  other arithmetic: 3.98 us -> 1.32 us
    pallas_call x3 -> x2, Pallas kernels: 9.78 us -> 52.2 us  [the longest x1 49.7 us: span_step(): pl.pallas_call(span_kernel, out_shape=[jax.ShapeDtypeStruct((n_panel, NX,...]
    ppermute x7 -> x0, waiting for transfers between devices: 26.3 us -> none  [the longest x4 26.3 us: local(): forward = lax.ppermute(forward, 'cz', up)]
    all_to_all x4 -> x0, starting transfers between devices: 20.1 us -> none  [the longest x2 11.8 us: sent_to_all(): lax.all_to_all(jnp.broadcast_to(x[None], (peers, *x.shape)), axis, 0, 0,...]
    ppermute x7 -> x0, starting transfers between devices: 11.6 us -> none  [the longest x3 10.5 us: local(): backward = lax.ppermute(backward, 'cz', down)]
    all_to_all x4 -> x0, waiting for transfers between devices: 3.93 us -> none  [the longest x2 3.92 us: sent_to_all(): lax.all_to_all(jnp.broadcast_to(x[None], (peers, *x.shape)), axis, 0, 0,...]
    reshape x9 -> x1, local copies, waits for them, and re-layouts: 5.24 us -> 1.36 us  [local(): offs = span_offsets.reshape(-1)]
    pallas_call x1, Pallas kernels: 41.6 us -> 38.2 us  [panel_step(): pl.pallas_call(panel_kernel, out_shape=jax.ShapeDtypeStruct((NX, rows //...]
    dynamic_update_slice x8 -> x0, local copies, waits for them, and re-layouts: 3.31 us -> none  [local(): lax.dynamic_update_slice(gathered, piece, (0, 0, (at_z - step) % NZ, 0, 0))]
  transfers between devices with their start and end apart: 11 -> 0, of which waited for: 4 -> 0; matrix products, arithmetic and copies ran while one was open for 12% -> 0% of each run, Pallas kernels for 7% -> 0%
where the time goes in v3:
time: 97.4 us; the launch traced here: 97.1 us
  Pallas kernels  90.4 us (93%)
  local copies, waits for them, and re-layouts  5.38 us (6%)
  other arithmetic  1.32 us (1%)
    pallas_call x1, Pallas kernels, span_step(): pl.pallas_call(span_kernel, out_shape=[jax.ShapeDtypeStruct((n_panel, NX,...  49.7 us
    pallas_call x1, Pallas kernels, panel_step(): pl.pallas_call(panel_kernel, out_shape=jax.ShapeDtypeStruct((NX, rows //...  38.2 us
    unnamed x10, local copies, waits for them, and re-layouts  3.96 us
    pallas_call x1, Pallas kernels, prepare(): pl.pallas_call(prepare_kernel, out_shape=[jax.ShapeDtypeStruct((offs.shap...  2.49 us

profile of v3, /device:TPU:1, one launch (start us, length us, event | category | flops | bytes accessed | tf_op | source)
XLA Modules:
  0.0 97.1 jit_solution(4818678833223848560)
XLA Ops:
  0.0 0.0 copy-start.3
  0.0 1.4 %reshape.15.offs = s32[16]{0:T(128)} reshape(s32[2,8]{1,0:T(2,128)} %param.6) | data formatting | bytes 128 | tf_op jit(solution)/shard_map/reshape | solution.py:684
  1.4 0.0 copy-start
  1.4 2.5 %shard_map.46 = (f32[512,256]{1,0:T(8,128)}, bf16[4,2,8,3200]{3,2,1,0:T(8,128)(2,1)}) custom-call(s32[16]{0:T(128)} %reshape.15.offs, f32[32,12544]{1,0:T(8,128)} %eigen.3, bf16[2,8,12544]{2,1,0:T(8,128)(2,1)} %panels.1), custom_call_target="tpu_custom_call" | custom-call | tf_op jit(solution)/shard_map/pallas_call | solution.py:667
  3.9 0.0 copy-done.3
  3.9 0.0 copy-done
  3.9 0.0 copy-start.1
  3.9 1.0 %copy-done.1 = f32[512,256]{1,0:T(8,128)S(1)} copy-done((f32[512,256]{1,0:T(8,128)S(1)}, f32[512,256]{1,0:T(8,128)}, u32[]{:S(2)}) %copy-start.1) | copy-done | bytes 524312
  4.9 0.0 copy-start.2
  4.9 1.0 %copy-done.2 = bf16[4,2,8,3200]{3,2,1,0:T(8,128)(2,1)S(1)} copy-done((bf16[4,2,8,3200]{3,2,1,0:T(8,128)(2,1)S(1)}, bf16[4,2,8,3200]{3,2,1,0:T(8,128)(2,1)}, u32[]{:S(2)}) %copy-start.2) | copy-done | bytes 409624
  5.9 49.7 %shard_map.47 = (bf16[2,4,8,8,3200]{4,3,2,1,0:T(8,128)(2,1)}, bf16[4,32,3200]{2,1,0:T(8,128)(2,1)S(1)}, f32[32,12544]{1,0:T(8,128)S(1)}) custom-call(s32[16]{0:T(128)S(1)} %copy-done, f32[64,128]{1,0:T(8,128)S(1)} %bitcast.7, f32[512,256]{1,0:T(8,128)S(1)} %copy-done.1, f32[32,12544]{1,0:T(8,128)} %eigen.3, bf16[4,2,8,3200]{3,2,1,0:T(8,128)(2,1)S(1)} %copy-done.2), custom_call_target="tpu_custom_call" | custom-call | flops 20000000000 | bytes 8000000 | tf_op jit(solution)/shard_map/pallas_call | solution.py:607
  55.6 0.0 copy-start.4
  55.6 1.9 %copy-done.4 = bf16[2,4,8,8,3200]{4,3,2,1,0:T(8,128)(2,1)S(1)} copy-done((bf16[2,4,8,8,3200]{4,3,2,1,0:T(8,128)(2,1)S(1)}, bf16[2,4,8,8,3200]{4,3,2,1,0:T(8,128)(2,1)}, u32[]{:S(2)}) %copy-start.4) | copy-done | bytes 3276824
  57.6 38.2 %shard_map.48 = bf16[4,32,3200]{2,1,0:T(8,128)(2,1)S(1)} custom-call(bf16[128,3200]{1,0:T(8,128)(2,1)S(1)} %bitcast.9, bf16[512,3200]{1,0:T(8,128)(2,1)S(1)} %bitcast.8), custom_call_target="tpu_custom_call" | custom-call | flops 20000000000 | bytes 4000000 | tf_op jit(solution)/shard_map/pallas_call | solution.py:227
  95.7 0.1 copy.6
  95.8 1.3 %convert_subtract_fusion = f32[32,12544]{1,0:T(8,128)} fusion(f32[32,12544]{1,0:T(8,128)S(1)} %get-tuple-element.12, bf16[32,12800]{1,0:T(8,128)(2,1)S(1)} %bitcast.10), kind=kLoop, calls=%fused_computation | loop fusion | flops 802816 | bytes 4014080 | tf_op jit(solution)/shard_map/sub | solution.py:689
Async XLA Ops:
  0.0 3.9 %copy-start.3 = (f32[2,8,4,128]{3,2,1,0:T(4,128)S(1)}, f32[2,8,4,128]{3,2,1,0:T(4,128)}, u32[]{:S(2)}) copy-start(f32[2,8,4,128]{3,2,1,0:T(4,128)} %param.5) | copy-start | bytes 98308
  1.4 2.5 %copy-start = (s32[16]{0:T(128)S(1)}, s32[16]{0:T(128)}, u32[]{:S(2)}) copy-start(s32[16]{0:T(128)} %reshape.15.offs) | copy-start | bytes 196
  3.9 1.0 %copy-start.1 = (f32[512,256]{1,0:T(8,128)S(1)}, f32[512,256]{1,0:T(8,128)}, u32[]{:S(2)}) copy-start(f32[512,256]{1,0:T(8,128)} %get-tuple-element.10.windows) | copy-start | bytes 1572868
  4.9 1.0 %copy-start.2 = (bf16[4,2,8,3200]{3,2,1,0:T(8,128)(2,1)S(1)}, bf16[4,2,8,3200]{3,2,1,0:T(8,128)(2,1)}, u32[]{:S(2)}) copy-start(bf16[4,2,8,3200]{3,2,1,0:T(8,128)(2,1)} %get-tuple-element.11.cut) | copy-start | bytes 1228804
  55.6 1.9 %copy-start.4 = (bf16[2,4,8,8,3200]{4,3,2,1,0:T(8,128)(2,1)S(1)}, bf16[2,4,8,8,3200]{4,3,2,1,0:T(8,128)(2,1)}, u32[]{:S(2)}) copy-start(bf16[2,4,8,8,3200]{4,3,2,1,0:T(8,128)(2,1)} %get-tuple-element.14) | copy-start | bytes 9830404

commit v4 on v0

v4 whole, which is shorter than its diff:
```python
import functools

import jax
import jax.numpy as jnp
from jax import lax
from jax.experimental import pallas as pl
from jax.experimental.pallas import tpu as pltpu
from jax.sharding import Mesh
from jax.sharding import PartitionSpec as P

LANE = 128
BLOCK = 128
NX = 4
NZ = 8
CHUNKS = 5
F32 = jnp.float32
BF16 = jnp.bfloat16
NT = (((1,), (1,)), ((), ()))
NN = (((1,), (0,)), ((), ()))


def halves(a):
    top = a.astype(BF16)
    return top, (a - top.astype(F32)).astype(BF16)


def dot3(a, b):
    a_top, a_low = halves(a)
    b_top, b_low = halves(b)
    d = functools.partial(lax.dot_general, dimension_numbers=NN, preferred_element_type=F32)
    return d(a_top, b_top) + (d(a_top, b_low) + d(a_low, b_top))


GRAM_TILES = ((0, 0), (0, 2), (0, 3), (1, 0), (1, 1), (1, 2), (1, 3), (2, 2), (3, 2), (3, 3))


def dot3_nt(a, b):
    a_top, a_low = halves(a)
    b_top, b_low = halves(b)
    d = functools.partial(lax.dot_general, dimension_numbers=NT, preferred_element_type=F32)
    return d(a_top, b_top) + (d(a_top, b_low) + d(a_low, b_top))


def tile_inverses(tiles):
    bp = lax.broadcasted_iota(jnp.int32, (BLOCK, BLOCK), 0)
    bq = lax.broadcasted_iota(jnp.int32, (BLOCK, BLOCK), 1)
    eye = (bp == bq).astype(F32)
    inverse = [eye - jnp.where(bp // 2 == bq // 2, tile, 0.0) for tile in tiles]
    size = 2
    while size < BLOCK:
        joined = (bp // (2 * size) == bq // (2 * size)) & (bp // size != bq // size)
        left = [dot3(inv, jnp.where(joined, tile, 0.0)) for inv, tile in zip(inverse, tiles)]
        inverse = [inv - dot3(lhs, inv) for inv, lhs in zip(inverse, left)]
        size *= 2
    return inverse


def fused_kernel(offs, vectors, eigen, panels, kept, home, cut, gathered, packs, inners, wide, tile_of, placed_top,
                 placed_low, outgoing, traded, acc_top, acc_low, work, slots, whole, change, send_a, recv_a, send_p,
                 recv_p, send_w, recv_w, send_f, recv_f, send_b, recv_b, send_x, recv_x, send_rs, recv_rs, send_ag,
                 recv_ag, send_h, recv_h, own_sem):
    row, cx, cz = lax.axis_index("row"), lax.axis_index("cx"), lax.axis_index("cz")
    n_row = lax.axis_size("row")
    rows, cols = eigen.shape
    tiles_dev = cols // LANE
    part = cut.shape[3]
    per_part = part // LANE
    chunk = part // CHUNKS
    per_dev = vectors.shape[0]
    half = per_dev // 2
    refl = 4
    spans = half // refl
    per_tile = BLOCK // half
    peers = n_row * NX
    me = row * NX + cx
    owners = work.shape[0]
    mesh = pl.DeviceIdType.MESH

    def device(place):
        return {"row": place // NX, "cx": place % NX}

    barrier = pltpu.get_barrier_semaphore()
    for k in (1, NZ - 1):
        pl.semaphore_signal(barrier, inc=1, device_id={"cz": (cz + k) % NZ}, device_id_type=mesh)
    for k in range(1, peers):
        pl.semaphore_signal(barrier, inc=1, device_id=device((me + k) % peers), device_id_type=mesh)

    for x in range(NX):
        size = min(part, cols - x * part)
        for p in range(panels.shape[0]):
            cut[x, p, :, :size] = panels[p, :, x * part : x * part + size]
            if size < part:
                cut[x, p, :, size:] = jnp.zeros((panels.shape[1], part - size), BF16)

    lane8 = lax.broadcasted_iota(jnp.int32, (8, LANE), 1)
    line8 = lax.broadcasted_iota(jnp.int32, (8, LANE), 0)
    line64 = lax.broadcasted_iota(jnp.int32, (per_dev, LANE), 0) // refl
    meta = jnp.zeros((8, LANE), F32)
    own_tile = jnp.zeros((per_dev, LANE), F32)
    own_shift = jnp.zeros((per_dev, LANE), jnp.int32)
    for s in range(2):
        for b in range(spans):
            at = offs[s, b]
            tile_at = at >> 7
            shift_at = at & 127
            place = (row % per_tile) * half + b * refl
            mine = (lane8 >= place) & (lane8 < place + refl)
            line = s * 2 + row // per_tile
            meta = jnp.where(mine & (line8 == line), (tile_at + row * tiles_dev).astype(F32), meta)
            meta = jnp.where(mine & (line8 == line + 4), shift_at.astype(F32), meta)
            own_tile = jnp.where(line64 == s * spans + b, tile_at.astype(F32), own_tile)
            own_shift = jnp.where(line64 == s * spans + b, shift_at, own_shift)
    packs[row, :per_dev] = vectors[...]
    packs[row, per_dev:] = meta

    def over_x(j, k):
        at = pl.ds(j * chunk, chunk)
        return pltpu.make_async_remote_copy(
            src_ref=cut.at[(cx + k) % NX, :, :, at],
            dst_ref=gathered.at[:, cx, cz, :, at],
            send_sem=send_a.at[j, k - 1],
            recv_sem=recv_a.at[j, k - 1],
            device_id={"cx": (cx + k) % NX},
            device_id_type=mesh,
        )

    def over_x_arrival(j, k):
        at = pl.ds(j * chunk, chunk)
        source = (cx + NX - k) % NX
        return pltpu.make_async_remote_copy(
            src_ref=cut.at[source, :, :, at],
            dst_ref=gathered.at[:, source, cz, :, at],
            send_sem=send_a.at[j, k - 1],
            recv_sem=recv_a.at[j, k - 1],
            device_id={"cx": source},
            device_id_type=mesh,
        )

    def over_row(ref, sends, recvs, k):
        return pltpu.make_async_remote_copy(
            src_ref=ref.at[row],
            dst_ref=ref.at[row],
            send_sem=sends.at[k - 1],
            recv_sem=recvs.at[k - 1],
            device_id={"row": (row + k) % n_row},
            device_id_type=mesh,
        )

    def over_row_arrival(ref, sends, recvs, k):
        source = (row + n_row - k) % n_row
        return pltpu.make_async_remote_copy(
            src_ref=ref.at[source],
            dst_ref=ref.at[source],
            send_sem=sends.at[k - 1],
            recv_sem=recvs.at[k - 1],
            device_id={"row": source},
            device_id_type=mesh,
        )

    last = NZ // 2 - 1

    def ring(ahead, d, j, arriving):
        step = 1 if ahead else NZ - 1
        held = (cz + (NZ - d)) % NZ if ahead else (cz + d) % NZ
        if arriving:
            held = (held + (NZ - step)) % NZ
        at = pl.ds(j * chunk, chunk)
        panel = slice(None) if d < last else (pl.ds(0, 1) if ahead else pl.ds(1, 1))
        place = gathered.at[panel, :, held, :, at]
        return pltpu.make_async_remote_copy(
            src_ref=place,
            dst_ref=place,
            send_sem=(send_f if ahead else send_b).at[d * CHUNKS + j],
            recv_sem=(recv_f if ahead else recv_b).at[d * CHUNKS + j],
            device_id={"cz": (cz + step) % NZ},
            device_id_type=mesh,
        )

    def launch(d, j):
        for ahead in (True, False):
            ring(ahead, d, j, False).start()

    def pump(d, j):
        for ahead in (True, False):
            ring(ahead, d, j, True).wait_recv()
            if d < last:
                ring(ahead, d + 1, j, False).start()

    own_copy = pltpu.make_async_copy(cut.at[cx], gathered.at[:, cx, cz], own_sem)
    own_copy.start()
    pl.semaphore_wait(barrier, peers - 1 + 2)
    for j in range(CHUNKS):
        for k in (1, 3, 2):
            over_x(j, k).start()
        if j == 0:
            for k in range(1, n_row):
                over_row(packs, send_p, recv_p, k).start()

    def shifted(values, amount):
        both = jnp.concatenate([values, jnp.zeros_like(values)], axis=1)
        for bit in range(7):
            both = jnp.where(((amount >> bit) & 1) == 1, pltpu.roll(both, 1 << bit, 1), both)
        return both

    own_wide = shifted(vectors[...], jnp.concatenate([own_shift, own_shift], axis=1))
    low_top, low_low = [v.astype(F32) for v in halves(own_wide[:, :LANE])]
    high_top, high_low = [v.astype(F32) for v in halves(own_wide[:, LANE:])]
    group = 7

    def build(step, carry):
        for k in range(group):
            tile = (step * group + k).astype(F32)
            first, second = own_tile == tile, own_tile == tile - 1.0
            at = pl.ds(pl.multiple_of((step * group + k) * LANE, LANE), LANE)
            placed_top[:, at] = jnp.where(first, low_top, jnp.where(second, high_top, 0.0)).astype(BF16)
            placed_low[:, at] = jnp.where(first, low_low, jnp.where(second, high_low, 0.0)).astype(BF16)
        return carry

    lax.fori_loop(0, tiles_dev // group, build, 0)
    own_copy.wait()
    for j in range(CHUNKS):
        for k in (1, 3, 2):
            over_x_arrival(j, k).wait_recv()
        launch(0, j)

    mxu_nt = functools.partial(lax.dot_general, dimension_numbers=NT, preferred_element_type=F32)
    mxu = functools.partial(lax.dot_general, dimension_numbers=NN, preferred_element_type=F32)

    def inner_step(step, total):
        at = pl.ds(pl.multiple_of(step * group * LANE, LANE), group * LANE)
        top, low = halves(eigen[:, at])
        first = mxu_nt(jnp.concatenate([top, low], axis=0), placed_top[:, at])
        return total + first[:rows] + first[rows:] + mxu_nt(top, placed_low[:, at])

    total = lax.fori_loop(0, tiles_dev // group, inner_step, jnp.zeros((rows, per_dev), F32))

    for k in range(1, n_row):
        over_row_arrival(packs, send_p, recv_p, k).wait_recv()
    every_meta = packs[0, per_dev:]
    for r in range(1, n_row):
        every_meta = every_meta + packs[r, per_dev:]
    bp = lax.broadcasted_iota(jnp.int32, (BLOCK, BLOCK), 0)
    bq = lax.broadcasted_iota(jnp.int32, (BLOCK, BLOCK), 1)
    diag = bp == bq

    def turned(line):
        return jnp.sum(jnp.where(diag, line, 0.0), axis=1, keepdims=True)

    count = 2 * n_row * half // BLOCK
    across_tile = [every_meta[u : u + 1] for u in range(count)]
    down_tile = []
    for u in range(count):
        s, h = u // 2, u % 2
        low = jnp.concatenate(
            [packs[h * per_tile + k, s * half : (s + 1) * half] for k in range(per_tile)], axis=0
        )
        wide[u * BLOCK : (u + 1) * BLOCK] = shifted(low, turned(every_meta[u + 4 : u + 5]).astype(jnp.int32))
        down = turned(across_tile[u])
        down_tile.append(down)
        tile_of[u * BLOCK : (u + 1) * BLOCK] = jnp.broadcast_to(down, (BLOCK, LANE))

    def of_row(ref, r):
        return jnp.concatenate(
            [ref[pl.ds(pl.multiple_of(s * n_row * half + r * half, half), half)] for s in range(2)], axis=0
        )

    prev_row = jnp.maximum(row - 1, 0)
    prev_tile = of_row(tile_of, prev_row) - (row * tiles_dev).astype(F32)
    prev_high = jnp.where(prev_tile == -1.0, of_row(wide, prev_row)[:, LANE:], 0.0)
    behind = dot3_nt(eigen[:, :LANE], prev_high)
    inners[row] = jnp.concatenate([total, behind], axis=1)
    for k in range(1, n_row):
        over_row(inners, send_w, recv_w, k).start()
    pump(0, 0)
    pump(0, 1)

    keep = (((bp // refl) == (bq // refl)) & (bp > bq)) | (((bp // refl) != (bq // refl)) & (bp < bq))
    strict, across = {}, []
    for u in range(count):
        mine = wide[u * BLOCK : (u + 1) * BLOCK]
        rest = wide[u * BLOCK :]
        level = dot3_nt(mine, rest)
        after = dot3_nt(mine[:, LANE:], rest[:, :LANE])
        before = dot3_nt(mine[:, :LANE], rest[:, LANE:])
        for t in range(u, count):
            cols_at = slice((t - u) * BLOCK, (t - u + 1) * BLOCK)
            gap = across_tile[t] - down_tile[u]
            tile = jnp.where(
                gap == 0.0,
                level[:, cols_at],
                jnp.where(gap == 1.0, after[:, cols_at], jnp.where(gap == -1.0, before[:, cols_at], 0.0)),
            )
            if t == u:
                picked = jnp.where(diag, tile, 0.0)
                scale = 2.0 / jnp.sum(picked, axis=1, keepdims=True)
                across.append(2.0 / jnp.sum(picked, axis=0, keepdims=True))
                tile = jnp.where(keep, tile, 0.0)
            strict[u, t] = tile * scale
        if u == 1:
            pump(0, 2)
    pump(0, 3)
    inverse = tile_inverses([strict[t, t] for t in range(count)])
    pump(0, 4)

    for k in range(1, n_row):
        over_row_arrival(inners, send_w, recv_w, k).wait_recv()
    lane = lax.broadcasted_iota(jnp.int32, (rows, LANE), 1) // half
    right = [jnp.zeros((rows, LANE), F32) for _ in range(count)]
    for r in range(n_row):
        values = inners[r]
        for s in range(2):
            u = s * 2 + r // per_tile
            moved = pltpu.roll(values, (half * (r % per_tile) - half * s) % LANE, 1)
            right[u] = right[u] + jnp.where(lane == r % per_tile, moved, 0.0)
            if r > 0:
                u = s * 2 + (r - 1) // per_tile
                moved = pltpu.roll(values, (half * ((r - 1) % per_tile) - per_dev - half * s) % LANE, 1)
                right[u] = right[u] + jnp.where(lane == (r - 1) % per_tile, moved, 0.0)
    found = []
    for t in range(count):
        value = right[t]
        for u in range(t):
            value = value - dot3(found[u], strict[u, t])
        found.append(dot3(value, inverse[t]))
    solved = [found[t] * across[t] for t in range(count)]
    pump(1, 0)

    def coeffs_of(r):
        result = jnp.zeros((rows, LANE), F32)
        for s in range(2):
            tile = jnp.where(r // per_tile == 0, solved[s * 2], solved[s * 2 + 1])
            moved = pltpu.roll(tile, (LANE - half * (r % per_tile) + half * s) % LANE, 1)
            result = jnp.where(lane == s, moved, result)
        return result[:, :per_dev]

    coeffs_top, coeffs_low = halves(coeffs_of(row))
    coeffs_both = jnp.concatenate([coeffs_top, coeffs_low], axis=0)
    first_change = dot3(coeffs_of(prev_row), prev_high)

    def changed(at):
        first = mxu(coeffs_both, placed_top[:, at])
        return first[:rows] + first[rows:] + mxu(coeffs_top, placed_low[:, at])

    def trade(x):
        return pltpu.make_async_remote_copy(
            src_ref=outgoing.at[x],
            dst_ref=traded.at[cx],
            send_sem=send_x.at[x],
            recv_sem=recv_x.at[cx],
            device_id={"cx": x},
            device_id_type=mesh,
        )

    def trade_arrival(x):
        return pltpu.make_async_remote_copy(
            src_ref=outgoing.at[x],
            dst_ref=traded.at[x],
            send_sem=send_x.at[x],
            recv_sem=recv_x.at[x],
            device_id={"cx": x},
            device_id_type=mesh,
        )

    five = 5

    def apply(x):
        whole_groups = min(per_part, tiles_dev - x * per_part) // five

        def one(step, carry):
            tile = x * per_part + step * five
            at = pl.ds(pl.multiple_of(tile * LANE, LANE), five * LANE)
            value = eigen[:, at] - changed(at)
            kept[:, at] = value
            outgoing[x, :, pl.ds(pl.multiple_of(step * five * LANE, LANE), five * LANE)] = value.astype(BF16)
            return carry

        lax.fori_loop(0, whole_groups, one, 0)
        tile = x * per_part + whole_groups * five
        over_tiles = min((x + 1) * per_part, tiles_dev) - tile
        begin = whole_groups * five * LANE
        if over_tiles > 0:
            at = slice(tile * LANE, (tile + over_tiles) * LANE)
            value = eigen[:, at] - changed(at)
            kept[:, at] = value
            outgoing[x, :, begin : begin + over_tiles * LANE] = value.astype(BF16)
            begin += over_tiles * LANE
        if begin < part:
            outgoing[x, :, begin:] = jnp.zeros((rows, part - begin), BF16)
        if x == 0:
            value = kept[:, :LANE] - first_change
            kept[:, :LANE] = value
            outgoing[0, :, :LANE] = value.astype(BF16)

    for x in range(NX):
        apply(x)
        pl.when(cx != x)(trade(x).start)
        pump(1, x + 1)
    keep_own = pltpu.make_async_copy(outgoing.at[cx], traded.at[cx], own_sem)
    keep_own.start()
    acc_top[...] = jnp.zeros_like(acc_top)
    acc_low[...] = jnp.zeros_like(acc_low)
    for j in range(CHUNKS):
        pump(2, j)
    keep_own.wait()
    for x in range(NX):
        pl.when(cx != x)(trade_arrival(x).wait_recv)

    def reflect(at, panel):
        return gathered[panel, :, :, :, at].reshape(-1, chunk)

    for j in range(CHUNKS):
        pump(last, j)
        at = slice(j * chunk, (j + 1) * chunk)
        upper, lower = reflect(at, 0), reflect(at, 1)
        both = jnp.concatenate([upper, lower], axis=0)
        top = jnp.concatenate([traded[:, :, at].reshape(-1, chunk), upper], axis=0)
        acc_top[...] += mxu_nt(top, both)
        acc_low[...] += mxu_nt(lower, lower)

    piece = BLOCK // 2

    def put(place, value):
        rounded = value.astype(BF16)
        work[2 * place] = rounded[:piece]
        work[2 * place + 1] = rounded[piece:]

    for place, (u, t) in enumerate(GRAM_TILES):
        if u < 2:
            put(place, acc_top[(1 + u) * BLOCK : (2 + u) * BLOCK, t * BLOCK : (t + 1) * BLOCK])
        else:
            put(place, acc_low[(u - 2) * BLOCK : (u - 1) * BLOCK, (t - 2) * BLOCK : (t - 1) * BLOCK])
    for t in range(4):
        put(len(GRAM_TILES) + t, acc_top[:BLOCK, t * BLOCK : (t + 1) * BLOCK])

    def scatter(k):
        target = (me + k) % peers
        return target, pltpu.make_async_remote_copy(
            src_ref=work.at[lax.rem(target, owners)],
            dst_ref=slots.at[k - 1],
            send_sem=send_rs.at[k - 1],
            recv_sem=recv_rs.at[k - 1],
            device_id=device(target),
            device_id_type=mesh,
        )

    def gather(k):
        return pltpu.make_async_remote_copy(
            src_ref=whole.at[lax.rem(me, owners)],
            dst_ref=whole.at[lax.rem(me, owners)],
            send_sem=send_ag.at[k - 1],
            recv_sem=recv_ag.at[k - 1],
            device_id=device((me + k) % peers),
            device_id_type=mesh,
        )

    def arrival(k):
        source = lax.rem((me + peers - k) % peers, owners)
        return pltpu.make_async_remote_copy(
            src_ref=whole.at[source],
            dst_ref=whole.at[source],
            send_sem=send_ag.at[k - 1],
            recv_sem=recv_ag.at[k - 1],
            device_id=device((me + k) % peers),
            device_id_type=mesh,
        )

    for k in range(1, peers):
        target, copy = scatter(k)
        pl.when(target < owners)(copy.start)

    @pl.when(me < owners)
    def _():
        value = work[lax.rem(me, owners)].astype(F32)
        for k in range(1, peers):
            scatter(k)[1].wait_recv()
            value = value + slots[k - 1].astype(F32)
        whole[lax.rem(me, owners)] = value.astype(BF16)
        for k in range(1, peers):
            gather(k).start()

    for k in range(1, peers):
        source = (me + peers - k) % peers
        pl.when(source < owners)(arrival(k).wait_recv)

    def got(place):
        return jnp.concatenate([whole[2 * place].astype(F32), whole[2 * place + 1].astype(F32)], axis=0)

    gram = {key: got(place) for place, key in enumerate(GRAM_TILES)}
    picked = [jnp.where(diag, gram[t, t], 0.0) for t in range(4)]
    down = [2.0 / jnp.sum(p, axis=1, keepdims=True) for p in picked]
    beside = [2.0 / jnp.sum(p, axis=0, keepdims=True) for p in picked]
    panel_strict = {(u, t): gram[u, t] * down[u] for u, t in GRAM_TILES}
    for t in range(4):
        panel_strict[t, t] = jnp.where(bp > bq, panel_strict[t, t], 0.0)
    panel_inverse = tile_inverses([panel_strict[t, t] for t in range(4)])
    answer = {}
    for t in (1, 0, 3, 2):
        value = got(len(GRAM_TILES) + t)
        for u in tuple(answer):
            value = value - dot3(answer[u], panel_strict[u, t])
        answer[t] = dot3(value, panel_inverse[t])
    coeffs = jnp.concatenate([(answer[t] * beside[t]).astype(BF16) for t in range(4)], axis=1)

    def back(j, k):
        target = (cx + k) % NX
        at = pl.ds(j * chunk, chunk)
        return pltpu.make_async_remote_copy(
            src_ref=change.at[target, :, at],
            dst_ref=home.at[cx, :, at],
            send_sem=send_h.at[j, k - 1],
            recv_sem=recv_h.at[j, k - 1],
            device_id={"cx": target},
            device_id_type=mesh,
        )

    def back_arrival(j, k):
        source = (cx + NX - k) % NX
        at = pl.ds(j * chunk, chunk)
        return pltpu.make_async_remote_copy(
            src_ref=change.at[source, :, at],
            dst_ref=home.at[source, :, at],
            send_sem=send_h.at[j, k - 1],
            recv_sem=recv_h.at[j, k - 1],
            device_id={"cx": source},
            device_id_type=mesh,
        )

    for j in range(CHUNKS):
        at = slice(j * chunk, (j + 1) * chunk)
        value = mxu(coeffs, jnp.concatenate([reflect(at, 0), reflect(at, 1)], axis=0)).astype(BF16)
        for x in range(NX):
            change[x, :, at] = value[x * rows : (x + 1) * rows]
        for k in (2, 1, 3):
            back(j, k).start()
    keep_home = pltpu.make_async_copy(change.at[cx], home.at[cx], own_sem)
    keep_home.start()

    for x in range(NX):
        pl.when(cx != x)(trade(x).wait_send)
    for k in range(1, n_row):
        over_row(packs, send_p, recv_p, k).wait_send()
        over_row(inners, send_w, recv_w, k).wait_send()
    for d in range(last + 1):
        for j in range(CHUNKS):
            for ahead in (True, False):
                ring(ahead, d, j, False).wait_send()
    for k in range(1, peers):
        target, copy = scatter(k)
        pl.when(target < owners)(copy.wait_send)

    @pl.when(me < owners)
    def _():
        for k in range(1, peers):
            gather(k).wait_send()

    keep_home.wait()
    for j in range(CHUNKS):
        for k in range(1, NX):
            over_x(j, k).wait_send()
            back(j, k).wait_send()
            back_arrival(j, k).wait_recv()


def fused_step(offs, vectors, eigen, panels, n_row):
    rows, cols = eigen.shape
    n_panel, refl_dev, _ = panels.shape
    part = -(-(cols // LANE) // NX) * LANE
    per_dev, band = vectors.shape
    peers = n_row * NX
    owners = 2 * (len(GRAM_TILES) + 4)
    piece = BLOCK // 2
    dma = pltpu.SemaphoreType.DMA
    vmem = pl.BlockSpec(memory_space=pltpu.VMEM)
    units = (NZ // 2) * CHUNKS
    return pl.pallas_call(
        fused_kernel,
        out_shape=[jax.ShapeDtypeStruct((rows, cols), F32), jax.ShapeDtypeStruct((NX, rows, part), BF16)],
        in_specs=[pl.BlockSpec(memory_space=pltpu.SMEM), vmem, vmem, vmem],
        out_specs=[vmem] * 2,
        scratch_shapes=[
            pltpu.VMEM((NX, n_panel, refl_dev, part), BF16),
            pltpu.VMEM((n_panel, NX, NZ, refl_dev, part), BF16),
            pltpu.VMEM((n_row, per_dev + 8, band), F32),
            pltpu.VMEM((n_row, rows, LANE), F32),
            pltpu.VMEM((n_row * per_dev, 2 * LANE), F32),
            pltpu.VMEM((n_row * per_dev, LANE), F32),
            pltpu.VMEM((per_dev, cols), BF16),
            pltpu.VMEM((per_dev, cols), BF16),
            pltpu.VMEM((NX, rows, part), BF16),
            pltpu.VMEM((NX, rows, part), BF16),
            pltpu.VMEM((NX * rows + 2 * BLOCK, 4 * BLOCK), F32),
            pltpu.VMEM((2 * BLOCK, 2 * BLOCK), F32),
            pltpu.VMEM((owners, piece, BLOCK), BF16),
            pltpu.VMEM((peers - 1, piece, BLOCK), BF16),
            pltpu.VMEM((owners, piece, BLOCK), BF16),
            pltpu.VMEM((NX, rows, part), BF16),
            dma((CHUNKS, NX - 1)),
            dma((CHUNKS, NX - 1)),
            dma((n_row - 1,)),
            dma((n_row - 1,)),
            dma((n_row - 1,)),
            dma((n_row - 1,)),
            dma((units,)),
            dma((units,)),
            dma((units,)),
            dma((units,)),
            dma((NX,)),
            dma((NX,)),
            dma((peers - 1,)),
            dma((peers - 1,)),
            dma((peers - 1,)),
            dma((peers - 1,)),
            dma((CHUNKS, NX - 1)),
            dma((CHUNKS, NX - 1)),
            dma(()),
        ],
        compiler_params=pltpu.CompilerParams(
            collective_id=0, has_side_effects=True, vmem_limit_bytes=40 * 1024 * 1024
        ),
        cost_estimate=pl.CostEstimate(flops=20_000_000_000, bytes_accessed=8_000_000, transcendentals=0),
    )(offs, vectors, eigen, panels)


def local(eigvecs, span_vectors, span_offsets, panels):
    rows, cols = eigvecs.shape
    band = span_vectors.shape[3]
    n_row = lax.psum(1, "row")
    eigen, home = fused_step(span_offsets, span_vectors.reshape(-1, band), eigvecs, panels, n_row)
    home = home.transpose(1, 0, 2).reshape(rows, -1)[:, :cols]
    return eigen - home.astype(F32)


def solution(mesh):
    finer = Mesh(mesh.devices.reshape(mesh.shape["row"], NX, NZ), ("row", "cx", "cz"))
    col = ("cx", "cz")
    placed = (P(col, "row"), P(None, "row", None, None), P(None, "row"), P(None, col, "row"))
    return jax.shard_map(local, mesh=finer, in_specs=placed, out_specs=P(col, "row"), check_vma=False)
```

time: 2030 us -> 87.6 us (0.04)
  starting transfers between devices: 850 us -> 0 us
  matrix products: 416 us -> 0 us
  local copies, waits for them, and re-layouts: 375 us -> 3.91 us
  waiting for transfers between devices: 231 us -> 0 us
  other arithmetic: 101 us -> 1.29 us
  Pallas kernels: 0 us -> 82.2 us
  loops' own time: 38 us -> 0 us
    ppermute x18 -> x0, starting transfers between devices: 569 us -> none  [from_behind(): lax.ppermute(value, axis, [(source, source + steps) for source in range(f...]
    dot_general x566 -> x0, matrix products: 416 us -> none  [the longest x512 377 us: step(): partial_sum = jnp.dot(matrow, solution)]
    dynamic_slice x528 -> x0, local copies, waits for them, and re-layouts: 312 us -> none  [the longest x512 303 us: step(): pivot = lax.dynamic_index_in_dim(matrow, place, 0, keepdims=False)]
    all_to_all x4 -> x0, starting transfers between devices: 281 us -> none  [sent_to_all(): lax.all_to_all(jnp.broadcast_to(x[None], (peers, *x.shape)), axis, 0, 0,...]
    ppermute x18 -> x0, waiting for transfers between devices: 186 us -> none  [from_behind(): lax.ppermute(value, axis, [(source, source + steps) for source in range(f...]
    div x16 -> x0, other arithmetic: 97.9 us -> none  [upper_solve(): solved[back_at] = value / matrix[back_at, back_at]]
    pallas_call x0 -> x1, Pallas kernels: none -> 82.2 us  [fused_step(): pl.pallas_call(fused_kernel, out_shape=[jax.ShapeDtypeStruct((rows, cols)...]
    another operation x22 -> x0, loops' own time: 38 us -> none  [the longest x2 28.4 us: run_spans(): return lax.fori_loop(0, vectors.shape[0], advance, block)]
  transfers between devices with their start and end apart: 24 -> 0, of which waited for: 21 -> 0; matrix products, arithmetic and copies ran while one was open for 22% -> 0% of each run, Pallas kernels for 0% -> 0%
where the time goes in v4:
time: 87.6 us; the launch traced here: 87.4 us
  Pallas kernels  82.2 us (94%)
  local copies, waits for them, and re-layouts  3.91 us (4%)
  other arithmetic  1.29 us (1%)
    pallas_call x1, Pallas kernels, fused_step(): pl.pallas_call(fused_kernel, out_shape=[jax.ShapeDtypeStruct((rows, cols)...  82.2 us
    unnamed x8, local copies, waits for them, and re-layouts  3.85 us

profile of v4, /device:TPU:1, one launch (start us, length us, event | category | flops | bytes accessed | tf_op | source)
XLA Modules:
  0.0 87.4 jit_solution(8904877855958969031)
XLA Ops:
  0.0 0.0 copy-start
  0.0 1.4 %copy-done = f32[32,12544]{1,0:T(8,128)S(1)} copy-done((f32[32,12544]{1,0:T(8,128)S(1)}, f32[32,12544]{1,0:T(8,128)}, u32[]{:S(2)}) %copy-start) | copy-done | bytes 1605656
  1.4 0.0 copy-start.1
  1.4 1.0 %copy-done.1 = bf16[2,8,12544]{2,1,0:T(8,128)(2,1)S(1)} copy-done((bf16[2,8,12544]{2,1,0:T(8,128)(2,1)S(1)}, bf16[2,8,12544]{2,1,0:T(8,128)(2,1)}, u32[]{:S(2)}) %copy-start.1) | copy-done | bytes 401432
  2.4 0.0 copy-start.2
  2.4 0.8 copy-done.2
  3.2 0.0 copy-start.3
  3.2 0.7 copy-done.3
  3.9 82.2 %shard_map.46 = (f32[32,12544]{1,0:T(8,128)S(1)}, bf16[4,32,3200]{2,1,0:T(8,128)(2,1)S(1)}) custom-call(s32[2,8]{1,0:T(2,128)S(1)} %copy-done.3, f32[64,128]{1,0:T(8,128)S(1)} %bitcast.5, f32[32,12544]{1,0:T(8,128)S(1)} %copy-done, bf16[2,8,12544]{2,1,0:T(8,128)(2,1)S(1)} %copy-done.1), custom_call_target="tpu_custom_call" | custom-call | flops 20000000000 | bytes 8000000 | tf_op jit(solution)/shard_map/pallas_call | solution.py:575
  86.0 0.1 copy.6
  86.1 1.3 %convert_subtract_fusion = f32[32,12544]{1,0:T(8,128)} fusion(f32[32,12544]{1,0:T(8,128)S(1)} %get-tuple-element.7, bf16[32,12800]{1,0:T(8,128)(2,1)S(1)} %bitcast.6), kind=kLoop, calls=%fused_computation | loop fusion | flops 802816 | bytes 4014080 | tf_op jit(solution)/shard_map/sub | solution.py:630
Async XLA Ops:
  0.0 1.4 %copy-start = (f32[32,12544]{1,0:T(8,128)S(1)}, f32[32,12544]{1,0:T(8,128)}, u32[]{:S(2)}) copy-start(f32[32,12544]{1,0:T(8,128)} %eigen.1) | copy-start | bytes 4816900
  1.4 1.0 %copy-start.1 = (bf16[2,8,12544]{2,1,0:T(8,128)(2,1)S(1)}, bf16[2,8,12544]{2,1,0:T(8,128)(2,1)}, u32[]{:S(2)}) copy-start(bf16[2,8,12544]{2,1,0:T(8,128)(2,1)} %panels.1) | copy-start | bytes 1204228
  2.4 0.8 copy-start.2
  3.2 0.7 copy-start.3

commit v5 on v4

v5 whole, which is shorter than its diff:
```python
import functools

import jax
import jax.numpy as jnp
from jax import lax
from jax.experimental import pallas as pl
from jax.experimental.pallas import tpu as pltpu
from jax.sharding import Mesh
from jax.sharding import PartitionSpec as P

LANE = 128
BLOCK = 128
NX = 4
NZ = 8
CHUNKS = 5
F32 = jnp.float32
BF16 = jnp.bfloat16
NT = (((1,), (1,)), ((), ()))
NN = (((1,), (0,)), ((), ()))


def halves(a):
    top = a.astype(BF16)
    return top, (a - top.astype(F32)).astype(BF16)


def dot3(a, b):
    a_top, a_low = halves(a)
    b_top, b_low = halves(b)
    d = functools.partial(lax.dot_general, dimension_numbers=NN, preferred_element_type=F32)
    return d(a_top, b_top) + (d(a_top, b_low) + d(a_low, b_top))


def dot3_nt(a, b):
    a_top, a_low = halves(a)
    b_top, b_low = halves(b)
    d = functools.partial(lax.dot_general, dimension_numbers=NT, preferred_element_type=F32)
    return d(a_top, b_top) + (d(a_top, b_low) + d(a_low, b_top))


def tile_inverses(tiles, between=None):
    bp = lax.broadcasted_iota(jnp.int32, (BLOCK, BLOCK), 0)
    bq = lax.broadcasted_iota(jnp.int32, (BLOCK, BLOCK), 1)
    eye = (bp == bq).astype(F32)
    inverse = [eye - jnp.where(bp // 2 == bq // 2, tile, 0.0) for tile in tiles]
    size = 2
    while size < BLOCK:
        joined = (bp // (2 * size) == bq // (2 * size)) & (bp // size != bq // size)
        left = [dot3(inv, jnp.where(joined, tile, 0.0)) for inv, tile in zip(inverse, tiles)]
        inverse = [inv - dot3(lhs, inv) for inv, lhs in zip(inverse, left)]
        if between is not None:
            between(size)
        size *= 2
    return inverse


def fused_kernel(offs_hbm, vectors_hbm, eigen_hbm, panels_hbm, kept, home, offs, vectors, eigen, cut, gathered, packs,
                 inners, wide, tile_of, placed_top, placed_low, outgoing, traded, shared, held, rounded, delta, acc,
                 work, slots, whole, change, load, send_a, recv_a, send_p, recv_p, send_w, recv_w, send_f, recv_f,
                 send_b, recv_b, send_x, recv_x, send_c, recv_c, send_rs, recv_rs, send_ag, recv_ag, send_h, recv_h,
                 own_sem):
    row, cx, cz = lax.axis_index("row"), lax.axis_index("cx"), lax.axis_index("cz")
    n_row = lax.axis_size("row")
    rows, cols = eigen.shape
    every = NX * rows
    tiles_dev = cols // LANE
    part = cut.shape[3]
    chunk = part // CHUNKS
    n_panel = cut.shape[1]
    per_dev = vectors.shape[0]
    half = per_dev // 2
    refl = 4
    spans = half // refl
    per_tile = BLOCK // half
    peers = n_row * NX
    me = row * NX + cx
    owners = work.shape[1]
    mesh = pl.DeviceIdType.MESH
    mxu_nt = functools.partial(lax.dot_general, dimension_numbers=NT, preferred_element_type=F32)
    mxu = functools.partial(lax.dot_general, dimension_numbers=NN, preferred_element_type=F32)

    def device(place):
        return {"row": place // NX, "cx": place % NX}

    loads = [
        pltpu.make_async_copy(offs_hbm, offs, load.at[0]),
        pltpu.make_async_copy(vectors_hbm, vectors, load.at[1]),
        pltpu.make_async_copy(eigen_hbm, eigen, load.at[2]),
    ]
    for x in range(NX):
        size = min(part, cols - x * part)
        loads.append(
            pltpu.make_async_copy(
                panels_hbm.at[:, :, pl.ds(x * part, size)], cut.at[x, :, :, pl.ds(0, size)], load.at[3 + x]
            )
        )
        if size < part:
            cut[x, :, :, size:] = jnp.zeros((n_panel, cut.shape[2], part - size), BF16)
    for copy in loads:
        copy.start()
    barrier = pltpu.get_barrier_semaphore()
    for k in (1, NZ - 1):
        pl.semaphore_signal(barrier, inc=1, device_id={"cz": (cz + k) % NZ}, device_id_type=mesh)
    for k in range(1, peers):
        pl.semaphore_signal(barrier, inc=1, device_id=device((me + k) % peers), device_id_type=mesh)
    for copy in loads:
        copy.wait()

    lane8 = lax.broadcasted_iota(jnp.int32, (8, LANE), 1)
    line8 = lax.broadcasted_iota(jnp.int32, (8, LANE), 0)
    line64 = lax.broadcasted_iota(jnp.int32, (per_dev, LANE), 0) // refl
    meta = jnp.zeros((8, LANE), F32)
    own_tile = jnp.zeros((per_dev, LANE), F32)
    own_shift = jnp.zeros((per_dev, LANE), jnp.int32)
    for s in range(2):
        for b in range(spans):
            at = offs[s, b]
            tile_at = at >> 7
            shift_at = at & 127
            place = (row % per_tile) * half + b * refl
            mine = (lane8 >= place) & (lane8 < place + refl)
            line = s * 2 + row // per_tile
            meta = jnp.where(mine & (line8 == line), (tile_at + row * tiles_dev).astype(F32), meta)
            meta = jnp.where(mine & (line8 == line + 4), shift_at.astype(F32), meta)
            own_tile = jnp.where(line64 == s * spans + b, tile_at.astype(F32), own_tile)
            own_shift = jnp.where(line64 == s * spans + b, shift_at, own_shift)
    packs[row, :per_dev] = vectors[...]
    packs[row, per_dev:] = meta
    for x in range(NX):
        size = min(part, cols - x * part)
        outgoing[x, :, :size] = eigen[:, x * part : x * part + size].astype(BF16)
        if size < part:
            outgoing[x, :, size:] = jnp.zeros((rows, part - size), BF16)

    def over_x(p, j, k):
        at = pl.ds(j * chunk, chunk)
        return pltpu.make_async_remote_copy(
            src_ref=cut.at[(cx + k) % NX, p, :, at],
            dst_ref=gathered.at[p, cx, cz, :, at],
            send_sem=send_a.at[p * CHUNKS + j, k - 1],
            recv_sem=recv_a.at[p * CHUNKS + j, k - 1],
            device_id={"cx": (cx + k) % NX},
            device_id_type=mesh,
        )

    def over_x_arrival(p, j, k):
        at = pl.ds(j * chunk, chunk)
        source = (cx + NX - k) % NX
        return pltpu.make_async_remote_copy(
            src_ref=cut.at[source, p, :, at],
            dst_ref=gathered.at[p, source, cz, :, at],
            send_sem=send_a.at[p * CHUNKS + j, k - 1],
            recv_sem=recv_a.at[p * CHUNKS + j, k - 1],
            device_id={"cx": source},
            device_id_type=mesh,
        )

    def over_row(ref, sends, recvs, k):
        return pltpu.make_async_remote_copy(
            src_ref=ref.at[row],
            dst_ref=ref.at[row],
            send_sem=sends.at[k - 1],
            recv_sem=recvs.at[k - 1],
            device_id={"row": (row + k) % n_row},
            device_id_type=mesh,
        )

    def over_row_arrival(ref, sends, recvs, k):
        source = (row + n_row - k) % n_row
        return pltpu.make_async_remote_copy(
            src_ref=ref.at[source],
            dst_ref=ref.at[source],
            send_sem=sends.at[k - 1],
            recv_sem=recvs.at[k - 1],
            device_id={"row": source},
            device_id_type=mesh,
        )

    def along_x(source_ref, target_ref, sends, recvs, k):
        target = (cx + k) % NX
        return pltpu.make_async_remote_copy(
            src_ref=source_ref.at[target] if source_ref is not target_ref else source_ref.at[cx],
            dst_ref=target_ref.at[cx],
            send_sem=sends.at[k - 1],
            recv_sem=recvs.at[k - 1],
            device_id={"cx": target},
            device_id_type=mesh,
        )

    def along_x_arrival(source_ref, target_ref, sends, recvs, k):
        source = (cx + NX - k) % NX
        return pltpu.make_async_remote_copy(
            src_ref=source_ref.at[source],
            dst_ref=target_ref.at[source],
            send_sem=sends.at[k - 1],
            recv_sem=recvs.at[k - 1],
            device_id={"cx": source},
            device_id_type=mesh,
        )

    last = NZ // 2 - 1

    def ring(p, ahead, d, j, arriving):
        step = 1 if ahead else NZ - 1
        held_at = (cz + (NZ - d)) % NZ if ahead else (cz + d) % NZ
        if arriving:
            held_at = (held_at + (NZ - step)) % NZ
        at = pl.ds(j * chunk, chunk)
        share = slice(None) if d < last else (pl.ds(0, NX // 2) if ahead else pl.ds(NX // 2, NX // 2))
        place = gathered.at[p, share, held_at, :, at]
        unit = ((last + 1) * p + d) * CHUNKS + j
        return pltpu.make_async_remote_copy(
            src_ref=place,
            dst_ref=place,
            send_sem=(send_f if ahead else send_b).at[unit],
            recv_sem=(recv_f if ahead else recv_b).at[unit],
            device_id={"cz": (cz + step) % NZ},
            device_id_type=mesh,
        )

    def launch(p, j):
        for k in (1, 3, 2):
            over_x_arrival(p, j, k).wait_recv()
        for ahead in (True, False):
            ring(p, ahead, 0, j, False).start()

    def reflect(p, at):
        return gathered[p, :, :, :, at].reshape(-1, chunk)

    def product(p, j):
        at = slice(j * chunk, (j + 1) * chunk)
        mine = reflect(p, at)
        value = mxu_nt(jnp.concatenate([rounded[:, at], mine], axis=0), mine)
        acc[...] = value if j == 0 else acc[...] + value

    queue = [(p, d, j) for p in range(n_panel) for d in range(last + 1) for j in range(CHUNKS)]

    def pump(count):
        for _ in range(count):
            p, d, j = queue.pop(0)
            for ahead in (True, False):
                ring(p, ahead, d, j, True).wait_recv()
                if d < last:
                    ring(p, ahead, d + 1, j, False).start()
            if p == 0 and d == last - 1:
                launch(1, j)
            if d == last:
                product(p, j)

    def shifted(values, amount):
        both = jnp.concatenate([values, jnp.zeros_like(values)], axis=1)
        for bit in range(7):
            both = jnp.where(((amount >> bit) & 1) == 1, pltpu.roll(both, 1 << bit, 1), both)
        return both

    own_wide = shifted(vectors[...], jnp.concatenate([own_shift, own_shift], axis=1))
    low_top, low_low = [v.astype(F32) for v in halves(own_wide[:, :LANE])]
    high_top, high_low = [v.astype(F32) for v in halves(own_wide[:, LANE:])]
    group = 7

    def build(step, carry):
        for k in range(group):
            tile = (step * group + k).astype(F32)
            first, second = own_tile == tile, own_tile == tile - 1.0
            at = pl.ds(pl.multiple_of((step * group + k) * LANE, LANE), LANE)
            placed_top[:, at] = jnp.where(first, low_top, jnp.where(second, high_top, 0.0)).astype(BF16)
            placed_low[:, at] = jnp.where(first, low_low, jnp.where(second, high_low, 0.0)).astype(BF16)
        return carry

    lax.fori_loop(0, tiles_dev // group, build, 0)
    placed_top[:, cols:] = jnp.zeros((per_dev, NX * part - cols), BF16)
    placed_low[:, cols:] = jnp.zeros((per_dev, NX * part - cols), BF16)
    own_copy = pltpu.make_async_copy(cut.at[cx], gathered.at[:, cx, cz], own_sem.at[0])
    own_copy.start()
    own_trade = pltpu.make_async_copy(outgoing.at[cx], traded.at[cx], own_sem.at[1])
    own_trade.start()
    own_copy.wait()

    pl.semaphore_wait(barrier, peers - 1 + 2)
    for j in range(CHUNKS):
        for k in (1, 3, 2):
            over_x(0, j, k).start()
    for k in range(1, n_row):
        over_row(packs, send_p, recv_p, k).start()
    for j in range(CHUNKS):
        for k in (1, 3, 2):
            over_x(1, j, k).start()
    for k in (1, 3, 2):
        along_x(outgoing, traded, send_x, recv_x, k).start()
    for j in range(CHUNKS):
        launch(0, j)

    def inner_step(step, total):
        at = pl.ds(pl.multiple_of(step * group * LANE, LANE), group * LANE)
        top, low = halves(eigen[:, at])
        first = mxu_nt(jnp.concatenate([top, low], axis=0), placed_top[:, at])
        return total + first[:rows] + first[rows:] + mxu_nt(top, placed_low[:, at])

    steps = tiles_dev // group
    total = lax.fori_loop(0, steps // 2, inner_step, jnp.zeros((rows, per_dev), F32))
    pump(1)
    total = lax.fori_loop(steps // 2, steps, inner_step, total)
    pump(2)

    for k in range(1, n_row):
        over_row_arrival(packs, send_p, recv_p, k).wait_recv()
    every_meta = packs[0, per_dev:]
    for r in range(1, n_row):
        every_meta = every_meta + packs[r, per_dev:]
    bp = lax.broadcasted_iota(jnp.int32, (BLOCK, BLOCK), 0)
    bq = lax.broadcasted_iota(jnp.int32, (BLOCK, BLOCK), 1)
    diag = bp == bq

    def turned(line):
        return jnp.sum(jnp.where(diag, line, 0.0), axis=1, keepdims=True)

    count = 2 * n_row * half // BLOCK
    across_tile = [every_meta[u : u + 1] for u in range(count)]
    down_tile = []
    for u in range(count):
        s, h = u // 2, u % 2
        low = jnp.concatenate(
            [packs[h * per_tile + k, s * half : (s + 1) * half] for k in range(per_tile)], axis=0
        )
        wide[u * BLOCK : (u + 1) * BLOCK] = shifted(low, turned(every_meta[u + 4 : u + 5]).astype(jnp.int32))
        down = turned(across_tile[u])
        down_tile.append(down)
        tile_of[u * BLOCK : (u + 1) * BLOCK] = jnp.broadcast_to(down, (BLOCK, LANE))
        if u == 1:
            pump(1)

    def of_row(ref, r):
        return jnp.concatenate(
            [ref[pl.ds(pl.multiple_of(s * n_row * half + r * half, half), half)] for s in range(2)], axis=0
        )

    prev_row = jnp.maximum(row - 1, 0)
    prev_tile = of_row(tile_of, prev_row) - (row * tiles_dev).astype(F32)
    prev_high = jnp.where(prev_tile == -1.0, of_row(wide, prev_row)[:, LANE:], 0.0)
    behind = dot3_nt(eigen[:, :LANE], prev_high)
    inners[row] = jnp.concatenate([total, behind], axis=1)
    for k in range(1, n_row):
        over_row(inners, send_w, recv_w, k).start()
    pump(2)

    keep = (((bp // refl) == (bq // refl)) & (bp > bq)) | (((bp // refl) != (bq // refl)) & (bp < bq))
    strict, across = {}, []
    for u in range(count):
        mine = wide[u * BLOCK : (u + 1) * BLOCK]
        rest = wide[u * BLOCK :]
        level = dot3_nt(mine, rest)
        after = dot3_nt(mine[:, LANE:], rest[:, :LANE])
        before = dot3_nt(mine[:, :LANE], rest[:, LANE:])
        for t in range(u, count):
            cols_at = slice((t - u) * BLOCK, (t - u + 1) * BLOCK)
            gap = across_tile[t] - down_tile[u]
            tile = jnp.where(
                gap == 0.0,
                level[:, cols_at],
                jnp.where(gap == 1.0, after[:, cols_at], jnp.where(gap == -1.0, before[:, cols_at], 0.0)),
            )
            if t == u:
                picked = jnp.where(diag, tile, 0.0)
                scale = 2.0 / jnp.sum(picked, axis=1, keepdims=True)
                across.append(2.0 / jnp.sum(picked, axis=0, keepdims=True))
                tile = jnp.where(keep, tile, 0.0)
            strict[u, t] = tile * scale
        if u in (0, 2):
            pump(1)
    inverse = tile_inverses([strict[t, t] for t in range(count)], lambda size: pump(1) if size == 8 else None)
    pump(2)

    for k in range(1, n_row):
        over_row_arrival(inners, send_w, recv_w, k).wait_recv()
    lane = lax.broadcasted_iota(jnp.int32, (rows, LANE), 1) // half
    right = [jnp.zeros((rows, LANE), F32) for _ in range(count)]
    for r in range(n_row):
        values = inners[r]
        for s in range(2):
            u = s * 2 + r // per_tile
            moved = pltpu.roll(values, (half * (r % per_tile) - half * s) % LANE, 1)
            right[u] = right[u] + jnp.where(lane == r % per_tile, moved, 0.0)
            if r > 0:
                u = s * 2 + (r - 1) // per_tile
                moved = pltpu.roll(values, (half * ((r - 1) % per_tile) - per_dev - half * s) % LANE, 1)
                right[u] = right[u] + jnp.where(lane == (r - 1) % per_tile, moved, 0.0)
    found = []
    for t in range(count):
        value = right[t]
        for u in range(t):
            value = value - dot3(found[u], strict[u, t])
        found.append(dot3(value, inverse[t]))
    solved = [found[t] * across[t] for t in range(count)]

    def coeffs_of(r):
        result = jnp.zeros((rows, LANE), F32)
        for s in range(2):
            tile = jnp.where(r // per_tile == 0, solved[s * 2], solved[s * 2 + 1])
            moved = pltpu.roll(tile, (LANE - half * (r % per_tile) + half * s) % LANE, 1)
            result = jnp.where(lane == s, moved, result)
        return result[:, :per_dev]

    own_coeffs, prev_coeffs = coeffs_of(row), coeffs_of(prev_row)
    shared[cx] = jnp.concatenate([own_coeffs, prev_coeffs], axis=1)
    for k in (1, 3, 2):
        along_x(shared, shared, send_c, recv_c, k).start()
    pump(2)

    def both_halves(values):
        top, low = halves(values)
        return top, jnp.concatenate([top, low], axis=0)

    def changed(top, both, at):
        size = top.shape[0]
        first = mxu(both, placed_top[:, at])
        return first[:size] + first[size:] + mxu(top, placed_low[:, at])

    coeffs_top, coeffs_both = both_halves(own_coeffs)
    first_change = dot3(prev_coeffs, prev_high)

    def keep_step(step, carry):
        at = pl.ds(pl.multiple_of(step * group * LANE, LANE), group * LANE)
        kept[:, at] = eigen[:, at] - changed(coeffs_top, coeffs_both, at)
        return carry

    lax.fori_loop(0, steps // 4, keep_step, 0)
    pump(1)
    kept[:, :LANE] = kept[:, :LANE] - first_change

    own_trade.wait()
    for k in (1, 3, 2):
        along_x_arrival(outgoing, traded, send_x, recv_x, k).wait_recv()
    for k in (1, 3, 2):
        along_x_arrival(shared, shared, send_c, recv_c, k).wait_recv()
    all_shared = shared[...].reshape(every, LANE)
    slice_top, slice_both = both_halves(all_shared[:, :per_dev])
    begin_change = jnp.where(cx == 0, 1.0, 0.0).astype(F32) * dot3(all_shared[:, per_dev:], prev_high)
    for j in range(CHUNKS):
        at = slice(j * chunk, (j + 1) * chunk)
        source = pl.ds(pl.multiple_of(cx * part + j * chunk, LANE), chunk)
        value = traded[:, :, at].reshape(every, chunk).astype(F32) - changed(slice_top, slice_both, source)
        if j == 0:
            value = jnp.concatenate([value[:, :LANE] - begin_change, value[:, LANE:]], axis=1)
        held[:, at] = value
        rounded[:, at] = value.astype(BF16)
        if j == 1:
            pump(1)
    pump(CHUNKS)

    piece = work.shape[2]
    per_block = BLOCK // piece

    def piece_of(place):
        return jnp.minimum((place * 5 + 7) // 8, owners - 1)

    def owns(place):
        return (((place * 5 + 7) // 8) * 8) // 5 == place

    def put(p):
        blocks = (
            acc[every : every + BLOCK, :BLOCK],
            acc[every + BLOCK :, :BLOCK],
            acc[every + BLOCK :, BLOCK:],
            acc[:every, :BLOCK],
            acc[:every, BLOCK:],
        )
        for place, block in enumerate(blocks):
            value = block.astype(BF16)
            for k in range(per_block):
                work[p, place * per_block + k] = value[k * piece : (k + 1) * piece]

    def scatter(p, k):
        target = (me + k) % peers
        return pltpu.make_async_remote_copy(
            src_ref=work.at[p, piece_of(target)],
            dst_ref=slots.at[p, k - 1],
            send_sem=send_rs.at[p, k - 1],
            recv_sem=recv_rs.at[p, k - 1],
            device_id=device(target),
            device_id_type=mesh,
        )

    def gather(p, k, arriving):
        place = piece_of((me + peers - k) % peers if arriving else me)
        return pltpu.make_async_remote_copy(
            src_ref=whole.at[p, place],
            dst_ref=whole.at[p, place],
            send_sem=send_ag.at[p, k - 1],
            recv_sem=recv_ag.at[p, k - 1],
            device_id=device((me + k) % peers),
            device_id_type=mesh,
        )

    def start_reduce(p):
        put(p)
        for k in range(1, peers):
            pl.when(owns((me + k) % peers))(scatter(p, k).start)

    def finish_reduce(p):
        @pl.when(owns(me))
        def _():
            value = work[p, piece_of(me)].astype(F32)
            for k in range(1, peers):
                scatter(p, k).wait_recv()
                value = value + slots[p, k - 1].astype(F32)
            whole[p, piece_of(me)] = value.astype(BF16)
            for k in range(1, peers):
                gather(p, k, False).start()

    def finish_gather(p):
        for k in range(1, peers):
            pl.when(owns((me + peers - k) % peers))(gather(p, k, True).wait_recv)

    def panel_solve(p, between):
        def got(place):
            return jnp.concatenate(
                [whole[p, place * per_block + k].astype(F32) for k in range(per_block)], axis=0
            )

        gram = {(0, 0): got(0), (1, 0): got(1), (1, 1): got(2)}
        picked = [jnp.where(diag, gram[t, t], 0.0) for t in range(2)]
        down = [2.0 / jnp.sum(v, axis=1, keepdims=True) for v in picked]
        beside = [2.0 / jnp.sum(v, axis=0, keepdims=True) for v in picked]
        below = [jnp.where(bp > bq, gram[t, t] * down[t], 0.0) for t in range(2)]
        inverses = tile_inverses(below, between)
        second = dot3(got(4), inverses[1])
        first = dot3(got(3) - dot3(second, gram[1, 0] * down[1]), inverses[0])
        return jnp.concatenate([(first * beside[0]).astype(BF16), (second * beside[1]).astype(BF16)], axis=1)

    start_reduce(0)
    pump(1)
    lax.fori_loop(steps // 4, steps // 2, keep_step, 0)
    pump(1)
    lax.fori_loop(steps // 2, 3 * steps // 4, keep_step, 0)
    pump(1)
    finish_reduce(0)
    pump(1)
    lax.fori_loop(3 * steps // 4, steps, keep_step, 0)
    pump(3)
    finish_gather(0)
    coeffs = panel_solve(0, lambda size: pump(1) if size in (4, 32) else None)
    pump(1)
    for j in range(CHUNKS):
        at = slice(j * chunk, (j + 1) * chunk)
        value = mxu(coeffs, reflect(0, at))
        delta[:, at] = value
        rounded[:, at] = (held[:, at] - value).astype(BF16)
        if j in (1, 3):
            pump(1)
    pump(len(queue))
    start_reduce(1)
    finish_reduce(1)
    finish_gather(1)
    coeffs = panel_solve(1, None)

    def back(j, k, arriving):
        source = (cx + NX - k) % NX if arriving else (cx + k) % NX
        at = pl.ds(j * chunk, chunk)
        return pltpu.make_async_remote_copy(
            src_ref=change.at[source, :, at],
            dst_ref=home.at[source if arriving else cx, :, at],
            send_sem=send_h.at[j, k - 1],
            recv_sem=recv_h.at[j, k - 1],
            device_id={"cx": source},
            device_id_type=mesh,
        )

    for j in range(CHUNKS):
        at = slice(j * chunk, (j + 1) * chunk)
        value = (delta[:, at] + mxu(coeffs, reflect(1, at))).astype(BF16)
        for x in range(NX):
            change[x, :, at] = value[x * rows : (x + 1) * rows]
        for k in (2, 1, 3):
            back(j, k, False).start()
    keep_home = pltpu.make_async_copy(change.at[cx], home.at[cx], own_sem.at[0])
    keep_home.start()

    for k in range(1, n_row):
        over_row(packs, send_p, recv_p, k).wait_send()
        over_row(inners, send_w, recv_w, k).wait_send()
    for k in range(1, NX):
        along_x(outgoing, traded, send_x, recv_x, k).wait_send()
        along_x(shared, shared, send_c, recv_c, k).wait_send()
        for p in range(n_panel):
            for j in range(CHUNKS):
                over_x(p, j, k).wait_send()
    for p in range(n_panel):
        for d in range(last + 1):
            for j in range(CHUNKS):
                for ahead in (True, False):
                    ring(p, ahead, d, j, False).wait_send()
        for k in range(1, peers):
            pl.when(owns((me + k) % peers))(scatter(p, k).wait_send)

        @pl.when(owns(me))
        def _():
            for k in range(1, peers):
                gather(p, k, False).wait_send()

    keep_home.wait()
    for j in range(CHUNKS):
        for k in range(1, NX):
            back(j, k, False).wait_send()
            back(j, k, True).wait_recv()


def fused_step(offs, vectors, eigen, panels, n_row):
    rows, cols = eigen.shape
    n_panel, refl_dev, _ = panels.shape
    part = -(-(cols // LANE) // NX) * LANE
    per_dev, band = vectors.shape
    peers = n_row * NX
    owners, piece = 20, 32
    every = NX * rows
    dma = pltpu.SemaphoreType.DMA
    vmem = pl.BlockSpec(memory_space=pltpu.VMEM)
    hbm = pl.BlockSpec(memory_space=pltpu.HBM)
    units = n_panel * (NZ // 2) * CHUNKS
    trade = (NX, rows, part)
    return pl.pallas_call(
        fused_kernel,
        out_shape=[jax.ShapeDtypeStruct((rows, cols), F32), jax.ShapeDtypeStruct(trade, BF16)],
        in_specs=[hbm] * 4,
        out_specs=[vmem] * 2,
        scratch_shapes=[
            pltpu.SMEM(offs.shape, jnp.int32),
            pltpu.VMEM((per_dev, band), F32),
            pltpu.VMEM((rows, cols), F32),
            pltpu.VMEM((NX, n_panel, refl_dev, part), BF16),
            pltpu.VMEM((n_panel, NX, NZ, refl_dev, part), BF16),
            pltpu.VMEM((n_row, per_dev + 8, band), F32),
            pltpu.VMEM((n_row, rows, LANE), F32),
            pltpu.VMEM((n_row * per_dev, 2 * LANE), F32),
            pltpu.VMEM((n_row * per_dev, LANE), F32),
            pltpu.VMEM((per_dev, NX * part), BF16),
            pltpu.VMEM((per_dev, NX * part), BF16),
            pltpu.VMEM(trade, BF16),
            pltpu.VMEM(trade, BF16),
            pltpu.VMEM((NX, rows, LANE), F32),
            pltpu.VMEM((every, part), F32),
            pltpu.VMEM((every, part), BF16),
            pltpu.VMEM((every, part), F32),
            pltpu.VMEM((every + 2 * BLOCK, 2 * BLOCK), F32),
            pltpu.VMEM((n_panel, owners, piece, BLOCK), BF16),
            pltpu.VMEM((n_panel, peers - 1, piece, BLOCK), BF16),
            pltpu.VMEM((n_panel, owners, piece, BLOCK), BF16),
            pltpu.VMEM(trade, BF16),
            dma((3 + NX,)),
            dma((n_panel * CHUNKS, NX - 1)),
            dma((n_panel * CHUNKS, NX - 1)),
            dma((n_row - 1,)),
            dma((n_row - 1,)),
            dma((n_row - 1,)),
            dma((n_row - 1,)),
            dma((units,)),
            dma((units,)),
            dma((units,)),
            dma((units,)),
            dma((NX - 1,)),
            dma((NX - 1,)),
            dma((NX - 1,)),
            dma((NX - 1,)),
            dma((n_panel, peers - 1)),
            dma((n_panel, peers - 1)),
            dma((n_panel, peers - 1)),
            dma((n_panel, peers - 1)),
            dma((CHUNKS, NX - 1)),
            dma((CHUNKS, NX - 1)),
            dma((2,)),
        ],
        compiler_params=pltpu.CompilerParams(
            collective_id=0, has_side_effects=True, vmem_limit_bytes=40 * 1024 * 1024
        ),
        cost_estimate=pl.CostEstimate(flops=20_000_000_000, bytes_accessed=8_000_000, transcendentals=0),
    )(offs, vectors, eigen, panels)


def local(eigvecs, span_vectors, span_offsets, panels):
    rows, cols = eigvecs.shape
    band = span_vectors.shape[3]
    n_row = lax.psum(1, "row")
    eigen, home = fused_step(span_offsets, span_vectors.reshape(-1, band), eigvecs, panels, n_row)
    home = home.transpose(1, 0, 2).reshape(rows, -1)[:, :cols]
    return eigen - home.astype(F32)


def solution(mesh):
    finer = Mesh(mesh.devices.reshape(mesh.shape["row"], NX, NZ), ("row", "cx", "cz"))
    col = ("cx", "cz")
    placed = (P(col, "row"), P(None, "row", None, None), P(None, "row"), P(None, col, "row"))
    return jax.shard_map(local, mesh=finer, in_specs=placed, out_specs=P(col, "row"), check_vma=False)
```

time: 87.6 us -> 93.9 us (1.072)
  Pallas kernels: 82.2 us -> 88.4 us
    pallas_call x1, Pallas kernels: 82.2 us -> 88.4 us  [fused_step(): pl.pallas_call(fused_kernel, out_shape=[jax.ShapeDtypeStruct((rows, cols)...]
where the time goes in v5:
time: 93.9 us; the launch traced here: 93.6 us
  Pallas kernels  88.4 us (94%)
  local copies, waits for them, and re-layouts  3.91 us (4%)
  other arithmetic  1.29 us (1%)
    pallas_call x1, Pallas kernels, fused_step(): pl.pallas_call(fused_kernel, out_shape=[jax.ShapeDtypeStruct((rows, cols)...  88.4 us
    unnamed x8, local copies, waits for them, and re-layouts  3.85 us

profile of v5, /device:TPU:1, one launch (start us, length us, event | category | flops | bytes accessed | tf_op | source)
XLA Modules:
  0.0 93.6 jit_solution(12347985097664072043)
XLA Ops:
  0.0 0.0 copy-start
  0.0 1.4 %copy-done = f32[32,12544]{1,0:T(8,128)S(1)} copy-done((f32[32,12544]{1,0:T(8,128)S(1)}, f32[32,12544]{1,0:T(8,128)}, u32[]{:S(2)}) %copy-start) | copy-done | bytes 1605656
  1.4 0.0 copy-start.1
  1.4 1.0 %copy-done.1 = bf16[2,8,12544]{2,1,0:T(8,128)(2,1)S(1)} copy-done((bf16[2,8,12544]{2,1,0:T(8,128)(2,1)S(1)}, bf16[2,8,12544]{2,1,0:T(8,128)(2,1)}, u32[]{:S(2)}) %copy-start.1) | copy-done | bytes 401432
  2.4 0.0 copy-start.2
  2.4 0.8 copy-done.2
  3.2 0.0 copy-start.3
  3.2 0.7 copy-done.3
  3.9 88.4 %shard_map.46 = (f32[32,12544]{1,0:T(8,128)S(1)}, bf16[4,32,3200]{2,1,0:T(8,128)(2,1)S(1)}) custom-call(s32[2,8]{1,0:T(2,128)S(1)} %copy-done.3, f32[64,128]{1,0:T(8,128)S(1)} %bitcast.5, f32[32,12544]{1,0:T(8,128)S(1)} %copy-done, bf16[2,8,12544]{2,1,0:T(8,128)(2,1)S(1)} %copy-done.1), custom_call_target="tpu_custom_call" | custom-call | flops 20000000000 | bytes 8000000 | tf_op jit(solution)/shard_map/pallas_call | solution.py:620
  92.3 0.1 copy.6
  92.3 1.3 %convert_subtract_fusion = f32[32,12544]{1,0:T(8,128)} fusion(f32[32,12544]{1,0:T(8,128)S(1)} %get-tuple-element.7, bf16[32,12800]{1,0:T(8,128)(2,1)S(1)} %bitcast.6), kind=kLoop, calls=%fused_computation | loop fusion | flops 802816 | bytes 4014080 | tf_op jit(solution)/shard_map/sub | solution.py:684
Async XLA Ops:
  0.0 1.4 %copy-start = (f32[32,12544]{1,0:T(8,128)S(1)}, f32[32,12544]{1,0:T(8,128)}, u32[]{:S(2)}) copy-start(f32[32,12544]{1,0:T(8,128)} %eigen_hbm.1) | copy-start | bytes 4816900
  1.4 1.0 %copy-start.1 = (bf16[2,8,12544]{2,1,0:T(8,128)(2,1)S(1)}, bf16[2,8,12544]{2,1,0:T(8,128)(2,1)}, u32[]{:S(2)}) copy-start(bf16[2,8,12544]{2,1,0:T(8,128)(2,1)} %panels_hbm.1) | copy-start | bytes 1204228
  2.4 0.8 copy-start.2
  3.2 0.7 copy-start.3

commit v6 on v5

--- a/solution.py
+++ b/solution.py
@@ -54,10 +54,10 @@
     return inverse
 
 
-def fused_kernel(offs_hbm, vectors_hbm, eigen_hbm, panels_hbm, kept, home, offs, vectors, eigen, cut, gathered, packs,
+def fused_kernel(offs_hbm, vectors_hbm, eigen_hbm, panels_hbm, kept_hbm, home, kept, offs, vectors, eigen, cut, gathered, packs,
                  inners, wide, tile_of, placed_top, placed_low, outgoing, traded, shared, held, rounded, delta, acc,
                  work, slots, whole, change, load, send_a, recv_a, send_p, recv_p, send_w, recv_w, send_f, recv_f,
-                 send_b, recv_b, send_x, recv_x, send_c, recv_c, send_rs, recv_rs, send_ag, recv_ag, send_h, recv_h,
+                 send_x, recv_x, send_c, recv_c, send_rs, recv_rs, send_ag, recv_ag, send_h, recv_h,
                  own_sem):
     row, cx, cz = lax.axis_index("row"), lax.axis_index("cx"), lax.axis_index("cz")
     n_row = lax.axis_size("row")
@@ -85,8 +85,8 @@
     loads = [
         pltpu.make_async_copy(offs_hbm, offs, load.at[0]),
         pltpu.make_async_copy(vectors_hbm, vectors, load.at[1]),
-        pltpu.make_async_copy(eigen_hbm, eigen, load.at[2]),
     ]
+    eigen_load = pltpu.make_async_copy(eigen_hbm, eigen, load.at[2])
     for x in range(NX):
         size = min(part, cols - x * part)
         loads.append(
@@ -98,6 +98,7 @@
             cut[x, :, :, size:] = jnp.zeros((n_panel, cut.shape[2], part - size), BF16)
     for copy in loads:
         copy.start()
+    eigen_load.start()
     barrier = pltpu.get_barrier_semaphore()
     for k in (1, NZ - 1):
         pl.semaphore_signal(barrier, inc=1, device_id={"cz": (cz + k) % NZ}, device_id_type=mesh)
@@ -126,103 +127,64 @@
             own_shift = jnp.where(line64 == s * spans + b, shift_at, own_shift)
     packs[row, :per_dev] = vectors[...]
     packs[row, per_dev:] = meta
-    for x in range(NX):
-        size = min(part, cols - x * part)
-        outgoing[x, :, :size] = eigen[:, x * part : x * part + size].astype(BF16)
-        if size < part:
-            outgoing[x, :, size:] = jnp.zeros((rows, part - size), BF16)
+    def sized(ref, send, recv):
+        return pltpu.make_async_remote_copy(
+            src_ref=ref, dst_ref=ref, send_sem=send, recv_sem=recv, device_id={"cx": (cx + 1) % NX}, device_id_type=mesh
+        )
 
     def over_x(p, j, k):
         at = pl.ds(j * chunk, chunk)
         return pltpu.make_async_remote_copy(
             src_ref=cut.at[(cx + k) % NX, p, :, at],
             dst_ref=gathered.at[p, cx, cz, :, at],
-            send_sem=send_a.at[p * CHUNKS + j, k - 1],
-            recv_sem=recv_a.at[p * CHUNKS + j, k - 1],
+            send_sem=send_a.at[0],
+            recv_sem=recv_a.at[p * CHUNKS + j],
             device_id={"cx": (cx + k) % NX},
             device_id_type=mesh,
         )
 
-    def over_x_arrival(p, j, k):
-        at = pl.ds(j * chunk, chunk)
-        source = (cx + NX - k) % NX
-        return pltpu.make_async_remote_copy(
-            src_ref=cut.at[source, p, :, at],
-            dst_ref=gathered.at[p, source, cz, :, at],
-            send_sem=send_a.at[p * CHUNKS + j, k - 1],
-            recv_sem=recv_a.at[p * CHUNKS + j, k - 1],
-            device_id={"cx": source},
-            device_id_type=mesh,
-        )
-
     def over_row(ref, sends, recvs, k):
         return pltpu.make_async_remote_copy(
             src_ref=ref.at[row],
             dst_ref=ref.at[row],
-            send_sem=sends.at[k - 1],
-            recv_sem=recvs.at[k - 1],
+            send_sem=sends.at[0],
+            recv_sem=recvs.at[0],
             device_id={"row": (row + k) % n_row},
             device_id_type=mesh,
         )
 
-    def over_row_arrival(ref, sends, recvs, k):
-        source = (row + n_row - k) % n_row
-        return pltpu.make_async_remote_copy(
-            src_ref=ref.at[source],
-            dst_ref=ref.at[source],
-            send_sem=sends.at[k - 1],
-            recv_sem=recvs.at[k - 1],
-            device_id={"row": source},
-            device_id_type=mesh,
-        )
-
     def along_x(source_ref, target_ref, sends, recvs, k):
         target = (cx + k) % NX
         return pltpu.make_async_remote_copy(
             src_ref=source_ref.at[target] if source_ref is not target_ref else source_ref.at[cx],
             dst_ref=target_ref.at[cx],
-            send_sem=sends.at[k - 1],
-            recv_sem=recvs.at[k - 1],
+            send_sem=sends.at[0],
+            recv_sem=recvs.at[0],
             device_id={"cx": target},
             device_id_type=mesh,
         )
 
-    def along_x_arrival(source_ref, target_ref, sends, recvs, k):
-        source = (cx + NX - k) % NX
-        return pltpu.make_async_remote_copy(
-            src_ref=source_ref.at[source],
-            dst_ref=target_ref.at[source],
-            send_sem=sends.at[k - 1],
-            recv_sem=recvs.at[k - 1],
-            device_id={"cx": source},
-            device_id_type=mesh,
-        )
-
     last = NZ // 2 - 1
 
-    def ring(p, ahead, d, j, arriving):
+    def ring(p, ahead, d, j):
         step = 1 if ahead else NZ - 1
-        held_at = (cz + (NZ - d)) % NZ if ahead else (cz + d) % NZ
-        if arriving:
-            held_at = (held_at + (NZ - step)) % NZ
         at = pl.ds(j * chunk, chunk)
         share = slice(None) if d < last else (pl.ds(0, NX // 2) if ahead else pl.ds(NX // 2, NX // 2))
-        place = gathered.at[p, share, held_at, :, at]
-        unit = ((last + 1) * p + d) * CHUNKS + j
+        place = gathered.at[p, share, (cz + NZ - d * step) % NZ if ahead else (cz + d) % NZ, :, at]
         return pltpu.make_async_remote_copy(
             src_ref=place,
             dst_ref=place,
-            send_sem=(send_f if ahead else send_b).at[unit],
-            recv_sem=(recv_f if ahead else recv_b).at[unit],
+            send_sem=send_f.at[0],
+            recv_sem=recv_f.at[((last + 1) * p + d) * CHUNKS + j],
             device_id={"cz": (cz + step) % NZ},
             device_id_type=mesh,
         )
 
     def launch(p, j):
-        for k in (1, 3, 2):
-            over_x_arrival(p, j, k).wait_recv()
+        at = pl.ds(j * chunk, chunk)
+        sized(gathered.at[p, pl.ds(0, NX - 1), cz, :, at], send_a.at[0], recv_a.at[p * CHUNKS + j]).wait_recv()
         for ahead in (True, False):
-            ring(p, ahead, 0, j, False).start()
+            ring(p, ahead, 0, j).start()
 
     def reflect(p, at):
         return gathered[p, :, :, :, at].reshape(-1, chunk)
@@ -238,10 +200,12 @@
     def pump(count):
         for _ in range(count):
             p, d, j = queue.pop(0)
-            for ahead in (True, False):
-                ring(p, ahead, d, j, True).wait_recv()
-                if d < last:
-                    ring(p, ahead, d + 1, j, False).start()
+            at = pl.ds(j * chunk, chunk)
+            both = gathered.at[p, :, pl.ds(0, 2 if d < last else 1), :, at]
+            sized(both, send_f.at[0], recv_f.at[((last + 1) * p + d) * CHUNKS + j]).wait_recv()
+            if d < last:
+                for ahead in (True, False):
+                    ring(p, ahead, d + 1, j).start()
             if p == 0 and d == last - 1:
                 launch(1, j)
             if d == last:
@@ -272,8 +236,6 @@
     placed_low[:, cols:] = jnp.zeros((per_dev, NX * part - cols), BF16)
     own_copy = pltpu.make_async_copy(cut.at[cx], gathered.at[:, cx, cz], own_sem.at[0])
     own_copy.start()
-    own_trade = pltpu.make_async_copy(outgoing.at[cx], traded.at[cx], own_sem.at[1])
-    own_trade.start()
     own_copy.wait()
 
     pl.semaphore_wait(barrier, peers - 1 + 2)
@@ -282,13 +244,22 @@
             over_x(0, j, k).start()
     for k in range(1, n_row):
         over_row(packs, send_p, recv_p, k).start()
-    for j in range(CHUNKS):
-        for k in (1, 3, 2):
-            over_x(1, j, k).start()
+    eigen_load.wait()
+    for x in range(NX):
+        size = min(part, cols - x * part)
+        outgoing[x, :, :size] = eigen[:, x * part : x * part + size].astype(BF16)
+        if size < part:
+            outgoing[x, :, size:] = jnp.zeros((rows, part - size), BF16)
+
+    own_trade = pltpu.make_async_copy(outgoing.at[cx], traded.at[cx], own_sem.at[1])
+    own_trade.start()
     for k in (1, 3, 2):
         along_x(outgoing, traded, send_x, recv_x, k).start()
     for j in range(CHUNKS):
         launch(0, j)
+    for j in range(CHUNKS):
+        for k in (1, 3, 2):
+            over_x(1, j, k).start()
 
     def inner_step(step, total):
         at = pl.ds(pl.multiple_of(step * group * LANE, LANE), group * LANE)
@@ -300,10 +271,9 @@
     total = lax.fori_loop(0, steps // 2, inner_step, jnp.zeros((rows, per_dev), F32))
     pump(1)
     total = lax.fori_loop(steps // 2, steps, inner_step, total)
-    pump(2)
-
-    for k in range(1, n_row):
-        over_row_arrival(packs, send_p, recv_p, k).wait_recv()
+    pump(3)
+
+    sized(packs.at[pl.ds(0, n_row - 1)], send_p.at[0], recv_p.at[0]).wait_recv()
     every_meta = packs[0, per_dev:]
     for r in range(1, n_row):
         every_meta = every_meta + packs[r, per_dev:]
@@ -370,8 +340,7 @@
     inverse = tile_inverses([strict[t, t] for t in range(count)], lambda size: pump(1) if size == 8 else None)
     pump(2)
 
-    for k in range(1, n_row):
-        over_row_arrival(inners, send_w, recv_w, k).wait_recv()
+    sized(inners.at[pl.ds(0, n_row - 1)], send_w.at[0], recv_w.at[0]).wait_recv()
     lane = lax.broadcasted_iota(jnp.int32, (rows, LANE), 1) // half
     right = [jnp.zeros((rows, LANE), F32) for _ in range(count)]
     for r in range(n_row):
@@ -404,7 +373,7 @@
     shared[cx] = jnp.concatenate([own_coeffs, prev_coeffs], axis=1)
     for k in (1, 3, 2):
         along_x(shared, shared, send_c, recv_c, k).start()
-    pump(2)
+    pump(1)
 
     def both_halves(values):
         top, low = halves(values)
@@ -428,10 +397,8 @@
     kept[:, :LANE] = kept[:, :LANE] - first_change
 
     own_trade.wait()
-    for k in (1, 3, 2):
-        along_x_arrival(outgoing, traded, send_x, recv_x, k).wait_recv()
-    for k in (1, 3, 2):
-        along_x_arrival(shared, shared, send_c, recv_c, k).wait_recv()
+    sized(traded.at[pl.ds(0, NX - 1)], send_x.at[0], recv_x.at[0]).wait_recv()
+    sized(shared.at[pl.ds(0, NX - 1)], send_c.at[0], recv_c.at[0]).wait_recv()
     all_shared = shared[...].reshape(every, LANE)
     slice_top, slice_both = both_halves(all_shared[:, :per_dev])
     begin_change = jnp.where(cx == 0, 1.0, 0.0).astype(F32) * dot3(all_shared[:, per_dev:], prev_high)
@@ -443,7 +410,7 @@
             value = jnp.concatenate([value[:, :LANE] - begin_change, value[:, LANE:]], axis=1)
         held[:, at] = value
         rounded[:, at] = value.astype(BF16)
-        if j == 1:
+        if j == 2:
             pump(1)
     pump(CHUNKS)
 
@@ -474,19 +441,19 @@
         return pltpu.make_async_remote_copy(
             src_ref=work.at[p, piece_of(target)],
             dst_ref=slots.at[p, k - 1],
-            send_sem=send_rs.at[p, k - 1],
-            recv_sem=recv_rs.at[p, k - 1],
+            send_sem=send_rs.at[p],
+            recv_sem=recv_rs.at[p],
             device_id=device(target),
             device_id_type=mesh,
         )
 
-    def gather(p, k, arriving):
-        place = piece_of((me + peers - k) % peers if arriving else me)
+    def gather(p, k):
+        place = piece_of(me)
         return pltpu.make_async_remote_copy(
             src_ref=whole.at[p, place],
             dst_ref=whole.at[p, place],
-            send_sem=send_ag.at[p, k - 1],
-            recv_sem=recv_ag.at[p, k - 1],
+            send_sem=send_ag.at[p],
+            recv_sem=recv_ag.at[p],
             device_id=device((me + k) % peers),
             device_id_type=mesh,
         )
@@ -499,17 +466,17 @@
     def finish_reduce(p):
         @pl.when(owns(me))
         def _():
+            sized(slots.at[p], send_rs.at[p], recv_rs.at[p]).wait_recv()
             value = work[p, piece_of(me)].astype(F32)
             for k in range(1, peers):
-                scatter(p, k).wait_recv()
                 value = value + slots[p, k - 1].astype(F32)
             whole[p, piece_of(me)] = value.astype(BF16)
             for k in range(1, peers):
-                gather(p, k, False).start()
+                gather(p, k).start()
 
     def finish_gather(p):
-        for k in range(1, peers):
-            pl.when(owns((me + peers - k) % peers))(gather(p, k, True).wait_recv)
+        pl.when(owns(me))(sized(whole.at[p, pl.ds(0, owners - 1)], send_ag.at[p], recv_ag.at[p]).wait_recv)
+        pl.when(jnp.logical_not(owns(me)))(sized(whole.at[p], send_ag.at[p], recv_ag.at[p]).wait_recv)
 
     def panel_solve(p, between):
         def got(place):
@@ -528,40 +495,37 @@
         return jnp.concatenate([(first * beside[0]).astype(BF16), (second * beside[1]).astype(BF16)], axis=1)
 
     start_reduce(0)
-    pump(1)
     lax.fori_loop(steps // 4, steps // 2, keep_step, 0)
-    pump(1)
+    pump(2)
     lax.fori_loop(steps // 2, 3 * steps // 4, keep_step, 0)
     pump(1)
+    lax.fori_loop(3 * steps // 4, steps, keep_step, 0)
+    kept_copy = pltpu.make_async_copy(kept, kept_hbm, load.at[2])
+    kept_copy.start()
+    pump(4)
     finish_reduce(0)
-    pump(1)
-    lax.fori_loop(3 * steps // 4, steps, keep_step, 0)
-    pump(3)
+    pump(5)
     finish_gather(0)
-    coeffs = panel_solve(0, lambda size: pump(1) if size in (4, 32) else None)
-    pump(1)
+    coeffs = panel_solve(0, lambda size: pump(1) if size in (2, 8, 32) else None)
     for j in range(CHUNKS):
         at = slice(j * chunk, (j + 1) * chunk)
         value = mxu(coeffs, reflect(0, at))
         delta[:, at] = value
         rounded[:, at] = (held[:, at] - value).astype(BF16)
-        if j in (1, 3):
-            pump(1)
     pump(len(queue))
     start_reduce(1)
     finish_reduce(1)
     finish_gather(1)
     coeffs = panel_solve(1, None)
 
-    def back(j, k, arriving):
-        source = (cx + NX - k) % NX if arriving else (cx + k) % NX
-        at = pl.ds(j * chunk, chunk)
-        return pltpu.make_async_remote_copy(
-            src_ref=change.at[source, :, at],
-            dst_ref=home.at[source if arriving else cx, :, at],
-            send_sem=send_h.at[j, k - 1],
-            recv_sem=recv_h.at[j, k - 1],
-            device_id={"cx": source},
+    def back(j, k):
+        target = (cx + k) % NX
+        return pltpu.make_async_remote_copy(
+            src_ref=change.at[target, :, pl.ds(j * chunk, chunk)],
+            dst_ref=home.at[:, pl.ds(pl.multiple_of(cx * part + j * chunk, LANE), chunk)],
+            send_sem=send_h.at[0],
+            recv_sem=recv_h.at[0],
+            device_id={"cx": target},
             device_id_type=mesh,
         )
 
@@ -571,37 +535,27 @@
         for x in range(NX):
             change[x, :, at] = value[x * rows : (x + 1) * rows]
         for k in (2, 1, 3):
-            back(j, k, False).start()
-    keep_home = pltpu.make_async_copy(change.at[cx], home.at[cx], own_sem.at[0])
+            back(j, k).start()
+    keep_home = pltpu.make_async_copy(
+        change.at[cx], home.at[:, pl.ds(pl.multiple_of(cx * part, LANE), part)], own_sem.at[0]
+    )
     keep_home.start()
 
-    for k in range(1, n_row):
-        over_row(packs, send_p, recv_p, k).wait_send()
-        over_row(inners, send_w, recv_w, k).wait_send()
-    for k in range(1, NX):
-        along_x(outgoing, traded, send_x, recv_x, k).wait_send()
-        along_x(shared, shared, send_c, recv_c, k).wait_send()
-        for p in range(n_panel):
-            for j in range(CHUNKS):
-                over_x(p, j, k).wait_send()
+    sized(packs.at[pl.ds(0, n_row - 1)], send_p.at[0], recv_p.at[0]).wait_send()
+    sized(inners.at[pl.ds(0, n_row - 1)], send_w.at[0], recv_w.at[0]).wait_send()
+    sized(outgoing.at[pl.ds(0, NX - 1)], send_x.at[0], recv_x.at[0]).wait_send()
+    sized(shared.at[pl.ds(0, NX - 1)], send_c.at[0], recv_c.at[0]).wait_send()
+    sized(cut.at[pl.ds(0, NX - 1)], send_a.at[0], recv_a.at[0]).wait_send()
+    sized(gathered.at[:, :, pl.ds(0, NZ - 1)], send_f.at[0], recv_f.at[0]).wait_send()
     for p in range(n_panel):
-        for d in range(last + 1):
-            for j in range(CHUNKS):
-                for ahead in (True, False):
-                    ring(p, ahead, d, j, False).wait_send()
-        for k in range(1, peers):
-            pl.when(owns((me + k) % peers))(scatter(p, k).wait_send)
-
-        @pl.when(owns(me))
-        def _():
-            for k in range(1, peers):
-                gather(p, k, False).wait_send()
-
+        less, full = work.at[p, pl.ds(0, owners - 1)], work.at[p]
+        pl.when(owns(me))(sized(less, send_rs.at[p], recv_rs.at[p]).wait_send)
+        pl.when(jnp.logical_not(owns(me)))(sized(full, send_rs.at[p], recv_rs.at[p]).wait_send)
+        pl.when(owns(me))(sized(slots.at[p], send_ag.at[p], recv_ag.at[p]).wait_send)
+    kept_copy.wait()
     keep_home.wait()
-    for j in range(CHUNKS):
-        for k in range(1, NX):
-            back(j, k, False).wait_send()
-            back(j, k, True).wait_recv()
+    sized(change.at[pl.ds(0, NX - 1)], send_h.at[0], recv_h.at[0]).wait_send()
+    sized(home.at[:, pl.ds(0, (NX - 1) * part)], send_h.at[0], recv_h.at[0]).wait_recv()
 
 
 def fused_step(offs, vectors, eigen, panels, n_row):
@@ -613,16 +567,16 @@
     owners, piece = 20, 32
     every = NX * rows
     dma = pltpu.SemaphoreType.DMA
-    vmem = pl.BlockSpec(memory_space=pltpu.VMEM)
     hbm = pl.BlockSpec(memory_space=pltpu.HBM)
     units = n_panel * (NZ // 2) * CHUNKS
     trade = (NX, rows, part)
     return pl.pallas_call(
         fused_kernel,
-        out_shape=[jax.ShapeDtypeStruct((rows, cols), F32), jax.ShapeDtypeStruct(trade, BF16)],
+        out_shape=[jax.ShapeDtypeStruct((rows, cols), F32), jax.ShapeDtypeStruct((rows, NX * part), BF16)],
         in_specs=[hbm] * 4,
-        out_specs=[vmem] * 2,
+        out_specs=[hbm] * 2,
         scratch_shapes=[
+            pltpu.VMEM((rows, cols), F32),
             pltpu.SMEM(offs.shape, jnp.int32),
             pltpu.VMEM((per_dev, band), F32),
             pltpu.VMEM((rows, cols), F32),
@@ -646,42 +600,39 @@
             pltpu.VMEM((n_panel, owners, piece, BLOCK), BF16),
             pltpu.VMEM(trade, BF16),
             dma((3 + NX,)),
-            dma((n_panel * CHUNKS, NX - 1)),
-            dma((n_panel * CHUNKS, NX - 1)),
-            dma((n_row - 1,)),
-            dma((n_row - 1,)),
-            dma((n_row - 1,)),
-            dma((n_row - 1,)),
+            dma((1,)),
+            dma((n_panel * CHUNKS,)),
+            dma((1,)),
+            dma((1,)),
+            dma((1,)),
+            dma((1,)),
+            dma((1,)),
             dma((units,)),
-            dma((units,)),
-            dma((units,)),
-            dma((units,)),
-            dma((NX - 1,)),
-            dma((NX - 1,)),
-            dma((NX - 1,)),
-            dma((NX - 1,)),
-            dma((n_panel, peers - 1)),
-            dma((n_panel, peers - 1)),
-            dma((n_panel, peers - 1)),
-            dma((n_panel, peers - 1)),
-            dma((CHUNKS, NX - 1)),
-            dma((CHUNKS, NX - 1)),
+            dma((1,)),
+            dma((1,)),
+            dma((1,)),
+            dma((1,)),
+            dma((n_panel,)),
+            dma((n_panel,)),
+            dma((n_panel,)),
+            dma((n_panel,)),
+            dma((1,)),
+            dma((1,)),
             dma((2,)),
         ],
         compiler_params=pltpu.CompilerParams(
-            collective_id=0, has_side_effects=True, vmem_limit_bytes=40 * 1024 * 1024
+            collective_id=0, has_side_effects=True, vmem_limit_bytes=60 * 1024 * 1024
         ),
         cost_estimate=pl.CostEstimate(flops=20_000_000_000, bytes_accessed=8_000_000, transcendentals=0),
     )(offs, vectors, eigen, panels)
 
 
 def local(eigvecs, span_vectors, span_offsets, panels):
-    rows, cols = eigvecs.shape
+    cols = eigvecs.shape[1]
     band = span_vectors.shape[3]
     n_row = lax.psum(1, "row")
     eigen, home = fused_step(span_offsets, span_vectors.reshape(-1, band), eigvecs, panels, n_row)
-    home = home.transpose(1, 0, 2).reshape(rows, -1)[:, :cols]
-    return eigen - home.astype(F32)
+    return eigen - home[:, :cols].astype(F32)
 
 
 def solution(mesh):

time: 93.9 us -> 83.8 us (0.89)
  Pallas kernels: 88.4 us -> 80.8 us
  local copies, waits for them, and re-layouts: 3.91 us -> 0 us
  other arithmetic: 1.29 us -> 2.91 us
    pallas_call x1, Pallas kernels: 88.4 us -> 80.8 us  [fused_step(): pl.pallas_call(fused_kernel, out_shape=[jax.ShapeDtypeStruct((rows, cols)...]
    unnamed x8 -> x0, local copies, waits for them, and re-layouts: 3.85 us -> none
    sub x1, other arithmetic: 1.29 us -> 2.91 us  [local(): return eigen - home[:, :cols].astype(F32)]
where the time goes in v6:
time: 83.8 us; the launch traced here: 83.7 us
  Pallas kernels  80.8 us (96%)
  other arithmetic  2.91 us (3%)
    pallas_call x1, Pallas kernels, fused_step(): pl.pallas_call(fused_kernel, out_shape=[jax.ShapeDtypeStruct((rows, cols)...  80.8 us
    sub x1, other arithmetic, local(): return eigen - home[:, :cols].astype(F32)  2.91 us

profile of v6, /device:TPU:1, one launch (start us, length us, event | category | flops | bytes accessed | tf_op | source)
XLA Modules:
  0.0 83.7 jit_solution(11683363926534221358)
XLA Ops:
  0.0 80.8 %shard_map.46 = (f32[32,12544]{1,0:T(8,128)}, bf16[32,12800]{1,0:T(8,128)(2,1)}) custom-call(s32[2,8]{1,0:T(2,128)} %offs_hbm.1, f32[64,128]{1,0:T(8,128)} %bitcast.1, f32[32,12544]{1,0:T(8,128)} %eigen_hbm.1, bf16[2,8,12544]{2,1,0:T(8,128)(2,1)} %panels_hbm.1), custom_call_target="tpu_custom_call" | custom-call | flops 20000000000 | bytes 8000000 | tf_op jit(solution)/shard_map/pallas_call | solution.py:573
  80.8 2.9 %convert_subtract_fusion = f32[32,12544]{1,0:T(8,128)} fusion(f32[32,12544]{1,0:T(8,128)} %get-tuple-element.7, bf16[32,12800]{1,0:T(8,128)(2,1)} %get-tuple-element.8), kind=kLoop, calls=%fused_computation | loop fusion | flops 802816 | bytes 4014080 | tf_op jit(solution)/shard_map/sub | solution.py:635

commit v7 on v6

--- a/solution.py
+++ b/solution.py
@@ -29,6 +29,9 @@
     b_top, b_low = halves(b)
     d = functools.partial(lax.dot_general, dimension_numbers=NN, preferred_element_type=F32)
     return d(a_top, b_top) + (d(a_top, b_low) + d(a_low, b_top))
+
+
+GRAM_TILES = ((0, 0), (0, 2), (0, 3), (1, 0), (1, 1), (1, 2), (1, 3), (2, 2), (3, 2), (3, 3))
 
 
 def dot3_nt(a, b):
@@ -55,7 +58,7 @@
 
 
 def fused_kernel(offs_hbm, vectors_hbm, eigen_hbm, panels_hbm, kept_hbm, home, kept, offs, vectors, eigen, cut, gathered, packs,
-                 inners, wide, tile_of, placed_top, placed_low, outgoing, traded, shared, held, rounded, delta, acc,
+                 inners, wide, tile_of, placed_top, placed_low, outgoing, traded, shared, rounded, acc_top, acc_low,
                  work, slots, whole, change, load, send_a, recv_a, send_p, recv_p, send_w, recv_w, send_f, recv_f,
                  send_x, recv_x, send_c, recv_c, send_rs, recv_rs, send_ag, recv_ag, send_h, recv_h,
                  own_sem):
@@ -74,7 +77,7 @@
     per_tile = BLOCK // half
     peers = n_row * NX
     me = row * NX + cx
-    owners = work.shape[1]
+    owners = work.shape[0]
     mesh = pl.DeviceIdType.MESH
     mxu_nt = functools.partial(lax.dot_general, dimension_numbers=NT, preferred_element_type=F32)
     mxu = functools.partial(lax.dot_general, dimension_numbers=NN, preferred_element_type=F32)
@@ -132,13 +135,13 @@
             src_ref=ref, dst_ref=ref, send_sem=send, recv_sem=recv, device_id={"cx": (cx + 1) % NX}, device_id_type=mesh
         )
 
-    def over_x(p, j, k):
+    def over_x(j, k):
         at = pl.ds(j * chunk, chunk)
         return pltpu.make_async_remote_copy(
-            src_ref=cut.at[(cx + k) % NX, p, :, at],
-            dst_ref=gathered.at[p, cx, cz, :, at],
+            src_ref=cut.at[(cx + k) % NX, :, :, at],
+            dst_ref=gathered.at[:, cx, cz, :, at],
             send_sem=send_a.at[0],
-            recv_sem=recv_a.at[p * CHUNKS + j],
+            recv_sem=recv_a.at[j],
             device_id={"cx": (cx + k) % NX},
             device_id_type=mesh,
         )
@@ -166,50 +169,51 @@
 
     last = NZ // 2 - 1
 
-    def ring(p, ahead, d, j):
+    def ring(ahead, d, j):
         step = 1 if ahead else NZ - 1
         at = pl.ds(j * chunk, chunk)
-        share = slice(None) if d < last else (pl.ds(0, NX // 2) if ahead else pl.ds(NX // 2, NX // 2))
-        place = gathered.at[p, share, (cz + NZ - d * step) % NZ if ahead else (cz + d) % NZ, :, at]
+        panel = slice(None) if d < last else (pl.ds(0, 1) if ahead else pl.ds(1, 1))
+        place = gathered.at[panel, :, (cz + NZ - d * step) % NZ if ahead else (cz + d) % NZ, :, at]
         return pltpu.make_async_remote_copy(
             src_ref=place,
             dst_ref=place,
             send_sem=send_f.at[0],
-            recv_sem=recv_f.at[((last + 1) * p + d) * CHUNKS + j],
+            recv_sem=recv_f.at[d * CHUNKS + j],
             device_id={"cz": (cz + step) % NZ},
             device_id_type=mesh,
         )
 
-    def launch(p, j):
+    def launch(j):
         at = pl.ds(j * chunk, chunk)
-        sized(gathered.at[p, pl.ds(0, NX - 1), cz, :, at], send_a.at[0], recv_a.at[p * CHUNKS + j]).wait_recv()
+        sized(gathered.at[:, pl.ds(0, NX - 1), cz, :, at], send_a.at[0], recv_a.at[j]).wait_recv()
         for ahead in (True, False):
-            ring(p, ahead, 0, j).start()
-
-    def reflect(p, at):
-        return gathered[p, :, :, :, at].reshape(-1, chunk)
-
-    def product(p, j):
+            ring(ahead, 0, j).start()
+
+    def reflect(at, panel):
+        return gathered[panel, :, :, :, at].reshape(-1, chunk)
+
+    def product(j):
         at = slice(j * chunk, (j + 1) * chunk)
-        mine = reflect(p, at)
-        value = mxu_nt(jnp.concatenate([rounded[:, at], mine], axis=0), mine)
-        acc[...] = value if j == 0 else acc[...] + value
-
-    queue = [(p, d, j) for p in range(n_panel) for d in range(last + 1) for j in range(CHUNKS)]
+        upper, lower = reflect(at, 0), reflect(at, 1)
+        top = jnp.concatenate([rounded[:, at], upper], axis=0)
+        first = mxu_nt(top, jnp.concatenate([upper, lower], axis=0))
+        second = mxu_nt(lower, lower)
+        acc_top[...] = first if j == 0 else acc_top[...] + first
+        acc_low[...] = second if j == 0 else acc_low[...] + second
+
+    queue = [(d, j) for d in range(last + 1) for j in range(CHUNKS)]
 
     def pump(count):
         for _ in range(count):
-            p, d, j = queue.pop(0)
+            d, j = queue.pop(0)
             at = pl.ds(j * chunk, chunk)
-            both = gathered.at[p, :, pl.ds(0, 2 if d < last else 1), :, at]
-            sized(both, send_f.at[0], recv_f.at[((last + 1) * p + d) * CHUNKS + j]).wait_recv()
+            both = gathered.at[:, :, pl.ds(0, 2 if d < last else 1), :, at]
+            sized(both, send_f.at[0], recv_f.at[d * CHUNKS + j]).wait_recv()
             if d < last:
                 for ahead in (True, False):
-                    ring(p, ahead, d + 1, j).start()
-            if p == 0 and d == last - 1:
-                launch(1, j)
-            if d == last:
-                product(p, j)
+                    ring(ahead, d + 1, j).start()
+            else:
+                product(j)
 
     def shifted(values, amount):
         both = jnp.concatenate([values, jnp.zeros_like(values)], axis=1)
@@ -241,7 +245,7 @@
     pl.semaphore_wait(barrier, peers - 1 + 2)
     for j in range(CHUNKS):
         for k in (1, 3, 2):
-            over_x(0, j, k).start()
+            over_x(j, k).start()
     for k in range(1, n_row):
         over_row(packs, send_p, recv_p, k).start()
     eigen_load.wait()
@@ -256,10 +260,7 @@
     for k in (1, 3, 2):
         along_x(outgoing, traded, send_x, recv_x, k).start()
     for j in range(CHUNKS):
-        launch(0, j)
-    for j in range(CHUNKS):
-        for k in (1, 3, 2):
-            over_x(1, j, k).start()
+        launch(j)
 
     def inner_step(step, total):
         at = pl.ds(pl.multiple_of(step * group * LANE, LANE), group * LANE)
@@ -268,10 +269,8 @@
         return total + first[:rows] + first[rows:] + mxu_nt(top, placed_low[:, at])
 
     steps = tiles_dev // group
-    total = lax.fori_loop(0, steps // 2, inner_step, jnp.zeros((rows, per_dev), F32))
-    pump(1)
-    total = lax.fori_loop(steps // 2, steps, inner_step, total)
-    pump(3)
+    total = lax.fori_loop(0, steps, inner_step, jnp.zeros((rows, per_dev), F32))
+    pump(1)
 
     sized(packs.at[pl.ds(0, n_row - 1)], send_p.at[0], recv_p.at[0]).wait_recv()
     every_meta = packs[0, per_dev:]
@@ -296,8 +295,6 @@
         down = turned(across_tile[u])
         down_tile.append(down)
         tile_of[u * BLOCK : (u + 1) * BLOCK] = jnp.broadcast_to(down, (BLOCK, LANE))
-        if u == 1:
-            pump(1)
 
     def of_row(ref, r):
         return jnp.concatenate(
@@ -311,7 +308,7 @@
     inners[row] = jnp.concatenate([total, behind], axis=1)
     for k in range(1, n_row):
         over_row(inners, send_w, recv_w, k).start()
-    pump(2)
+    pump(1)
 
     keep = (((bp // refl) == (bq // refl)) & (bp > bq)) | (((bp // refl) != (bq // refl)) & (bp < bq))
     strict, across = {}, []
@@ -335,10 +332,10 @@
                 across.append(2.0 / jnp.sum(picked, axis=0, keepdims=True))
                 tile = jnp.where(keep, tile, 0.0)
             strict[u, t] = tile * scale
-        if u in (0, 2):
+        if u == 1:
             pump(1)
     inverse = tile_inverses([strict[t, t] for t in range(count)], lambda size: pump(1) if size == 8 else None)
-    pump(2)
+    pump(1)
 
     sized(inners.at[pl.ds(0, n_row - 1)], send_w.at[0], recv_w.at[0]).wait_recv()
     lane = lax.broadcasted_iota(jnp.int32, (rows, LANE), 1) // half
@@ -408,115 +405,87 @@
         value = traded[:, :, at].reshape(every, chunk).astype(F32) - changed(slice_top, slice_both, source)
         if j == 0:
             value = jnp.concatenate([value[:, :LANE] - begin_change, value[:, LANE:]], axis=1)
-        held[:, at] = value
         rounded[:, at] = value.astype(BF16)
-        if j == 2:
-            pump(1)
-    pump(CHUNKS)
-
-    piece = work.shape[2]
-    per_block = BLOCK // piece
-
-    def piece_of(place):
-        return jnp.minimum((place * 5 + 7) // 8, owners - 1)
-
-    def owns(place):
-        return (((place * 5 + 7) // 8) * 8) // 5 == place
-
-    def put(p):
-        blocks = (
-            acc[every : every + BLOCK, :BLOCK],
-            acc[every + BLOCK :, :BLOCK],
-            acc[every + BLOCK :, BLOCK:],
-            acc[:every, :BLOCK],
-            acc[:every, BLOCK:],
-        )
-        for place, block in enumerate(blocks):
-            value = block.astype(BF16)
-            for k in range(per_block):
-                work[p, place * per_block + k] = value[k * piece : (k + 1) * piece]
-
-    def scatter(p, k):
-        target = (me + k) % peers
-        return pltpu.make_async_remote_copy(
-            src_ref=work.at[p, piece_of(target)],
-            dst_ref=slots.at[p, k - 1],
-            send_sem=send_rs.at[p],
-            recv_sem=recv_rs.at[p],
-            device_id=device(target),
-            device_id_type=mesh,
-        )
-
-    def gather(p, k):
-        place = piece_of(me)
-        return pltpu.make_async_remote_copy(
-            src_ref=whole.at[p, place],
-            dst_ref=whole.at[p, place],
-            send_sem=send_ag.at[p],
-            recv_sem=recv_ag.at[p],
-            device_id=device((me + k) % peers),
-            device_id_type=mesh,
-        )
-
-    def start_reduce(p):
-        put(p)
-        for k in range(1, peers):
-            pl.when(owns((me + k) % peers))(scatter(p, k).start)
-
-    def finish_reduce(p):
-        @pl.when(owns(me))
-        def _():
-            sized(slots.at[p], send_rs.at[p], recv_rs.at[p]).wait_recv()
-            value = work[p, piece_of(me)].astype(F32)
-            for k in range(1, peers):
-                value = value + slots[p, k - 1].astype(F32)
-            whole[p, piece_of(me)] = value.astype(BF16)
-            for k in range(1, peers):
-                gather(p, k).start()
-
-    def finish_gather(p):
-        pl.when(owns(me))(sized(whole.at[p, pl.ds(0, owners - 1)], send_ag.at[p], recv_ag.at[p]).wait_recv)
-        pl.when(jnp.logical_not(owns(me)))(sized(whole.at[p], send_ag.at[p], recv_ag.at[p]).wait_recv)
-
-    def panel_solve(p, between):
-        def got(place):
-            return jnp.concatenate(
-                [whole[p, place * per_block + k].astype(F32) for k in range(per_block)], axis=0
-            )
-
-        gram = {(0, 0): got(0), (1, 0): got(1), (1, 1): got(2)}
-        picked = [jnp.where(diag, gram[t, t], 0.0) for t in range(2)]
-        down = [2.0 / jnp.sum(v, axis=1, keepdims=True) for v in picked]
-        beside = [2.0 / jnp.sum(v, axis=0, keepdims=True) for v in picked]
-        below = [jnp.where(bp > bq, gram[t, t] * down[t], 0.0) for t in range(2)]
-        inverses = tile_inverses(below, between)
-        second = dot3(got(4), inverses[1])
-        first = dot3(got(3) - dot3(second, gram[1, 0] * down[1]), inverses[0])
-        return jnp.concatenate([(first * beside[0]).astype(BF16), (second * beside[1]).astype(BF16)], axis=1)
-
-    start_reduce(0)
+    pump(1)
     lax.fori_loop(steps // 4, steps // 2, keep_step, 0)
-    pump(2)
+    pump(1)
     lax.fori_loop(steps // 2, 3 * steps // 4, keep_step, 0)
     pump(1)
     lax.fori_loop(3 * steps // 4, steps, keep_step, 0)
     kept_copy = pltpu.make_async_copy(kept, kept_hbm, load.at[2])
     kept_copy.start()
-    pump(4)
-    finish_reduce(0)
-    pump(5)
-    finish_gather(0)
-    coeffs = panel_solve(0, lambda size: pump(1) if size in (2, 8, 32) else None)
-    for j in range(CHUNKS):
-        at = slice(j * chunk, (j + 1) * chunk)
-        value = mxu(coeffs, reflect(0, at))
-        delta[:, at] = value
-        rounded[:, at] = (held[:, at] - value).astype(BF16)
     pump(len(queue))
-    start_reduce(1)
-    finish_reduce(1)
-    finish_gather(1)
-    coeffs = panel_solve(1, None)
+
+    piece = BLOCK // 2
+
+    def put(place, value):
+        rounded = value.astype(BF16)
+        work[2 * place] = rounded[:piece]
+        work[2 * place + 1] = rounded[piece:]
+
+    for place, (u, t) in enumerate(GRAM_TILES):
+        if u < 2:
+            put(place, acc_top[(1 + u) * BLOCK : (2 + u) * BLOCK, t * BLOCK : (t + 1) * BLOCK])
+        else:
+            put(place, acc_low[(u - 2) * BLOCK : (u - 1) * BLOCK, (t - 2) * BLOCK : (t - 1) * BLOCK])
+    for t in range(4):
+        put(len(GRAM_TILES) + t, acc_top[:BLOCK, t * BLOCK : (t + 1) * BLOCK])
+
+    def scatter(k):
+        return pltpu.make_async_remote_copy(
+            src_ref=work.at[lax.rem((me + k) % peers, owners)],
+            dst_ref=slots.at[k - 1],
+            send_sem=send_rs.at[0],
+            recv_sem=recv_rs.at[0],
+            device_id=device((me + k) % peers),
+            device_id_type=mesh,
+        )
+
+    def gather(k):
+        place = lax.rem(me, owners)
+        return pltpu.make_async_remote_copy(
+            src_ref=whole.at[place],
+            dst_ref=whole.at[place],
+            send_sem=send_ag.at[0],
+            recv_sem=recv_ag.at[0],
+            device_id=device((me + k) % peers),
+            device_id_type=mesh,
+        )
+
+    for k in range(1, peers):
+        pl.when((me + k) % peers < owners)(scatter(k).start)
+
+    @pl.when(me < owners)
+    def _():
+        sized(slots, send_rs.at[0], recv_rs.at[0]).wait_recv()
+        value = work[lax.rem(me, owners)].astype(F32)
+        for k in range(1, peers):
+            value = value + slots[k - 1].astype(F32)
+        whole[lax.rem(me, owners)] = value.astype(BF16)
+        for k in range(1, peers):
+            gather(k).start()
+
+    pl.when(me < owners)(sized(whole.at[pl.ds(0, owners - 1)], send_ag.at[0], recv_ag.at[0]).wait_recv)
+    pl.when(me >= owners)(sized(whole, send_ag.at[0], recv_ag.at[0]).wait_recv)
+
+    def got(place):
+        return jnp.concatenate([whole[2 * place].astype(F32), whole[2 * place + 1].astype(F32)], axis=0)
+
+    gram = {key: got(place) for place, key in enumerate(GRAM_TILES)}
+    picked = [jnp.where(diag, gram[t, t], 0.0) for t in range(4)]
+    down = [2.0 / jnp.sum(p, axis=1, keepdims=True) for p in picked]
+    beside = [2.0 / jnp.sum(p, axis=0, keepdims=True) for p in picked]
+    panel_strict = {(u, t): gram[u, t] * down[u] for u, t in GRAM_TILES}
+    for t in range(4):
+        panel_strict[t, t] = jnp.where(bp > bq, panel_strict[t, t], 0.0)
+    panel_inverse = tile_inverses([panel_strict[t, t] for t in range(4)])
+    answer = {}
+    for t in (1, 0, 3, 2):
+        value = got(len(GRAM_TILES) + t)
+        for u in tuple(answer):
+            value = value - dot3(answer[u], panel_strict[u, t])
+        answer[t] = dot3(value, panel_inverse[t])
+    coeffs = jnp.concatenate([(answer[t] * beside[t]).astype(BF16) for t in range(4)], axis=1)
 
     def back(j, k):
         target = (cx + k) % NX
@@ -531,7 +500,7 @@
 
     for j in range(CHUNKS):
         at = slice(j * chunk, (j + 1) * chunk)
-        value = (delta[:, at] + mxu(coeffs, reflect(1, at))).astype(BF16)
+        value = mxu(coeffs, jnp.concatenate([reflect(at, 0), reflect(at, 1)], axis=0)).astype(BF16)
         for x in range(NX):
             change[x, :, at] = value[x * rows : (x + 1) * rows]
         for k in (2, 1, 3):
@@ -547,11 +516,9 @@
     sized(shared.at[pl.ds(0, NX - 1)], send_c.at[0], recv_c.at[0]).wait_send()
     sized(cut.at[pl.ds(0, NX - 1)], send_a.at[0], recv_a.at[0]).wait_send()
     sized(gathered.at[:, :, pl.ds(0, NZ - 1)], send_f.at[0], recv_f.at[0]).wait_send()
-    for p in range(n_panel):
-        less, full = work.at[p, pl.ds(0, owners - 1)], work.at[p]
-        pl.when(owns(me))(sized(less, send_rs.at[p], recv_rs.at[p]).wait_send)
-        pl.when(jnp.logical_not(owns(me)))(sized(full, send_rs.at[p], recv_rs.at[p]).wait_send)
-        pl.when(owns(me))(sized(slots.at[p], send_ag.at[p], recv_ag.at[p]).wait_send)
+    pl.when(me < owners)(sized(work.at[pl.ds(0, owners - 1)], send_rs.at[0], recv_rs.at[0]).wait_send)
+    pl.when(me >= owners)(sized(work, send_rs.at[0], recv_rs.at[0]).wait_send)
+    pl.when(me < owners)(sized(slots, send_ag.at[0], recv_ag.at[0]).wait_send)
     kept_copy.wait()
     keep_home.wait()
     sized(change.at[pl.ds(0, NX - 1)], send_h.at[0], recv_h.at[0]).wait_send()
@@ -564,11 +531,11 @@
     part = -(-(cols // LANE) // NX) * LANE
     per_dev, band = vectors.shape
     peers = n_row * NX
-    owners, piece = 20, 32
+    owners, piece = 2 * (len(GRAM_TILES) + 4), BLOCK // 2
     every = NX * rows
     dma = pltpu.SemaphoreType.DMA
     hbm = pl.BlockSpec(memory_space=pltpu.HBM)
-    units = n_panel * (NZ // 2) * CHUNKS
+    units = (NZ // 2) * CHUNKS
     trade = (NX, rows, part)
     return pl.pallas_call(
         fused_kernel,
@@ -591,17 +558,16 @@
             pltpu.VMEM(trade, BF16),
             pltpu.VMEM(trade, BF16),
             pltpu.VMEM((NX, rows, LANE), F32),
-            pltpu.VMEM((every, part), F32),
             pltpu.VMEM((every, part), BF16),
-            pltpu.VMEM((every, part), F32),
-            pltpu.VMEM((every + 2 * BLOCK, 2 * BLOCK), F32),
-            pltpu.VMEM((n_panel, owners, piece, BLOCK), BF16),
-            pltpu.VMEM((n_panel, peers - 1, piece, BLOCK), BF16),
-            pltpu.VMEM((n_panel, owners, piece, BLOCK), BF16),
+            pltpu.VMEM((every + 2 * BLOCK, 4 * BLOCK), F32),
+            pltpu.VMEM((2 * BLOCK, 2 * BLOCK), F32),
+            pltpu.VMEM((owners, piece, BLOCK), BF16),
+            pltpu.VMEM((peers - 1, piece, BLOCK), BF16),
+            pltpu.VMEM((owners, piece, BLOCK), BF16),
             pltpu.VMEM(trade, BF16),
             dma((3 + NX,)),
             dma((1,)),
-            dma((n_panel * CHUNKS,)),
+            dma((CHUNKS,)),
             dma((1,)),
             dma((1,)),
             dma((1,)),
@@ -612,10 +578,10 @@
             dma((1,)),
             dma((1,)),
             dma((1,)),
-            dma((n_panel,)),
-            dma((n_panel,)),
-            dma((n_panel,)),
-            dma((n_panel,)),
+            dma((1,)),
+            dma((1,)),
+            dma((1,)),
+            dma((1,)),
             dma((1,)),
             dma((1,)),
             dma((2,)),

time: 83.8 us -> 81.7 us (0.975)
  Pallas kernels: 80.8 us -> 78.6 us
    pallas_call x1, Pallas kernels: 80.8 us -> 78.6 us  [fused_step(): pl.pallas_call(fused_kernel, out_shape=[jax.ShapeDtypeStruct((rows, cols)...]
where the time goes in v7:
time: 81.7 us; the launch traced here: 81.5 us
  Pallas kernels  78.6 us (96%)
  other arithmetic  2.91 us (4%)
    pallas_call x1, Pallas kernels, fused_step(): pl.pallas_call(fused_kernel, out_shape=[jax.ShapeDtypeStruct((rows, cols)...  78.6 us
    sub x1, other arithmetic, local(): return eigen - home[:, :cols].astype(F32)  2.91 us

profile of v7, /device:TPU:1, one launch (start us, length us, event | category | flops | bytes accessed | tf_op | source)
XLA Modules:
  0.0 81.5 jit_solution(5274731850333788661)
XLA Ops:
  0.0 78.6 %shard_map.46 = (f32[32,12544]{1,0:T(8,128)}, bf16[32,12800]{1,0:T(8,128)(2,1)}) custom-call(s32[2,8]{1,0:T(2,128)} %offs_hbm.1, f32[64,128]{1,0:T(8,128)} %bitcast.1, f32[32,12544]{1,0:T(8,128)} %eigen_hbm.1, bf16[2,8,12544]{2,1,0:T(8,128)(2,1)} %panels_hbm.1), custom_call_target="tpu_custom_call" | custom-call | flops 20000000000 | bytes 8000000 | tf_op jit(solution)/shard_map/pallas_call | solution.py:540
  78.6 2.9 %convert_subtract_fusion = f32[32,12544]{1,0:T(8,128)} fusion(f32[32,12544]{1,0:T(8,128)} %get-tuple-element.7, bf16[32,12800]{1,0:T(8,128)(2,1)} %get-tuple-element.8), kind=kLoop, calls=%fused_computation | loop fusion | flops 802816 | bytes 4014080 | tf_op jit(solution)/shard_map/sub | solution.py:601

commit v8 on v7

--- a/solution.py
+++ b/solution.py
@@ -59,8 +59,8 @@
 
 def fused_kernel(offs_hbm, vectors_hbm, eigen_hbm, panels_hbm, kept_hbm, home, kept, offs, vectors, eigen, cut, gathered, packs,
                  inners, wide, tile_of, placed_top, placed_low, outgoing, traded, shared, rounded, acc_top, acc_low,
-                 work, slots, whole, change, load, send_a, recv_a, send_p, recv_p, send_w, recv_w, send_f, recv_f,
-                 send_x, recv_x, send_c, recv_c, send_rs, recv_rs, send_ag, recv_ag, send_h, recv_h,
+                 work, joined, slots, whole, change, load, send_a, recv_a, send_p, recv_p, send_w, recv_w, send_f, recv_f,
+                 send_x, recv_x, send_c, recv_c, send_d, recv_d, send_rs, recv_rs, send_ag, recv_ag, send_h, recv_h,
                  own_sem):
     row, cx, cz = lax.axis_index("row"), lax.axis_index("cx"), lax.axis_index("cz")
     n_row = lax.axis_size("row")
@@ -77,7 +77,7 @@
     per_tile = BLOCK // half
     peers = n_row * NX
     me = row * NX + cx
-    owners = work.shape[0]
+    owners = joined.shape[0]
     mesh = pl.DeviceIdType.MESH
     mxu_nt = functools.partial(lax.dot_general, dimension_numbers=NT, preferred_element_type=F32)
     mxu = functools.partial(lax.dot_general, dimension_numbers=NN, preferred_element_type=F32)
@@ -183,11 +183,24 @@
             device_id_type=mesh,
         )
 
+    def own_block(ahead, j, k):
+        at = pl.ds(j * chunk, chunk)
+        place = gathered.at[:, (cx + NX - k) % NX, cz, :, at]
+        return pltpu.make_async_remote_copy(
+            src_ref=cut.at[cx, :, :, at] if k == 0 else place,
+            dst_ref=place,
+            send_sem=send_f.at[0],
+            recv_sem=recv_f.at[j],
+            device_id={"cz": (cz + (1 if ahead else NZ - 1)) % NZ},
+            device_id_type=mesh,
+        )
+
     def launch(j):
         at = pl.ds(j * chunk, chunk)
         sized(gathered.at[:, pl.ds(0, NX - 1), cz, :, at], send_a.at[0], recv_a.at[j]).wait_recv()
-        for ahead in (True, False):
-            ring(ahead, 0, j).start()
+        for k in range(1, NX):
+            for ahead in (True, False):
+                own_block(ahead, j, k).start()
 
     def reflect(at, panel):
         return gathered[panel, :, :, :, at].reshape(-1, chunk)
@@ -221,6 +234,19 @@
             both = jnp.where(((amount >> bit) & 1) == 1, pltpu.roll(both, 1 << bit, 1), both)
         return both
 
+    own_copy = pltpu.make_async_copy(cut.at[cx], gathered.at[:, cx, cz], own_sem.at[0])
+    own_copy.start()
+
+    pl.semaphore_wait(barrier, peers - 1 + 2)
+    for j in range(3):
+        for k in (1, 3, 2):
+            over_x(j, k).start()
+        if j == 0:
+            for i in range(CHUNKS):
+                for ahead in (True, False):
+                    own_block(ahead, i, 0).start()
+    for k in range(1, n_row):
+        over_row(packs, send_p, recv_p, k).start()
     own_wide = shifted(vectors[...], jnp.concatenate([own_shift, own_shift], axis=1))
     low_top, low_low = [v.astype(F32) for v in halves(own_wide[:, :LANE])]
     high_top, high_low = [v.astype(F32) for v in halves(own_wide[:, LANE:])]
@@ -238,16 +264,6 @@
     lax.fori_loop(0, tiles_dev // group, build, 0)
     placed_top[:, cols:] = jnp.zeros((per_dev, NX * part - cols), BF16)
     placed_low[:, cols:] = jnp.zeros((per_dev, NX * part - cols), BF16)
-    own_copy = pltpu.make_async_copy(cut.at[cx], gathered.at[:, cx, cz], own_sem.at[0])
-    own_copy.start()
-    own_copy.wait()
-
-    pl.semaphore_wait(barrier, peers - 1 + 2)
-    for j in range(CHUNKS):
-        for k in (1, 3, 2):
-            over_x(j, k).start()
-    for k in range(1, n_row):
-        over_row(packs, send_p, recv_p, k).start()
     eigen_load.wait()
     for x in range(NX):
         size = min(part, cols - x * part)
@@ -257,11 +273,6 @@
 
     own_trade = pltpu.make_async_copy(outgoing.at[cx], traded.at[cx], own_sem.at[1])
     own_trade.start()
-    for k in (1, 3, 2):
-        along_x(outgoing, traded, send_x, recv_x, k).start()
-    for j in range(CHUNKS):
-        launch(j)
-
     def inner_step(step, total):
         at = pl.ds(pl.multiple_of(step * group * LANE, LANE), group * LANE)
         top, low = halves(eigen[:, at])
@@ -269,7 +280,17 @@
         return total + first[:rows] + first[rows:] + mxu_nt(top, placed_low[:, at])
 
     steps = tiles_dev // group
-    total = lax.fori_loop(0, steps, inner_step, jnp.zeros((rows, per_dev), F32))
+    for j in range(2):
+        launch(j)
+        for k in (1, 3, 2):
+            over_x(j + 3, k).start()
+    for k in (1, 3, 2):
+        along_x(outgoing, traded, send_x, recv_x, k).start()
+    total = lax.fori_loop(0, steps // 2, inner_step, jnp.zeros((rows, per_dev), F32))
+    launch(2)
+    launch(3)
+    total = lax.fori_loop(steps // 2, steps, inner_step, total)
+    launch(4)
     pump(1)
 
     sized(packs.at[pl.ds(0, n_row - 1)], send_p.at[0], recv_p.at[0]).wait_recv()
@@ -393,6 +414,15 @@
     pump(1)
     kept[:, :LANE] = kept[:, :LANE] - first_change
 
+    pump(1)
+    lax.fori_loop(steps // 4, steps // 2, keep_step, 0)
+    pump(1)
+    lax.fori_loop(steps // 2, 3 * steps // 4, keep_step, 0)
+    pump(1)
+    lax.fori_loop(3 * steps // 4, steps, keep_step, 0)
+    kept_copy = pltpu.make_async_copy(kept, kept_hbm, load.at[2])
+    kept_copy.start()
+    own_copy.wait()
     own_trade.wait()
     sized(traded.at[pl.ds(0, NX - 1)], send_x.at[0], recv_x.at[0]).wait_recv()
     sized(shared.at[pl.ds(0, NX - 1)], send_c.at[0], recv_c.at[0]).wait_recv()
@@ -406,14 +436,6 @@
         if j == 0:
             value = jnp.concatenate([value[:, :LANE] - begin_change, value[:, LANE:]], axis=1)
         rounded[:, at] = value.astype(BF16)
-    pump(1)
-    lax.fori_loop(steps // 4, steps // 2, keep_step, 0)
-    pump(1)
-    lax.fori_loop(steps // 2, 3 * steps // 4, keep_step, 0)
-    pump(1)
-    lax.fori_loop(3 * steps // 4, steps, keep_step, 0)
-    kept_copy = pltpu.make_async_copy(kept, kept_hbm, load.at[2])
-    kept_copy.start()
     pump(len(queue))
 
     piece = BLOCK // 2
@@ -431,42 +453,69 @@
     for t in range(4):
         put(len(GRAM_TILES) + t, acc_top[:BLOCK, t * BLOCK : (t + 1) * BLOCK])
 
+    core, chip = row % 2, (row // 2) * NX + cx
+    chips = peers // 2
+
+    def across(source, target, send, recv):
+        return pltpu.make_async_remote_copy(
+            src_ref=source,
+            dst_ref=target,
+            send_sem=send,
+            recv_sem=recv,
+            device_id={"row": row + 1 - 2 * core},
+            device_id_type=mesh,
+        )
+
+    def on_chip(place):
+        return {"row": (place // NX) * 2 + core, "cx": place % NX}
+
     def scatter(k):
-        return pltpu.make_async_remote_copy(
-            src_ref=work.at[lax.rem((me + k) % peers, owners)],
+        target = (chip + k) % chips
+        return pltpu.make_async_remote_copy(
+            src_ref=joined.at[lax.rem(target, owners)],
             dst_ref=slots.at[k - 1],
             send_sem=send_rs.at[0],
             recv_sem=recv_rs.at[0],
-            device_id=device((me + k) % peers),
-            device_id_type=mesh,
-        )
+            device_id=on_chip(target),
+            device_id_type=mesh,
+        )
+
+    mine = core * owners + lax.rem(chip, owners)
 
     def gather(k):
-        place = lax.rem(me, owners)
-        return pltpu.make_async_remote_copy(
-            src_ref=whole.at[place],
-            dst_ref=whole.at[place],
+        return pltpu.make_async_remote_copy(
+            src_ref=whole.at[mine],
+            dst_ref=whole.at[mine],
             send_sem=send_ag.at[0],
             recv_sem=recv_ag.at[0],
-            device_id=device((me + k) % peers),
-            device_id_type=mesh,
-        )
-
-    for k in range(1, peers):
-        pl.when((me + k) % peers < owners)(scatter(k).start)
-
-    @pl.when(me < owners)
+            device_id=on_chip((chip + k) % chips),
+            device_id_type=mesh,
+        )
+
+    first_swap = across(work.at[pl.ds((1 - core) * owners, owners)], joined, send_d.at[0], recv_d.at[0])
+    first_swap.start()
+    first_swap.wait_recv()
+    for place in range(owners):
+        joined[place] = (joined[place].astype(F32) + work[core * owners + place].astype(F32)).astype(BF16)
+    for k in range(1, chips):
+        pl.when((chip + k) % chips < owners)(scatter(k).start)
+
+    @pl.when(chip < owners)
     def _():
         sized(slots, send_rs.at[0], recv_rs.at[0]).wait_recv()
-        value = work[lax.rem(me, owners)].astype(F32)
-        for k in range(1, peers):
+        value = joined[lax.rem(chip, owners)].astype(F32)
+        for k in range(1, chips):
             value = value + slots[k - 1].astype(F32)
-        whole[lax.rem(me, owners)] = value.astype(BF16)
-        for k in range(1, peers):
+        whole[mine] = value.astype(BF16)
+        for k in range(1, chips):
             gather(k).start()
 
-    pl.when(me < owners)(sized(whole.at[pl.ds(0, owners - 1)], send_ag.at[0], recv_ag.at[0]).wait_recv)
-    pl.when(me >= owners)(sized(whole, send_ag.at[0], recv_ag.at[0]).wait_recv)
+    pl.when(chip < owners)(sized(whole.at[pl.ds(0, owners - 1)], send_ag.at[0], recv_ag.at[0]).wait_recv)
+    pl.when(chip >= owners)(sized(whole.at[pl.ds(0, owners)], send_ag.at[0], recv_ag.at[0]).wait_recv)
+    half_whole = whole.at[pl.ds(core * owners, owners)]
+    second_swap = across(half_whole, half_whole, send_d.at[1], recv_d.at[1])
+    second_swap.start()
+    second_swap.wait_recv()
 
     def got(place):
         return jnp.concatenate([whole[2 * place].astype(F32), whole[2 * place + 1].astype(F32)], axis=0)
@@ -516,9 +565,11 @@
     sized(shared.at[pl.ds(0, NX - 1)], send_c.at[0], recv_c.at[0]).wait_send()
     sized(cut.at[pl.ds(0, NX - 1)], send_a.at[0], recv_a.at[0]).wait_send()
     sized(gathered.at[:, :, pl.ds(0, NZ - 1)], send_f.at[0], recv_f.at[0]).wait_send()
-    pl.when(me < owners)(sized(work.at[pl.ds(0, owners - 1)], send_rs.at[0], recv_rs.at[0]).wait_send)
-    pl.when(me >= owners)(sized(work, send_rs.at[0], recv_rs.at[0]).wait_send)
-    pl.when(me < owners)(sized(slots, send_ag.at[0], recv_ag.at[0]).wait_send)
+    first_swap.wait_send()
+    second_swap.wait_send()
+    pl.when(chip < owners)(sized(joined.at[pl.ds(0, owners - 1)], send_rs.at[0], recv_rs.at[0]).wait_send)
+    pl.when(chip >= owners)(sized(joined, send_rs.at[0], recv_rs.at[0]).wait_send)
+    pl.when(chip < owners)(sized(slots, send_ag.at[0], recv_ag.at[0]).wait_send)
     kept_copy.wait()
     keep_home.wait()
     sized(change.at[pl.ds(0, NX - 1)], send_h.at[0], recv_h.at[0]).wait_send()
@@ -530,7 +581,6 @@
     n_panel, refl_dev, _ = panels.shape
     part = -(-(cols // LANE) // NX) * LANE
     per_dev, band = vectors.shape
-    peers = n_row * NX
     owners, piece = 2 * (len(GRAM_TILES) + 4), BLOCK // 2
     every = NX * rows
     dma = pltpu.SemaphoreType.DMA
@@ -562,7 +612,8 @@
             pltpu.VMEM((every + 2 * BLOCK, 4 * BLOCK), F32),
             pltpu.VMEM((2 * BLOCK, 2 * BLOCK), F32),
             pltpu.VMEM((owners, piece, BLOCK), BF16),
-            pltpu.VMEM((peers - 1, piece, BLOCK), BF16),
+            pltpu.VMEM((owners // 2, piece, BLOCK), BF16),
+            pltpu.VMEM((n_row * NX // 2 - 1, piece, BLOCK), BF16),
             pltpu.VMEM((owners, piece, BLOCK), BF16),
             pltpu.VMEM(trade, BF16),
             dma((3 + NX,)),
@@ -578,6 +629,8 @@
             dma((1,)),
             dma((1,)),
             dma((1,)),
+            dma((2,)),
+            dma((2,)),
             dma((1,)),
             dma((1,)),
             dma((1,)),

time: 81.7 us -> 78.8 us (0.965)
  Pallas kernels: 78.6 us -> 75.8 us
    pallas_call x1, Pallas kernels: 78.6 us -> 75.8 us  [fused_step(): pl.pallas_call(fused_kernel, out_shape=[jax.ShapeDtypeStruct((rows, cols)...]
where the time goes in v8:
time: 78.8 us; the launch traced here: 78.7 us
  Pallas kernels  75.8 us (96%)
  other arithmetic  2.91 us (4%)
    pallas_call x1, Pallas kernels, fused_step(): pl.pallas_call(fused_kernel, out_shape=[jax.ShapeDtypeStruct((rows, cols)...  75.8 us
    sub x1, other arithmetic, local(): return eigen - home[:, :cols].astype(F32)  2.91 us

profile of v8, /device:TPU:1, one launch (start us, length us, event | category | flops | bytes accessed | tf_op | source)
XLA Modules:
  0.0 78.7 jit_solution(2676357068366799085)
XLA Ops:
  0.0 75.8 %shard_map.46 = (f32[32,12544]{1,0:T(8,128)}, bf16[32,12800]{1,0:T(8,128)(2,1)}) custom-call(s32[2,8]{1,0:T(2,128)} %offs_hbm.1, f32[64,128]{1,0:T(8,128)} %bitcast.1, f32[32,12544]{1,0:T(8,128)} %eigen_hbm.1, bf16[2,8,12544]{2,1,0:T(8,128)(2,1)} %panels_hbm.1), custom_call_target="tpu_custom_call" | custom-call | flops 20000000000 | bytes 8000000 | tf_op jit(solution)/shard_map/pallas_call | solution.py:590
  75.8 2.9 %convert_subtract_fusion = f32[32,12544]{1,0:T(8,128)} fusion(f32[32,12544]{1,0:T(8,128)} %get-tuple-element.7, bf16[32,12800]{1,0:T(8,128)(2,1)} %get-tuple-element.8), kind=kLoop, calls=%fused_computation | loop fusion | flops 802816 | bytes 4014080 | tf_op jit(solution)/shard_map/sub | solution.py:654

commit v9 on v8

--- a/solution.py
+++ b/solution.py
@@ -76,14 +76,10 @@
     spans = half // refl
     per_tile = BLOCK // half
     peers = n_row * NX
-    me = row * NX + cx
     owners = joined.shape[0]
     mesh = pl.DeviceIdType.MESH
     mxu_nt = functools.partial(lax.dot_general, dimension_numbers=NT, preferred_element_type=F32)
     mxu = functools.partial(lax.dot_general, dimension_numbers=NN, preferred_element_type=F32)
-
-    def device(place):
-        return {"row": place // NX, "cx": place % NX}
 
     loads = [
         pltpu.make_async_copy(offs_hbm, offs, load.at[0]),
@@ -105,8 +101,14 @@
     barrier = pltpu.get_barrier_semaphore()
     for k in (1, NZ - 1):
         pl.semaphore_signal(barrier, inc=1, device_id={"cz": (cz + k) % NZ}, device_id_type=mesh)
-    for k in range(1, peers):
-        pl.semaphore_signal(barrier, inc=1, device_id=device((me + k) % peers), device_id_type=mesh)
+    for k in range(1, NX):
+        pl.semaphore_signal(barrier, inc=1, device_id={"cx": (cx + k) % NX}, device_id_type=mesh)
+    for k in range(1, n_row):
+        pl.semaphore_signal(barrier, inc=1, device_id={"row": (row + k) % n_row}, device_id_type=mesh)
+    for i in range(1, n_row // 2):
+        for k in range(1, NX):
+            there = {"row": (row + 2 * i) % n_row, "cx": (cx + k) % NX}
+            pl.semaphore_signal(barrier, inc=1, device_id=there, device_id_type=mesh)
     for copy in loads:
         copy.wait()
 
@@ -237,7 +239,7 @@
     own_copy = pltpu.make_async_copy(cut.at[cx], gathered.at[:, cx, cz], own_sem.at[0])
     own_copy.start()
 
-    pl.semaphore_wait(barrier, peers - 1 + 2)
+    pl.semaphore_wait(barrier, 2 + NX - 1 + n_row - 1 + (n_row // 2 - 1) * (NX - 1))
     for j in range(3):
         for k in (1, 3, 2):
             over_x(j, k).start()
@@ -455,6 +457,15 @@
 
     core, chip = row % 2, (row // 2) * NX + cx
     chips = peers // 2
+    ys = n_row // 2
+    far_first = sorted(
+        ((i, k) for i in range(ys) for k in range(NX) if i or k),
+        key=lambda pair: -min(pair[0], ys - pair[0]) - min(pair[1], NX - pair[1]),
+    )
+
+    def chip_at(k):
+        i, shift = far_first[k - 1]
+        return ((row // 2 + i) % ys) * NX + (cx + shift) % NX
 
     def across(source, target, send, recv):
         return pltpu.make_async_remote_copy(
@@ -470,7 +481,7 @@
         return {"row": (place // NX) * 2 + core, "cx": place % NX}
 
     def scatter(k):
-        target = (chip + k) % chips
+        target = chip_at(k)
         return pltpu.make_async_remote_copy(
             src_ref=joined.at[lax.rem(target, owners)],
             dst_ref=slots.at[k - 1],
@@ -488,7 +499,7 @@
             dst_ref=whole.at[mine],
             send_sem=send_ag.at[0],
             recv_sem=recv_ag.at[0],
-            device_id=on_chip((chip + k) % chips),
+            device_id=on_chip(chip_at(k)),
             device_id_type=mesh,
         )
 
@@ -498,7 +509,7 @@
     for place in range(owners):
         joined[place] = (joined[place].astype(F32) + work[core * owners + place].astype(F32)).astype(BF16)
     for k in range(1, chips):
-        pl.when((chip + k) % chips < owners)(scatter(k).start)
+        pl.when(chip_at(k) < owners)(scatter(k).start)
 
     @pl.when(chip < owners)
     def _():
@@ -552,7 +563,7 @@
         value = mxu(coeffs, jnp.concatenate([reflect(at, 0), reflect(at, 1)], axis=0)).astype(BF16)
         for x in range(NX):
             change[x, :, at] = value[x * rows : (x + 1) * rows]
-        for k in (2, 1, 3):
+        for k in (1, 3, 2):
             back(j, k).start()
     keep_home = pltpu.make_async_copy(
         change.at[cx], home.at[:, pl.ds(pl.multiple_of(cx * part, LANE), part)], own_sem.at[0]

time: 78.8 us -> 77.8 us (0.987)
  Pallas kernels: 75.8 us -> 74.8 us
    pallas_call x1, Pallas kernels: 75.8 us -> 74.8 us  [fused_step(): pl.pallas_call(fused_kernel, out_shape=[jax.ShapeDtypeStruct((rows, cols)...]
where the time goes in v9:
time: 77.8 us; the launch traced here: 77.7 us
  Pallas kernels  74.8 us (96%)
  other arithmetic  2.91 us (4%)
    pallas_call x1, Pallas kernels, fused_step(): pl.pallas_call(fused_kernel, out_shape=[jax.ShapeDtypeStruct((rows, cols)...  74.8 us
    sub x1, other arithmetic, local(): return eigen - home[:, :cols].astype(F32)  2.91 us

profile of v9, /device:TPU:1, one launch (start us, length us, event | category | flops | bytes accessed | tf_op | source)
XLA Modules:
  0.0 77.7 jit_solution(9650556315056966962)
XLA Ops:
  0.0 74.8 %shard_map.46 = (f32[32,12544]{1,0:T(8,128)}, bf16[32,12800]{1,0:T(8,128)(2,1)}) custom-call(s32[2,8]{1,0:T(2,128)} %offs_hbm.1, f32[64,128]{1,0:T(8,128)} %bitcast.1, f32[32,12544]{1,0:T(8,128)} %eigen_hbm.1, bf16[2,8,12544]{2,1,0:T(8,128)(2,1)} %panels_hbm.1), custom_call_target="tpu_custom_call" | custom-call | flops 20000000000 | bytes 8000000 | tf_op jit(solution)/shard_map/pallas_call | solution.py:601
  74.8 2.9 %convert_subtract_fusion = f32[32,12544]{1,0:T(8,128)} fusion(f32[32,12544]{1,0:T(8,128)} %get-tuple-element.7, bf16[32,12800]{1,0:T(8,128)(2,1)} %get-tuple-element.8), kind=kLoop, calls=%fused_computation | loop fusion | flops 802816 | bytes 4014080 | tf_op jit(solution)/shard_map/sub | solution.py:665

commit v10 on v9

--- a/solution.py
+++ b/solution.py
@@ -288,11 +288,11 @@
             over_x(j + 3, k).start()
     for k in (1, 3, 2):
         along_x(outgoing, traded, send_x, recv_x, k).start()
+    for j in range(2, CHUNKS):
+        launch(j)
     total = lax.fori_loop(0, steps // 2, inner_step, jnp.zeros((rows, per_dev), F32))
-    launch(2)
-    launch(3)
+    pump(1)
     total = lax.fori_loop(steps // 2, steps, inner_step, total)
-    launch(4)
     pump(1)
 
     sized(packs.at[pl.ds(0, n_row - 1)], send_p.at[0], recv_p.at[0]).wait_recv()

time: 77.8 us -> 77.9 us (level)
  no operation moved by 1% of the time
where the time goes in v10:
time: 77.9 us; the launch traced here: 77.8 us
  Pallas kernels  74.9 us (96%)
  other arithmetic  2.91 us (4%)
    pallas_call x1, Pallas kernels, fused_step(): pl.pallas_call(fused_kernel, out_shape=[jax.ShapeDtypeStruct((rows, cols)...  74.9 us
    sub x1, other arithmetic, local(): return eigen - home[:, :cols].astype(F32)  2.91 us

profile of v10, /device:TPU:1, one launch (start us, length us, event | category | flops | bytes accessed | tf_op | source)
XLA Modules:
  0.0 77.8 jit_solution(12867211936772827089)
XLA Ops:
  0.0 74.9 %shard_map.46 = (f32[32,12544]{1,0:T(8,128)}, bf16[32,12800]{1,0:T(8,128)(2,1)}) custom-call(s32[2,8]{1,0:T(2,128)} %offs_hbm.1, f32[64,128]{1,0:T(8,128)} %bitcast.1, f32[32,12544]{1,0:T(8,128)} %eigen_hbm.1, bf16[2,8,12544]{2,1,0:T(8,128)(2,1)} %panels_hbm.1), custom_call_target="tpu_custom_call" | custom-call | flops 20000000000 | bytes 8000000 | tf_op jit(solution)/shard_map/pallas_call | solution.py:601
  74.9 2.9 %convert_subtract_fusion = f32[32,12544]{1,0:T(8,128)} fusion(f32[32,12544]{1,0:T(8,128)} %get-tuple-element.7, bf16[32,12800]{1,0:T(8,128)(2,1)} %get-tuple-element.8), kind=kLoop, calls=%fused_computation | loop fusion | flops 802816 | bytes 4014080 | tf_op jit(solution)/shard_map/sub | solution.py:665
